TPU v7x, 32 devices: a whole 2x2x4 slice. The times are simulated.
32 devices in a mesh: fsdp: 32 (over z, y, x, core).
Axes of the slice: x: 2, y: 2, z: 4, core: 2. Of those that a mesh axis runs over, the one named last changes fastest.
Arguments:
- patches: bfloat16 [512, 196, 768], P('fsdp')
- keep: int32 [512, 49], P('fsdp')
- w_patch: float32 [768, 1024], P(None, 'fsdp')
- b_patch: float32 [1024], P('fsdp')
- pos_table: float32 [197, 1024], P(None, 'fsdp')
- cls_tok: float32 [1024], P('fsdp')
- lnp_g: float32 [1024], P('fsdp')
- lnp_b: float32 [1024], P('fsdp')
- ln1_g: float32 [1024], P('fsdp')
- ln1_b: float32 [1024], P('fsdp')
- w_qkv: float32 [1024, 3, 16, 64], P('fsdp')
- b_qkv: float32 [3072], P('fsdp')
- w_out: float32 [1024, 1024], P('fsdp')
- b_out: float32 [1024], P('fsdp')
- ln2_g: float32 [1024], P('fsdp')
- ln2_b: float32 [1024], P('fsdp')
- w_fc: float32 [1024, 4096], P('fsdp')
- b_fc: float32 [4096], P('fsdp')
- w_proj: float32 [4096, 1024], P('fsdp')
- b_proj: float32 [1024], P('fsdp')
- grad_h1: bfloat16 [512, 50, 1024], P('fsdp')
Outputs:
- output 1: bfloat16 [512, 50, 1024], P('fsdp')
- output 2: float32 [768, 1024], P(None, 'fsdp')
- output 3: float32 [1024], P('fsdp')
- output 4: float32 [197, 1024], P(None, 'fsdp')
- output 5: float32 [1024], P('fsdp')
- output 6: float32 [1024], P('fsdp')
- output 7: float32 [1024], P('fsdp')
- output 8: float32 [1024], P('fsdp')
- output 9: float32 [1024], P('fsdp')
- output 10: float32 [1024, 3, 16, 64], P('fsdp')
- output 11: float32 [3072], P('fsdp')
- output 12: float32 [1024, 1024], P('fsdp')
- output 13: float32 [1024], P('fsdp')
- output 14: float32 [1024], P('fsdp')
- output 15: float32 [1024], P('fsdp')
- output 16: float32 [1024, 4096], P('fsdp')
- output 17: float32 [4096], P('fsdp')
- output 18: float32 [4096, 1024], P('fsdp')
- output 19: float32 [1024], P('fsdp')
All inputs are finite; a program needn't handle non-finite values.
Results may differ from a plain program's by a relative error of at most 0.02.
Values are sent between devices in bfloat16 or wider.
A program may use at most 1 GiB of HBM per device.

v0:
```python
import jax
import jax.numpy as jnp
from jax import lax
from jax.sharding import PartitionSpec as P

MESH_AXIS = 'fsdp'
LN_EPS = 1e-5
INV_SQRT2 = 0.7071067811865476
INV_SQRT_2PI = 0.3989422804014327
PARAM_NAMES = ('w_patch', 'b_patch', 'pos_table', 'cls_tok', 'lnp_g', 'lnp_b', 'ln1_g', 'ln1_b', 'w_qkv', 'b_qkv', 'w_out', 'b_out', 'ln2_g', 'ln2_b', 'w_fc', 'b_fc', 'w_proj', 'b_proj')
VECTOR_NAMES = ('b_patch', 'cls_tok', 'lnp_g', 'lnp_b', 'ln1_g', 'ln1_b', 'b_qkv', 'b_out', 'ln2_g', 'ln2_b', 'b_fc', 'b_proj')
BACKWARD_NAMES = ('w_qkv', 'w_out', 'w_fc', 'w_proj', 'lnp_g', 'ln1_g', 'ln2_g')
LAST_SPLIT = ('w_patch', 'pos_table')


def product(einsum_form, left_op, right_op):
    return jnp.einsum(einsum_form, left_op, right_op, preferred_element_type=jnp.float32)


def norm_forward(x_in, gain_f, shift_f):
    centered = x_in - jnp.mean(x_in, axis=-1, keepdims=True)
    inv_std = lax.rsqrt(jnp.mean(centered * centered, axis=-1, keepdims=True) + LN_EPS)
    x_hat = centered * inv_std
    return x_hat * gain_f + shift_f, x_hat, inv_std


def norm_backward(d_norm, x_hat, inv_std, gain_f):
    d_hat = d_norm * gain_f
    d_in = inv_std * (d_hat - jnp.mean(d_hat, axis=-1, keepdims=True) - x_hat * jnp.mean(d_hat * x_hat, axis=-1, keepdims=True))
    return d_in, jnp.sum(d_norm * x_hat, axis=(0, 1)), jnp.sum(d_norm, axis=(0, 1))


def gelu_slope(pre_act):
    return 0.5 * (1.0 + lax.erf(pre_act * INV_SQRT2)) + pre_act * jnp.exp(-0.5 * pre_act * pre_act) * INV_SQRT_2PI


def forward(full_w, patches, keep):
    n_img, n_patch = patches.shape[0], patches.shape[1]
    d_model = full_w['w_out'].shape[0]
    n_heads, head_dim = full_w['w_qkv'].shape[2], full_w['w_qkv'].shape[3]
    logit_scale = head_dim ** -0.5
    as_f32 = {name: full_w[name].astype(jnp.float32) for name in VECTOR_NAMES}
    onehot_keep = (keep[:, :, None] == lax.broadcasted_iota(jnp.int32, (1, 1, n_patch), 2)).astype(jnp.bfloat16)
    kept_rows = product('bkp,bpq->bkq', onehot_keep, patches).astype(jnp.bfloat16)
    embed_rows = (product('bkq,qw->bkw', kept_rows, full_w['w_patch']) + as_f32['b_patch']
                  + product('bkp,pw->bkw', onehot_keep, full_w['pos_table'][1:]))
    head_row = as_f32['cls_tok'] + full_w['pos_table'][0].astype(jnp.float32)
    x_zero = jnp.concatenate([jnp.broadcast_to(head_row, (n_img, 1, d_model)), embed_rows], axis=1)
    h_zero, hat_p, inv_p = norm_forward(x_zero, as_f32['lnp_g'], as_f32['lnp_b'])
    y_one, hat_1, inv_1 = norm_forward(h_zero, as_f32['ln1_g'], as_f32['ln1_b'])
    a_in = y_one.astype(jnp.bfloat16)
    qkv_all = (product('btw,wchd->btchd', a_in, full_w['w_qkv']) + as_f32['b_qkv'].reshape(3, n_heads, head_dim)).astype(jnp.bfloat16)
    q_heads, k_heads, v_heads = qkv_all[:, :, 0], qkv_all[:, :, 1], qkv_all[:, :, 2]
    attn_prob = jax.nn.softmax(product('bqhd,bkhd->bhqk', q_heads, k_heads) * logit_scale, axis=-1)
    prob_b = attn_prob.astype(jnp.bfloat16)
    context = product('bhqk,bkhd->bqhd', prob_b, v_heads).astype(jnp.bfloat16)
    h_mid = h_zero + product('bqhd,hdw->bqw', context, full_w['w_out'].reshape(n_heads, head_dim, d_model)) + as_f32['b_out']
    y_two, hat_2, inv_2 = norm_forward(h_mid, as_f32['ln2_g'], as_f32['ln2_b'])
    c_in = y_two.astype(jnp.bfloat16)
    pre_act = product('btw,wf->btf', c_in, full_w['w_fc']) + as_f32['b_fc']
    gelu_out = jax.nn.gelu(pre_act, approximate=False).astype(jnp.bfloat16)
    h_one = (h_mid + product('btf,fw->btw', gelu_out, full_w['w_proj']) + as_f32['b_proj']).astype(jnp.bfloat16)
    saved = dict(onehot_keep=onehot_keep, kept_rows=kept_rows, hat_p=hat_p, inv_p=inv_p, hat_1=hat_1, inv_1=inv_1, a_in=a_in, q_heads=q_heads, k_heads=k_heads, v_heads=v_heads, attn_prob=attn_prob, prob_b=prob_b, context=context, hat_2=hat_2, inv_2=inv_2, c_in=c_in, pre_act=pre_act, gelu_out=gelu_out)
    return h_one, saved


def backward(weights, saved, grad_h1):
    d_model = weights['w_out'].shape[0]
    n_heads, head_dim = weights['w_qkv'].shape[2], weights['w_qkv'].shape[3]
    logit_scale = head_dim ** -0.5
    w_out3 = weights['w_out'].reshape(n_heads, head_dim, d_model)
    d_h = grad_h1.astype(jnp.float32)
    g_w_proj = product('btf,btw->fw', saved['gelu_out'], grad_h1)
    d_pre = product('btw,fw->btf', grad_h1, weights['w_proj']) * gelu_slope(saved['pre_act'])
    d_pre_b = d_pre.astype(jnp.bfloat16)
    g_w_fc = product('btw,btf->wf', saved['c_in'], d_pre_b)
    d_c = product('btf,wf->btw', d_pre_b, weights['w_fc'])
    d_norm2, g_ln2_g, g_ln2_b = norm_backward(d_c, saved['hat_2'], saved['inv_2'], weights['ln2_g'].astype(jnp.float32))
    d_mid = d_norm2 + d_h
    d_mid_b = d_mid.astype(jnp.bfloat16)
    g_w_out = product('bqhd,bqw->hdw', saved['context'], d_mid_b).reshape(d_model, d_model)
    d_ctx = product('bqw,hdw->bqhd', d_mid_b, w_out3).astype(jnp.bfloat16)
    g_v = product('bhqk,bqhd->bkhd', saved['prob_b'], d_ctx)
    d_prob = product('bqhd,bkhd->bhqk', d_ctx, saved['v_heads'])
    attn_prob = saved['attn_prob']
    d_logit = (attn_prob * (d_prob - jnp.sum(attn_prob * d_prob, axis=-1, keepdims=True)) * logit_scale).astype(jnp.bfloat16)
    g_q = product('bhqk,bkhd->bqhd', d_logit, saved['k_heads'])
    g_k = product('bhqk,bqhd->bkhd', d_logit, saved['q_heads'])
    d_qkv = jnp.stack([g_q, g_k, g_v], axis=2)
    d_qkv_b = d_qkv.astype(jnp.bfloat16)
    g_w_qkv = product('btw,btchd->wchd', saved['a_in'], d_qkv_b)
    d_a = product('btchd,wchd->btw', d_qkv_b, weights['w_qkv'])
    d_norm1, g_ln1_g, g_ln1_b = norm_backward(d_a, saved['hat_1'], saved['inv_1'], weights['ln1_g'].astype(jnp.float32))
    d_zero = d_norm1 + d_mid
    d_x, g_lnp_g, g_lnp_b = norm_backward(d_zero, saved['hat_p'], saved['inv_p'], weights['lnp_g'].astype(jnp.float32))
    d_head = jnp.sum(d_x[:, 0], axis=0)
    d_emb = d_x[:, 1:]
    d_emb_b = d_emb.astype(jnp.bfloat16)
    g_pos = jnp.concatenate([d_head[None], product('bkp,bkw->pw', saved['onehot_keep'], d_emb_b)], axis=0)
    return dict(w_patch=product('bkq,bkw->qw', saved['kept_rows'], d_emb_b), b_patch=jnp.sum(d_emb, axis=(0, 1)), pos_table=g_pos, cls_tok=d_head, lnp_g=g_lnp_g, lnp_b=g_lnp_b, ln1_g=g_ln1_g, ln1_b=g_ln1_b, w_qkv=g_w_qkv, b_qkv=jnp.sum(d_qkv, axis=(0, 1)).reshape(-1), w_out=g_w_out, b_out=jnp.sum(d_mid, axis=(0, 1)), ln2_g=g_ln2_g, ln2_b=g_ln2_b, w_fc=g_w_fc, b_fc=jnp.sum(d_pre, axis=(0, 1)), w_proj=g_w_proj, b_proj=jnp.sum(d_h, axis=(0, 1)))


def solution(mesh):
    def split_of(name):
        return 1 if name in LAST_SPLIT else 0

    def spec_of(name):
        return P(None, MESH_AXIS) if name in LAST_SPLIT else P(MESH_AXIS)

    def gather_whole(shard, name):
        return lax.all_gather(shard.astype(jnp.bfloat16), MESH_AXIS, axis=split_of(name), tiled=True)

    def local_step(patches, keep, *rest):
        shards = dict(zip(PARAM_NAMES, rest[:-1]))
        grad_h1 = rest[-1]
        full_w = {name: gather_whole(shards[name], name) for name in PARAM_NAMES}
        h_one, saved = forward(full_w, patches, keep)
        held, h_one = lax.optimization_barrier((shards, h_one))
        regathered = {name: gather_whole(held[name], name) for name in BACKWARD_NAMES}
        grad_map = backward(regathered, saved, grad_h1)
        summed = tuple(lax.psum_scatter(grad_map[name], MESH_AXIS, scatter_dimension=split_of(name), tiled=True) for name in PARAM_NAMES)
        return (h_one,) + summed

    batch_spec = P(MESH_AXIS)
    param_specs = tuple(spec_of(name) for name in PARAM_NAMES)
    return jax.shard_map(local_step, mesh=mesh, in_specs=(batch_spec, batch_spec) + param_specs + (batch_spec,), out_specs=(batch_spec,) + param_specs, check_vma=False)
```

profile of v0, /device:TPU:0, one launch (start us, length us, event | category | flops | bytes accessed | tf_op | source)
XLA Modules:
  0.0 1921.9 jit_solution(5821969084323533055)
XLA Ops:
  9.0 2.1 copy.108
  19.1 42.9 %all-reduce.28 = (bf16[3072]{0:T(1024)(128)(2,1)S(1)}, bf16[1024]{0:T(1024)(128)(2,1)S(1)}, bf16[1024]{0:T(1024)(128)(2,1)S(1)}, bf16[1024]{0:T(1024)(128)(2,1)S...) all-reduce(bf16[3072]{0:T(1024)(128)(2,1)S(1)} %dynamic-update-slic, ...), channel_id=1, replica_groups=mesh['fsdp'=32] {'fsdp'}, use_global_device_ids=true, to_apply=%add.6 | all-reduce | flops 13312 | bytes 53248
  62.0 41.5 %all_gather.76 = bf16[197,1024]{0,1:T(8,128)(2,1)S(1)} all-gather(bf16[197,32]{0,1:T(8,128)(2,1)S(1)} %convert_element_type.175), channel_id=1, replica_groups=mesh['fsdp'=32] {'fsdp'}, dimensions={1}, use_global_device_ids=true | all-gather | bytes 416064 | tf_op jit(solution)/shard_map/all_gather | solution.py:111
  103.9 37.1 %all-gather = bf16[32,1,128]{2,1,0:T(2,128)(2,1)S(1)} all-gather(bf16[1,1,128]{2,1,0:T(2,128)(2,1)S(1)} %convert_bitcast_fusion), channel_id=1, replica_groups=mesh['fsdp'=32] {'fsdp'}, dimensions={0}, use_global_device_ids=true | all-gather | bytes 8448 | tf_op jit(solution)/shard_map/all_gather | solution.py:111
  141.0 5.5 fusion.78
  146.6 3.5 fusion.83
  155.4 21.7 %all-gather.13.cloned.1.call-done = bf16[1024,3,16,64]{3,0,2,1:T(8,128)(2,1)} async-done(((bf16[32,3,16,64]{3,0,2,1:T(8,128)(2,1)}), bf16[1024,3,16,64]{3,0,2,1:T(8,128)(2,1)}) %all-gather.13.cloned.1.call-update) | async-done | bytes 6291472 | tf_op jit(solution)/shard_map/all_gather | solution.py:111
  177.1 18.4 add_convert_fusion
  197.7 5.1 fusion.102
  202.8 7.0 fusion.69
  209.9 25.7 %all-gather.15.cloned.1.call-done = bf16[1024,1024]{1,0:T(8,128)(2,1)} async-done(((bf16[32,1024]{1,0:T(8,128)(2,1)}), bf16[1024,1024]{1,0:T(8,128)(2,1)}) %all-gather.15.cloned.1.call-update) | async-done | bytes 2097168 | tf_op jit(solution)/shard_map/all_gather | solution.py:111
  235.6 6.5 fusion.103
  244.6 70.1 %all-gather.17.cloned.1.call-done = bf16[1024,4096]{1,0:T(8,128)(2,1)} async-done(((bf16[32,4096]{1,0:T(8,128)(2,1)}), bf16[1024,4096]{1,0:T(8,128)(2,1)}) %all-gather.17.cloned.1.call-update) | async-done | bytes 8388624 | tf_op jit(solution)/shard_map/all_gather | solution.py:111
  314.7 16.5 fusion.34
  331.2 5.2 copy-done.5
  336.4 34.4 %fusion.6 = bf16[16,50,4096]{2,1,0:T(8,128)(2,1)} fusion(f32[16,50,4096]{2,1,0:T(8,128)S(1)} %get-tuple-element.140, f32[4096]{0:T(1024)S(1)} %bitcast.165, u16[50,4096]{1,0:T(8,128)(2,1)S(1)} %get-tuple-element.93, u16[50,4096]{1,0:T(8,128)(2,1)S(1)} %get-tuple-element.92), kind=kLoop, calls=%fused_computation.10 | loop fusion | flops 232652800 | bytes 20496384 | tf_op jit(solution)/shard_map/convert_element_type | solution.py:61
  370.8 23.0 %all-gather.19.cloned.1.call-done = bf16[4096,1024]{1,0:T(8,128)(2,1)} async-done(((bf16[128,1024]{1,0:T(8,128)(2,1)}), bf16[4096,1024]{1,0:T(8,128)(2,1)}) %all-gather.19.cloned.1.call-update) | async-done | bytes 8388624 | tf_op jit(solution)/shard_map/all_gather | solution.py:111
  393.7 13.9 add_convert_fusion.1
  411.8 40.0 %all-reduce.27 = (bf16[1024]{0:T(1024)(128)(2,1)S(1)}, bf16[1024]{0:T(1024)(128)(2,1)S(1)}, bf16[1024]{0:T(1024)(128)(2,1)S(1)}) all-reduce(bf16[1024]{0:T(1024)(128)(2,1)S(1)} %dynamic-update-slice.11, bf16[1024]{0:T(1024)(128)(2,1)S(1)} %dynamic-update-slice.12, ...), channel_id=1, replica_groups=mesh['fsdp'=32] {'fsdp'}, use_global_device_ids=true, to_apply=%add.11 | all-reduce | flops 3072 | bytes 12288
  451.8 32.7 %all-gather.21.cloned.1.call-done = bf16[4096,1024]{1,0:T(8,128)(2,1)} async-done(((bf16[128,1024]{1,0:T(8,128)(2,1)}), bf16[4096,1024]{1,0:T(8,128)(2,1)}) %all-gather.21.cloned.1.call-update) | async-done | bytes 8388624 | tf_op jit(solution)/shard_map/all_gather | solution.py:111
  484.5 20.4 %fusion.104 = (f32[4096]{0:T(1024)}, bf16[16,50,4096]{2,1,0:T(8,128)(2,1)}) fusion(f32[16,50,4096]{2,1,0:T(8,128)} %copy-done.5, f32[4096]{0:T(1024)S(1)} %bitcast.166, bf16[16,50,1024]{2,0,1:T(8,128)(2,1)} %param.41, bf16[4096,1024]{1,0:T(8,128)(2,1)} %all-gather.21.cloned.1.call-done), kind=kOutput, calls=%fused_computation.161 | convolution fusion | flops 6750203904 | bytes 29720576 | tf_op jit(solution)/shard_map/btw,fw->btf/dot_general | solution.py:17
  504.9 58.9 %all-gather.23.cloned.1.call-done = bf16[1024,4096]{1,0:T(8,128)(2,1)} async-done(((bf16[32,4096]{1,0:T(8,128)(2,1)}), bf16[1024,4096]{1,0:T(8,128)(2,1)}) %all-gather.23.cloned.1.call-update) | async-done | bytes 8388624 | tf_op jit(solution)/shard_map/all_gather | solution.py:111
  563.8 14.6 multiply_reduce_fusion.2
  578.5 4.7 fusion.101
  583.2 39.2 %all-gather.25.cloned.1.call-done = bf16[1024,1024]{1,0:T(8,128)(2,1)} async-done(((bf16[32,1024]{1,0:T(8,128)(2,1)}), bf16[1024,1024]{1,0:T(8,128)(2,1)}) %all-gather.25.cloned.1.call-update) | async-done | bytes 2097168 | tf_op jit(solution)/shard_map/all_gather | solution.py:111
  622.4 6.8 convolution_convert_fusion
  631.1 7.1 fusion.60
  638.2 16.7 fusion.63
  654.9 15.9 fusion.66
  670.8 9.2 convolution_bitcast_fusion.3
  680.0 49.0 %all-gather.27.cloned.1.call-done = bf16[1024,3,16,64]{3,0,2,1:T(8,128)(2,1)} async-done(((bf16[32,3,16,64]{3,0,2,1:T(8,128)(2,1)}), bf16[1024,3,16,64]{3,0,2,1:T(8,128)(2,1)}) %all-gather.27.cloned.1.call-update) | async-done | bytes 6291472 | tf_op jit(solution)/shard_map/all_gather | solution.py:111
  729.0 24.9 %fusion.44 = (f32[1024]{0:T(1024)}, f32[16,50]{1,0:T(8,128)S(1)}, f32[16,50]{1,0:T(8,128)S(1)}, f32[1024]{0:T(1024)}, f32[16,50,1024,1,1]{2,1,4,0,3:T(8,128)}) fusion(f32[16,50]{1,0:T(8,128)S(1)} %copy-done.30, f32[16,50]{1,0:T(8,128)S(1)} %copy-done.27, f32[1024]{0:T(1024)S(1)} %convert_element_type.185, f32[1024]{0:T(1024)S(1)} %convert_element_type.183, ...), kind=kOutput, calls=%fused_computation.68 | convolution fusion | flops 5049544704 | bytes 22715136 | tf_op jit(solution)/shard_map/btchd,wchd->btw/dot_general | solution.py:17
  753.9 7.2 multiply_reduce_fusion.3
  767.1 3.9 fusion.2
  773.5 24.7 %convolution_bitcast_fusion = f32[1024,3,16,64]{3,0,2,1:T(8,128)} fusion(f32[1024]{0:T(1024)S(1)} %copy-done.37, f32[1024]{0:T(1024)S(1)} %copy-done.35, f32[16,50]{1,0:T(8,128)S(1)} %copy-done.30, f32[16,50]{1,0:T(8,128)S(1)} %copy-done.27, f32[16,50,1,16,64]{4,1,3,0,2:T(8,128)} %convolution_bitcast_fusion.3, f32[16,50,1,16,64]{4,1,3,0,2:T(8,128)} %fusion.66, ...), kind=kOutput, calls=%fused_computation.38 | convolution fusion | flops 5056102400 | bytes 25719296 | tf_op jit(solution)/shard_map/btw,btchd->wchd/dot_general | solution.py:17
  799.7 5.6 convolution_bitcast_fusion.4
  805.6 7.7 fusion.46
  814.8 14.9 convolution_bitcast_fusion.1
  830.5 16.0 convolution_bitcast_fusion.2
  847.9 2.1 copy.80
  850.0 64.4 %all-reduce.31.cloned.1.call-done = (f32[1024]{0:T(1024)}, f32[1024]{0:T(1024)}, f32[1024]{0:T(1024)}, f32[1024]{0:T(1024)}, f32[1024]{0:T(1024)}, /*index=5*/f3...) async-done(((f32[1024]{0:T(1024)}, f32[1024]{0:T(1024)}, f32[1024]{0:T(1024)}, ...) | async-done | bytes 69648
  929.5 230.5 %reduce-scatter.11.cloned.1.call-done = f32[32,3,16,64]{3,0,2,1:T(8,128)} async-done(((f32[1024,3,16,64]{3,0,2,1:T(8,128)}), f32[32,3,16,64]{3,0,2,1:T(8,128)}) %reduce-scatter.11.cloned.1.call-update) | async-done | bytes 393232 | tf_op jit(solution)/shard_map/reduce_scatter | solution.py:121
  1160.0 2.5 copy.82
  1162.5 136.3 %reduce-scatter.19.cloned.1.call-done = f32[32,197]{1,0:T(8,128)} async-done(((f32[1024,197]{1,0:T(8,128)}), f32[32,197]{1,0:T(8,128)}) %reduce-scatter.19.cloned.1.call-update) | async-done | bytes 25232
  1298.8 103.9 %reduce-scatter.9.cloned.1.call-done = f32[768,32]{0,1:T(8,128)} async-done(((f32[768,1024]{0,1:T(8,128)}), f32[768,32]{0,1:T(8,128)}) %reduce-scatter.9.cloned.1.call-update) | async-done | bytes 98320 | tf_op jit(solution)/shard_map/reduce_scatter | solution.py:121
  1402.7 143.5 %reduce-scatter.13.cloned.1.call-done = f32[32,1024]{1,0:T(8,128)} async-done(((f32[1024,1024]{1,0:T(8,128)}), f32[32,1024]{1,0:T(8,128)}) %reduce-scatter.13.cloned.1.call-update) | async-done | bytes 131088 | tf_op jit(solution)/shard_map/reduce_scatter | solution.py:121
  1546.2 181.4 %reduce-scatter.17.cloned.1.call-done = f32[128,1024]{1,0:T(8,128)} async-done(((f32[4096,1024]{1,0:T(8,128)}), f32[128,1024]{1,0:T(8,128)}) %reduce-scatter.17.cloned.1.call-update) | async-done | bytes 524304 | tf_op jit(solution)/shard_map/reduce_scatter | solution.py:121
  1727.6 187.3 %reduce-scatter.15.cloned.1.call-done = f32[32,4096]{1,0:T(8,128)} async-done(((f32[1024,4096]{1,0:T(8,128)}), f32[32,4096]{1,0:T(8,128)}) %reduce-scatter.15.cloned.1.call-update) | async-done | bytes 524304 | tf_op jit(solution)/shard_map/reduce_scatter | solution.py:121
  (248 shorter events, 54.3 us)
Async XLA Ops:
  7.2 9.4 copy-start.38
  7.2 9.4 copy-start.39
  7.2 9.4 copy-start.40
  7.2 9.4 copy-start.49
  7.2 9.4 copy-start.41
  7.2 9.4 copy-start.48
  7.3 9.4 copy-start.42
  7.3 9.4 copy-start.43
  7.3 9.4 copy-start.47
  7.3 9.5 copy-start.44
  7.3 9.5 copy-start.45
  7.3 54.7 %copy-start.31 = (f32[197,32]{0,1:T(8,128)S(1)}, f32[197,32]{0,1:T(8,128)}, u32[]{:S(2)}) copy-start(f32[197,32]{0,1:T(8,128)} %param.25) | copy-start | bytes 75652
  7.3 96.6 %copy-start.46 = (f32[128]{0:T(128)S(1)}, f32[128]{0:T(128)}, u32[]{:S(2)}) copy-start(f32[128]{0:T(128)} %param.38) | copy-start | bytes 1540
  7.3 133.7 %copy-start.32 = (s32[16,49]{1,0:T(8,128)S(1)}, s32[16,49]{1,0:T(8,128)}, u32[]{:S(2)}) copy-start(s32[16,49]{1,0:T(8,128)} %param.22) | copy-start | bytes 9412
  7.3 139.2 %all-gather.11.cloned.1.call-start = ((), (), s32[]{:S(2)}) async-start(), calls=%async_computation.6 | async-start | bytes 1622016 | tf_op jit(solution)/shard_map/all_gather | solution.py:111
  9.0 168.2 %all-gather.13.cloned.1.call-start = ((), (), s32[]{:S(2)}) async-start(), calls=%async_computation.7 | async-start | bytes 12976128 | tf_op jit(solution)/shard_map/all_gather | solution.py:111
  11.2 224.4 %all-gather.15.cloned.1.call-start = ((), (), s32[]{:S(2)}) async-start(), calls=%async_computation.8 | async-start | bytes 2162688 | tf_op jit(solution)/shard_map/all_gather | solution.py:111
  12.8 301.9 %all-gather.17.cloned.1.call-start = ((), (), s32[]{:S(2)}) async-start(), calls=%async_computation.9 | async-start | bytes 8650752 | tf_op jit(solution)/shard_map/all_gather | solution.py:111
  14.6 379.1 %all-gather.19.cloned.1.call-start = ((), (), s32[]{:S(2)}) async-start(), calls=%async_computation.10 | async-start | bytes 8650752 | tf_op jit(solution)/shard_map/all_gather | solution.py:111
  16.5 468.0 %all-gather.21.cloned.1.call-start = ((), (), s32[]{:S(2)}) async-start(), calls=%async_computation.11 | async-start | bytes 8650752 | tf_op jit(solution)/shard_map/all_gather | solution.py:111
  103.7 73.4 %copy-start.34 = (f32[1024]{0:T(1024)}, f32[1024]{0:T(1024)S(1)}, u32[]{:S(2)}) copy-start(f32[1024]{0:T(1024)S(1)} %convert_element_type.187) | copy-start | bytes 12292
  103.8 73.4 %copy-start.36 = (f32[1024]{0:T(1024)}, f32[1024]{0:T(1024)S(1)}, u32[]{:S(2)}) copy-start(f32[1024]{0:T(1024)S(1)} %convert_element_type.189) | copy-start | bytes 12292
  103.9 210.8 %copy-start.22 = (f32[1024]{0:T(1024)}, f32[1024]{0:T(1024)S(1)}, u32[]{:S(2)}) copy-start(f32[1024]{0:T(1024)S(1)} %convert_element_type.201) | copy-start | bytes 12292
  103.9 210.8 %copy-start.24 = (f32[1024]{0:T(1024)}, f32[1024]{0:T(1024)S(1)}, u32[]{:S(2)}) copy-start(f32[1024]{0:T(1024)S(1)} %convert_element_type.203) | copy-start | bytes 12292
  153.6 42.0 %copy-start.26 = (f32[16,50]{1,0:T(8,128)}, f32[16,50]{1,0:T(8,128)S(1)}, u32[]{:S(2)}) copy-start(f32[16,50]{1,0:T(8,128)S(1)} %broadcast_multiply_fusion.7) | copy-start | bytes 9604
  155.4 40.2 %copy-start.29 = (f32[16,50]{1,0:T(8,128)}, f32[16,50]{1,0:T(8,128)S(1)}, u32[]{:S(2)}) copy-start(f32[16,50]{1,0:T(8,128)S(1)} %add_rsqrt_fusion.1) | copy-start | bytes 9604
  242.1 336.3 %copy-start.17 = (f32[16,50]{1,0:T(8,128)}, f32[16,50]{1,0:T(8,128)S(1)}, u32[]{:S(2)}) copy-start(f32[16,50]{1,0:T(8,128)S(1)} %broadcast_multiply_fusion.6) | copy-start | bytes 9604
  244.6 333.8 %copy-start.19 = (f32[16,50]{1,0:T(8,128)}, f32[16,50]{1,0:T(8,128)S(1)}, u32[]{:S(2)}) copy-start(f32[16,50]{1,0:T(8,128)S(1)} %add_rsqrt_fusion) | copy-start | bytes 9604
  370.8 36.9 %copy-start.10 = (f32[128,1024]{1,0:T(8,128)S(1)}, f32[128,1024]{1,0:T(8,128)}, u32[]{:S(2)}) copy-start(f32[128,1024]{1,0:T(8,128)} %param.39) | copy-start | bytes 1572868
  370.8 37.7 %copy-start.11 = (f32[32,4096]{1,0:T(8,128)S(1)}, f32[32,4096]{1,0:T(8,128)}, u32[]{:S(2)}) copy-start(f32[32,4096]{1,0:T(8,128)} %param.37) | copy-start | bytes 1572868
  370.8 38.5 %copy-start.21 = (f32[32,1024]{1,0:T(8,128)S(1)}, f32[32,1024]{1,0:T(8,128)}, u32[]{:S(2)}) copy-start(f32[32,1024]{1,0:T(8,128)} %param.33) | copy-start | bytes 393220
  370.8 39.3 %copy-start.9 = (f32[32,3,16,64]{3,2,1,0:T(8,128)S(1)}, f32[32,3,16,64]{3,2,1,0:T(8,128)}, u32[]{:S(2)}) copy-start(f32[32,3,16,64]{3,2,1,0:T(8,128)} %param.31) | copy-start | bytes 1179652
  408.4 155.3 %all-gather.23.cloned.1.call-start = ((), (), s32[]{:S(2)}) async-start(), calls=%async_computation.12 | async-start | bytes 8650752 | tf_op jit(solution)/shard_map/all_gather | solution.py:111
  409.2 213.1 %all-gather.25.cloned.1.call-start = ((), (), s32[]{:S(2)}) async-start(), calls=%async_computation.13 | async-start | bytes 2162688 | tf_op jit(solution)/shard_map/all_gather | solution.py:111
  410.0 319.0 %all-gather.27.cloned.1.call-start = ((), (), s32[]{:S(2)}) async-start(), calls=%async_computation.14 | async-start | bytes 12976128 | tf_op jit(solution)/shard_map/all_gather | solution.py:111
  563.8 14.7 copy-start.3
  563.8 14.7 copy-start.13
  670.8 58.2 %copy-start.27 = (f32[16,50]{1,0:T(8,128)S(1)}, f32[16,50]{1,0:T(8,128)}, u32[]{:S(2)}) copy-start(f32[16,50]{1,0:T(8,128)} %copy-done.26) | copy-start | bytes 9604
  670.8 58.2 %copy-start.30 = (f32[16,50]{1,0:T(8,128)S(1)}, f32[16,50]{1,0:T(8,128)}, u32[]{:S(2)}) copy-start(f32[16,50]{1,0:T(8,128)} %copy-done.29) | copy-start | bytes 9604
  753.9 9.7 slice-start.2
  753.9 9.7 copy-start.7
  772.8 141.5 %all-reduce.31.cloned.1.call-start = ((), (), s32[]{:S(2)}) async-start(), calls=%async_computation.21 | async-start | bytes 139264
  773.4 386.6 %reduce-scatter.11.cloned.1.call-start = ((), (), s32[]{:S(2)}) async-start(), calls=%async_computation.16 | async-start | bytes 25952256 | tf_op jit(solution)/shard_map/reduce_scatter | solution.py:121
  798.2 500.6 %reduce-scatter.19.cloned.1.call-start = ((), (), s32[]{:S(2)}) async-start(), calls=%async_computation.20 | async-start | bytes 1081344
  799.6 603.1 %reduce-scatter.9.cloned.1.call-start = ((), (), s32[]{:S(2)}) async-start(), calls=%async_computation.15 | async-start | bytes 3244032 | tf_op jit(solution)/shard_map/reduce_scatter | solution.py:121
  805.3 740.9 %reduce-scatter.13.cloned.1.call-start = ((), (), s32[]{:S(2)}) async-start(), calls=%async_computation.17 | async-start | bytes 4325376 | tf_op jit(solution)/shard_map/reduce_scatter | solution.py:121
  813.4 914.2 %reduce-scatter.17.cloned.1.call-start = ((), (), s32[]{:S(2)}) async-start(), calls=%async_computation.19 | async-start | bytes 17301504 | tf_op jit(solution)/shard_map/reduce_scatter | solution.py:121
  829.8 1085.1 %reduce-scatter.15.cloned.1.call-start = ((), (), s32[]{:S(2)}) async-start(), calls=%async_computation.18 | async-start | bytes 17301504 | tf_op jit(solution)/shard_map/reduce_scatter | solution.py:121
  (22 other events, 71.4 us)
Sparse Core Ops, SparseCore 0:
  11.6 57.7 all-gather.10
  72.8 104.2 all-gather.12
  180.6 54.9 all-gather.14
  238.9 75.7 all-gather.16
  317.9 75.7 all-gather.18
  408.6 75.9 all-gather.20
  487.9 75.7 all-gather.22
  567.2 55.1 all-gather.24
  625.9 103.0 all-gather.26
  780.3 133.9 all-reduce.30
  920.8 239.1 reduce-scatter.10
  1162.7 136.0 reduce-scatter.18
  1304.8 97.8 reduce-scatter.8
  1405.4 140.7 reduce-scatter.12
  1548.9 178.5 reduce-scatter.16
  1730.3 184.4 reduce-scatter.14
where the time goes:
time: 1930 us; the launch traced here: 1920 us
  waiting for transfers between devices  1370 us (71%)
  matrix products  260 us (13%)
  blocking collectives  162 us (8%)
  other arithmetic  71.9 us (4%)
  local copies, waits for them, and re-layouts  43.8 us (2%)
    reduce_scatter x5, waiting for transfers between devices, local_step(): lax.psum_scatter(grad_map[name], MESH_AXIS, scatter_dimension=split_of(na...  847 us
    all_gather x9, waiting for transfers between devices, gather_whole(): lax.all_gather(shard.astype(jnp.bfloat16), MESH_AXIS, axis=split_of(name)...  320 us
    dot_general x23, matrix products, product(): jnp.einsum(einsum_form, left_op, right_op, preferred_element_type=jnp.flo...  260 us
    unnamed x18, waiting for transfers between devices  201 us
    unnamed x2, blocking collectives  82.9 us
    all_gather x2, blocking collectives, gather_whole(): lax.all_gather(shard.astype(jnp.bfloat16), MESH_AXIS, axis=split_of(name)...  78.6 us
    unnamed x152, local copies, waits for them, and re-layouts  42 us
  transfers between devices with their start and end apart: 16, of which 15 were waited for; matrix products, arithmetic and copies ran while one was open for 16% of the time, Pallas kernels for 0%

commit v1 on v0

--- a/solution.py
+++ b/solution.py
@@ -1,6 +1,8 @@
 import jax
 import jax.numpy as jnp
 from jax import lax
+from jax.experimental import pallas as pl
+from jax.experimental.pallas import tpu as pltpu
 from jax.sharding import PartitionSpec as P
 
 MESH_AXIS = 'fsdp'
@@ -9,7 +11,6 @@
 INV_SQRT_2PI = 0.3989422804014327
 PARAM_NAMES = ('w_patch', 'b_patch', 'pos_table', 'cls_tok', 'lnp_g', 'lnp_b', 'ln1_g', 'ln1_b', 'w_qkv', 'b_qkv', 'w_out', 'b_out', 'ln2_g', 'ln2_b', 'w_fc', 'b_fc', 'w_proj', 'b_proj')
 VECTOR_NAMES = ('b_patch', 'cls_tok', 'lnp_g', 'lnp_b', 'ln1_g', 'ln1_b', 'b_qkv', 'b_out', 'ln2_g', 'ln2_b', 'b_fc', 'b_proj')
-BACKWARD_NAMES = ('w_qkv', 'w_out', 'w_fc', 'w_proj', 'lnp_g', 'ln1_g', 'ln2_g')
 LAST_SPLIT = ('w_patch', 'pos_table')
 
 
@@ -100,26 +101,318 @@
     return dict(w_patch=product('bkq,bkw->qw', saved['kept_rows'], d_emb_b), b_patch=jnp.sum(d_emb, axis=(0, 1)), pos_table=g_pos, cls_tok=d_head, lnp_g=g_lnp_g, lnp_b=g_lnp_b, ln1_g=g_ln1_g, ln1_b=g_ln1_b, w_qkv=g_w_qkv, b_qkv=jnp.sum(d_qkv, axis=(0, 1)).reshape(-1), w_out=g_w_out, b_out=jnp.sum(d_mid, axis=(0, 1)), ln2_g=g_ln2_g, ln2_b=g_ln2_b, w_fc=g_w_fc, b_fc=jnp.sum(d_pre, axis=(0, 1)), w_proj=g_w_proj, b_proj=jnp.sum(d_h, axis=(0, 1)))
 
 
+RINGS = (
+    (0, 4, 8, 10, 11, 15, 14, 12, 13, 9, 5, 7, 6, 2, 3, 1),
+    (0, 2, 3, 7, 11, 9, 8, 12, 13, 15, 14, 10, 6, 4, 5, 1),
+    (0, 1, 3, 7, 5, 4, 8, 9, 11, 15, 13, 12, 14, 10, 6, 2),
+    (0, 1, 5, 7, 3, 2, 6, 10, 14, 15, 11, 9, 13, 12, 8, 4),
+    (0, 4, 6, 7, 11, 10, 8, 12, 14, 15, 13, 9, 5, 1, 3, 2),
+    (0, 2, 6, 7, 3, 1, 5, 9, 13, 15, 11, 10, 14, 12, 8, 4),
+)
+N_CHIP = 16
+MESH_ID = pl.DeviceIdType.MESH
+ARRAYS = ((32, 4096), (128, 1024), (32, 3072), (32, 1024), (32, 1024))
+FC, PROJ, QKV, OUT, MISC = range(5)
+GATHER_STREAMS = (
+    (MISC, 0, 32, 0, 256, 0), (MISC, 0, 32, 256, 256, 1), (MISC, 0, 32, 512, 256, 2), (MISC, 0, 32, 768, 256, 3),
+    (QKV, 0, 32, 0, 2048, 4), (QKV, 0, 32, 2048, 1024, 5), (OUT, 0, 32, 0, 1024, 5),
+    (FC, 0, 32, 0, 2048, 0), (FC, 0, 32, 2048, 2048, 1), (PROJ, 0, 64, 0, 1024, 2), (PROJ, 64, 64, 0, 1024, 3),
+)
+REDUCE_STREAMS = (
+    (FC, 0, 64, 0, 1024, 0), (FC, 0, 64, 1024, 1024, 1), (PROJ, 0, 128, 0, 512, 2), (PROJ, 128, 128, 0, 512, 3),
+    (QKV, 0, 64, 0, 1024, 4), (QKV, 0, 64, 1024, 512, 5), (OUT, 0, 64, 0, 512, 5),
+    (MISC, 0, 64, 0, 128, 0), (MISC, 0, 64, 128, 128, 1), (MISC, 0, 64, 256, 128, 2), (MISC, 0, 64, 384, 128, 3),
+)
+
+
+def pick(table, index):
+    value = jnp.int32(table[0])
+    for place in range(1, len(table)):
+        value = jnp.where(index == place, jnp.int32(table[place]), value)
+    return value
+
+
+class Place:
+    def __init__(self):
+        me = lax.axis_index(MESH_AXIS)
+        self.core = lax.rem(me, 2)
+        self.chip = lax.div(me, 2)
+        self.sibling = me + 1 - 2 * self.core
+        where_in = [[ring.index(chip) for chip in range(N_CHIP)] for ring in RINGS]
+        self.spot = [pick(table, self.chip) for table in where_in]
+        self.after = [2 * pick([ring[(table[chip] + 1) % N_CHIP] for chip in range(N_CHIP)], self.chip) + self.core
+                      for ring, table in zip(RINGS, where_in)]
+        self.before = [2 * pick([ring[(table[chip] - 1) % N_CHIP] for chip in range(N_CHIP)], self.chip) + self.core
+                       for ring, table in zip(RINGS, where_in)]
+
+    def chips_back(self, steps):
+        return [pick(ring, lax.rem(self.spot[k] + 2 * N_CHIP - steps, N_CHIP)) for k, ring in enumerate(RINGS)]
+
+    def meet(self):
+        barrier = pltpu.get_barrier_semaphore()
+        for other in self.after + self.before + [self.sibling]:
+            pl.semaphore_signal(barrier, inc=1, device_id=(other,), device_id_type=MESH_ID)
+        pl.semaphore_wait(barrier, 2 * len(RINGS) + 1)
+
+
+def gather_kernel(*refs):
+    shards, wholes = refs[:5], refs[5:10]
+    own_sem, send_sem, recv_sem, twin_send, twin_recv = refs[10:]
+    place = Place()
+
+    def block(i, chip, core):
+        arr, row, rows, col, cols, _ = GATHER_STREAMS[i]
+        first = (2 * chip + core) * ARRAYS[arr][0] + row
+        return wholes[arr].at[pl.ds(pl.multiple_of(first, 32), rows), pl.ds(col, cols)]
+
+    def remote(src, dst, sems, i, step, device):
+        return pltpu.make_async_remote_copy(src_ref=src, dst_ref=dst, send_sem=sems[0].at[i, step], recv_sem=sems[1].at[i, step],
+                                            device_id=(device,), device_id_type=MESH_ID)
+
+    place.meet()
+    n_streams = len(GATHER_STREAMS)
+    for i in range(n_streams):
+        arr, row, rows, col, cols, k = GATHER_STREAMS[i]
+        mine = shards[arr].at[pl.ds(row, rows), pl.ds(col, cols)]
+        here = block(i, place.chip, place.core)
+        remote(mine, here, (send_sem, recv_sem), i, 0, place.after[k]).start()
+        remote(mine, here, (twin_send, twin_recv), i, 0, place.sibling).start()
+    for arr in range(5):
+        rows = ARRAYS[arr][0]
+        first = pl.multiple_of((2 * place.chip + place.core) * rows, 32)
+        pltpu.make_async_copy(shards[arr], wholes[arr].at[pl.ds(first, rows), :], own_sem.at[arr]).start()
+
+    def ring_step(step, carry):
+        chips = place.chips_back(step)
+        for i in range(n_streams):
+            k = GATHER_STREAMS[i][5]
+            here = block(i, chips[k], place.core)
+            remote(here, here, (send_sem, recv_sem), i, step - 1, place.after[k]).wait_recv()
+
+            @pl.when(step < N_CHIP - 1)
+            def _():
+                remote(here, here, (send_sem, recv_sem), i, step, place.after[k]).start()
+
+            remote(here, here, (twin_send, twin_recv), i, step, place.sibling).start()
+        return carry
+
+    lax.fori_loop(1, N_CHIP, ring_step, 0)
+
+    def drain(step, carry):
+        chips = place.chips_back(step)
+        for i in range(n_streams):
+            k = GATHER_STREAMS[i][5]
+            here = block(i, chips[k], place.core)
+            there = block(i, chips[k], 1 - place.core)
+
+            @pl.when(step < N_CHIP - 1)
+            def _():
+                remote(here, here, (send_sem, recv_sem), i, step, place.after[k]).wait_send()
+
+            remote(here, here, (twin_send, twin_recv), i, step, place.sibling).wait_send()
+            remote(there, there, (twin_send, twin_recv), i, step, place.sibling).wait_recv()
+        return carry
+
+    lax.fori_loop(0, N_CHIP, drain, 0)
+    for arr in range(5):
+        rows = ARRAYS[arr][0]
+        first = pl.multiple_of((2 * place.chip + place.core) * rows, 32)
+        pltpu.make_async_copy(shards[arr], wholes[arr].at[pl.ds(first, rows), :], own_sem.at[arr]).wait()
+
+
+def gather_all(shards):
+    n_streams = len(GATHER_STREAMS)
+    ring_sems, twin_sems = pltpu.SemaphoreType.DMA((n_streams, N_CHIP - 1)), pltpu.SemaphoreType.DMA((n_streams, N_CHIP))
+    return pl.pallas_call(
+        gather_kernel,
+        out_shape=[jax.ShapeDtypeStruct((2 * N_CHIP * rows, cols), jnp.bfloat16) for rows, cols in ARRAYS],
+        in_specs=[pl.BlockSpec(memory_space=pltpu.VMEM)] * 5,
+        out_specs=[pl.BlockSpec(memory_space=pl.ANY)] * 5,
+        scratch_shapes=[pltpu.SemaphoreType.DMA((5,)), ring_sems, ring_sems, twin_sems, twin_sems],
+        compiler_params=pltpu.CompilerParams(collective_id=0, has_side_effects=True),
+        name='gather_all',
+    )(*shards)
+
+
+def reduce_kernel(*refs):
+    grads, outs = refs[:5], refs[5:10]
+    accs, owns, twins = refs[10:15], refs[15:20], refs[20:25]
+    own_sem, twin_send, twin_recv, send_sem, recv_sem, ring_free, twin_free, end_own, end_send, end_recv = refs[25:]
+    place = Place()
+    n_streams = len(REDUCE_STREAMS)
+
+    def part(i, ref, slot):
+        _, row, rows, col, cols, _ = REDUCE_STREAMS[i]
+        return ref.at[slot, pl.ds(row, rows), pl.ds(col, cols)]
+
+    def source(i, chip, core):
+        arr, row, rows, col, cols, _ = REDUCE_STREAMS[i]
+        half = ARRAYS[arr][1] // 2
+        first = pl.multiple_of(2 * chip * ARRAYS[arr][0] + row, 64)
+        return grads[arr].at[pl.ds(first, rows), pl.ds(pl.multiple_of(core * half + col, 128), cols)]
+
+    def load(i, chip, slot):
+        return pltpu.make_async_copy(source(i, chip, place.core), part(i, owns[REDUCE_STREAMS[i][0]], slot), own_sem.at[i, slot])
+
+    def push(i, chip, slot):
+        return pltpu.make_async_remote_copy(src_ref=source(i, chip, 1 - place.core), dst_ref=part(i, twins[REDUCE_STREAMS[i][0]], slot),
+                                            send_sem=twin_send.at[i, slot], recv_sem=twin_recv.at[i, slot],
+                                            device_id=(place.sibling,), device_id_type=MESH_ID)
+
+    def pass_on(i, slot, slot_next):
+        arr, k = REDUCE_STREAMS[i][0], REDUCE_STREAMS[i][5]
+        return pltpu.make_async_remote_copy(src_ref=part(i, accs[arr], slot), dst_ref=part(i, accs[arr], slot_next),
+                                            send_sem=send_sem.at[i, slot], recv_sem=recv_sem.at[i, slot_next],
+                                            device_id=(place.after[k],), device_id_type=MESH_ID)
+
+    place.meet()
+    for step in range(2):
+        chips = place.chips_back(step + 1)
+        for i in range(n_streams):
+            load(i, chips[REDUCE_STREAMS[i][5]], step).start()
+            push(i, chips[REDUCE_STREAMS[i][5]], step).start()
+
+    def ring_step(step, carry):
+        slot, pair = lax.rem(step, 3), lax.rem(step, 2)
+        slot_next, slot_last = lax.rem(step + 1, 3), lax.rem(step + 2, 3)
+        chips = place.chips_back(step + 3)
+        for i in range(n_streams):
+            arr, row, rows, col, cols, k = REDUCE_STREAMS[i]
+            load(i, chips[k], pair).wait()
+            push(i, chips[k], pair).wait_recv()
+
+            @pl.when(step == 0)
+            def _():
+                def add_two(r, c):
+                    at = pl.ds(pl.multiple_of(row + 8 * r, 8), 8)
+                    lanes = pl.ds(col, cols)
+                    accs[arr][slot, at, lanes] = owns[arr][pair, at, lanes] + twins[arr][pair, at, lanes]
+                    return c
+                lax.fori_loop(0, rows // 8, add_two, 0)
+
+            @pl.when(step > 0)
+            def _():
+                pass_on(i, slot, slot).wait_recv()
+
+                def add_three(r, c):
+                    at = pl.ds(pl.multiple_of(row + 8 * r, 8), 8)
+                    lanes = pl.ds(col, cols)
+                    accs[arr][slot, at, lanes] = accs[arr][slot, at, lanes] + (owns[arr][pair, at, lanes] + twins[arr][pair, at, lanes])
+                    return c
+                lax.fori_loop(0, rows // 8, add_three, 0)
+
+            @pl.when(jnp.logical_and(step >= 2, step < N_CHIP - 1))
+            def _():
+                pl.semaphore_wait(ring_free.at[i], 1)
+
+            @pl.when(step < N_CHIP - 1)
+            def _():
+                pass_on(i, slot, slot_next).start()
+
+            @pl.when(step < N_CHIP - 2)
+            def _():
+                pl.semaphore_signal(twin_free.at[i], inc=1, device_id=(place.sibling,), device_id_type=MESH_ID)
+                load(i, chips[k], pair).start()
+
+        for i in range(n_streams):
+            k = REDUCE_STREAMS[i][5]
+            push(i, chips[k], pair).wait_send()
+
+            @pl.when(step < N_CHIP - 2)
+            def _():
+                pl.semaphore_wait(twin_free.at[i], 1)
+                push(i, chips[k], pair).start()
+
+            @pl.when(step >= 1)
+            def _():
+                pass_on(i, slot_last, slot).wait_send()
+
+            @pl.when(jnp.logical_and(step >= 1, step < N_CHIP - 2))
+            def _():
+                pl.semaphore_signal(ring_free.at[i], inc=1, device_id=(place.before[k],), device_id_type=MESH_ID)
+        return carry
+
+    lax.fori_loop(0, N_CHIP, ring_step, 0)
+    last = (N_CHIP - 1) % 3
+
+    def end_copies(arr):
+        rows, half = ARRAYS[arr][0], ARRAYS[arr][1] // 2
+        target = outs[arr].at[:, pl.ds(pl.multiple_of(place.core * half, 128), half)]
+        keep_rows = accs[arr].at[last, pl.ds(pl.multiple_of(place.core * rows, 32), rows), :]
+        give_rows = accs[arr].at[last, pl.ds(pl.multiple_of((1 - place.core) * rows, 32), rows), :]
+        return (pltpu.make_async_copy(keep_rows, target, end_own.at[arr]),
+                pltpu.make_async_remote_copy(src_ref=give_rows, dst_ref=target, send_sem=end_send.at[arr], recv_sem=end_recv.at[arr],
+                                             device_id=(place.sibling,), device_id_type=MESH_ID))
+
+    for arr in range(5):
+        local, cross = end_copies(arr)
+        local.start()
+        cross.start()
+    for arr in range(5):
+        local, cross = end_copies(arr)
+        local.wait()
+        cross.wait()
+
+
+def reduce_all(grads):
+    n_streams = len(REDUCE_STREAMS)
+    slots = lambda n: [pltpu.VMEM((n, 2 * rows, cols // 2), jnp.float32) for rows, cols in ARRAYS]
+    sems = lambda n: pltpu.SemaphoreType.DMA((n_streams, n))
+    return pl.pallas_call(
+        reduce_kernel,
+        out_shape=[jax.ShapeDtypeStruct((rows, cols), jnp.float32) for rows, cols in ARRAYS],
+        in_specs=[pl.BlockSpec(memory_space=pl.ANY)] * 5,
+        out_specs=[pl.BlockSpec(memory_space=pl.ANY)] * 5,
+        scratch_shapes=slots(3) + slots(2) + slots(2) + [
+            sems(2), sems(2), sems(2), sems(3), sems(3),
+            pltpu.SemaphoreType.REGULAR((n_streams,)), pltpu.SemaphoreType.REGULAR((n_streams,)),
+            pltpu.SemaphoreType.DMA((5,)), pltpu.SemaphoreType.DMA((5,)), pltpu.SemaphoreType.DMA((5,)),
+        ],
+        compiler_params=pltpu.CompilerParams(collective_id=1, has_side_effects=True),
+        name='reduce_all',
+    )(*grads)
+
+
+ROW_VECTORS = ('b_patch', 'cls_tok', 'lnp_g', 'lnp_b', 'ln1_g', 'ln1_b', 'b_out', 'ln2_g', 'ln2_b', 'b_proj')
+N_PIXEL, N_POS = 768, 197
+MISC_USED = N_PIXEL + N_POS + len(ROW_VECTORS) + 3 + 4
+
+
 def solution(mesh):
-    def split_of(name):
-        return 1 if name in LAST_SPLIT else 0
-
     def spec_of(name):
         return P(None, MESH_AXIS) if name in LAST_SPLIT else P(MESH_AXIS)
 
-    def gather_whole(shard, name):
-        return lax.all_gather(shard.astype(jnp.bfloat16), MESH_AXIS, axis=split_of(name), tiled=True)
+    def pack_misc(part):
+        rows = part['w_patch'].shape[1]
+        columns = [part['w_patch'].T, part['pos_table'].T] + [part[name][:, None] for name in ROW_VECTORS]
+        columns += [part['b_qkv'].reshape(rows, 3), part['b_fc'].reshape(rows, 4)]
+        return jnp.pad(jnp.concatenate(columns, axis=1), ((0, 0), (0, 1024 - MISC_USED)))
+
+    def unpack_misc(misc):
+        part = {'w_patch': misc[:, :N_PIXEL].T, 'pos_table': misc[:, N_PIXEL:N_PIXEL + N_POS].T}
+        first = N_PIXEL + N_POS
+        for name in ROW_VECTORS:
+            part[name] = misc[:, first]
+            first += 1
+        part['b_qkv'] = misc[:, first:first + 3].reshape(-1)
+        part['b_fc'] = misc[:, first + 3:first + 7].reshape(-1)
+        return part
 
     def local_step(patches, keep, *rest):
         shards = dict(zip(PARAM_NAMES, rest[:-1]))
         grad_h1 = rest[-1]
-        full_w = {name: gather_whole(shards[name], name) for name in PARAM_NAMES}
+        n_rows, _, n_heads, head_dim = shards['w_qkv'].shape
+        casts = {name: shards[name].astype(jnp.bfloat16) for name in PARAM_NAMES}
+        w_fc, w_proj, w_qkv, w_out, misc = gather_all((casts['w_fc'], casts['w_proj'], casts['w_qkv'].reshape(n_rows, -1), casts['w_out'], pack_misc(casts)))
+        full_w = unpack_misc(misc)
+        full_w.update(w_fc=w_fc, w_proj=w_proj, w_qkv=w_qkv.reshape(-1, 3, n_heads, head_dim), w_out=w_out)
         h_one, saved = forward(full_w, patches, keep)
-        held, h_one = lax.optimization_barrier((shards, h_one))
-        regathered = {name: gather_whole(held[name], name) for name in BACKWARD_NAMES}
-        grad_map = backward(regathered, saved, grad_h1)
-        summed = tuple(lax.psum_scatter(grad_map[name], MESH_AXIS, scatter_dimension=split_of(name), tiled=True) for name in PARAM_NAMES)
-        return (h_one,) + summed
+        grad_map = backward(full_w, saved, grad_h1)
+        d_model = w_out.shape[0]
+        sums = reduce_all((grad_map['w_fc'], grad_map['w_proj'], grad_map['w_qkv'].reshape(d_model, -1), grad_map['w_out'], pack_misc(grad_map)))
+        own = unpack_misc(sums[MISC])
+        own.update(w_fc=sums[FC], w_proj=sums[PROJ], w_qkv=sums[QKV].reshape(n_rows, 3, n_heads, head_dim), w_out=sums[OUT])
+        return (h_one,) + tuple(own[name] for name in PARAM_NAMES)
 
     batch_spec = P(MESH_AXIS)
     param_specs = tuple(spec_of(name) for name in PARAM_NAMES)

time: 1930 us -> 738 us (0.38)
  waiting for transfers between devices: 1370 us -> 0 us
  Pallas kernels: 0 us -> 308 us
  blocking collectives: 162 us -> 0 us
  local copies, waits for them, and re-layouts: 43.8 us -> 88.2 us
  other arithmetic: 71.9 us -> 96.3 us
  matrix products: 260 us -> 238 us
    reduce_scatter x5 -> x0, waiting for transfers between devices: 847 us -> none  [local_step(): lax.psum_scatter(grad_map[name], MESH_AXIS, scatter_dimension=split_of(na...]
    all_gather x9 -> x0, waiting for transfers between devices: 320 us -> none  [gather_whole(): lax.all_gather(shard.astype(jnp.bfloat16), MESH_AXIS, axis=split_of(name)...]
    pallas_call x0 -> x2, Pallas kernels: none -> 308 us  [the longest x1 199 us: reduce_all(): pl.pallas_call(reduce_kernel, out_shape=[jax.ShapeDtypeStruct((rows, cols...]
    unnamed x18 -> x0, waiting for transfers between devices: 201 us -> none
    unnamed x2 -> x0, blocking collectives: 82.9 us -> none
    all_gather x2 -> x0, blocking collectives: 78.6 us -> none  [gather_whole(): lax.all_gather(shard.astype(jnp.bfloat16), MESH_AXIS, axis=split_of(name)...]
    unnamed x152 -> x98, local copies, waits for them, and re-layouts: 42 us -> 13.3 us
    dot_general x23, matrix products: 260 us -> 238 us  [product(): jnp.einsum(einsum_form, left_op, right_op, preferred_element_type=jnp.flo...]
  transfers between devices with their start and end apart: 16 -> 0, of which waited for: 15 -> 0; matrix products, arithmetic and copies ran while one was open for 16% -> 0% of each run, Pallas kernels for 0% -> 0%
where the time goes in v1:
time: 738 us; the launch traced here: 733 us
  Pallas kernels  308 us (42%)
  matrix products  238 us (32%)
  other arithmetic  96.3 us (13%)
  local copies, waits for them, and re-layouts  88.2 us (12%)
    dot_general x23, matrix products, product(): jnp.einsum(einsum_form, left_op, right_op, preferred_element_type=jnp.flo...  238 us
    pallas_call x1, Pallas kernels, reduce_all(): pl.pallas_call(reduce_kernel, out_shape=[jax.ShapeDtypeStruct((rows, cols...  199 us
    pallas_call x1, Pallas kernels, gather_all(): pl.pallas_call(gather_kernel, out_shape=[jax.ShapeDtypeStruct((2 * N_CHIP...  109 us
    convert_element_type x1, other arithmetic, forward(): gelu_out = jax.nn.gelu(pre_act, approximate=False).astype(jnp.bfloat16)  36 us

profile of v1, /device:TPU:0, one launch (start us, length us, event | category | flops | bytes accessed | tf_op | source)
XLA Modules:
  0.0 732.9 jit_solution(4365382522173020681)
XLA Ops:
  13.8 1.8 convert_element_type.232.refs_0_
  15.6 1.8 convert_element_type.233.refs_1_
  19.5 6.5 fusion.71
  26.0 108.9 %gather_all.1 = (bf16[1024,4096]{1,0:T(8,128)(2,1)}, bf16[4096,1024]{1,0:T(8,128)(2,1)}, bf16[1024,3072]{1,0:T(8,128)(2,1)}, bf16[1024,1024]{1,0:T(8,128)(2,1)}, bf16[1024,1024]{1,0:T(8,128)(2,1)}) custom-call(bf16[32,4096]{1,0:T(8,128)(2,1)} %convert_element_type.232.refs_0_, bf16[128,1024]{1,0:T(8,128)(2,1)} %convert_element_type.233.refs_1_, ...), custom_call_target="tpu_custom_call" | custom-call | tf_op jit(solution)/shard_map/gather_all/pallas_call | solution.py:226
  134.9 8.7 %copy.114 = bf16[1024,3072]{0,1:T(8,128)(2,1)} copy(bf16[1024,3072]{1,0:T(8,128)(2,1)} %get-tuple-element.30) | data formatting | bytes 12582912 | tf_op jit(solution)/shard_map/gather_all/pallas_call | solution.py:226
  146.4 3.0 fusion.76
  154.4 18.7 %add_convert_fusion = bf16[16,50,3,16,64]{4,1,3,2,0:T(8,128)(2,1)} fusion(f32[3,16,64]{2,1,0:T(8,128)S(1)} %reshape.237, bf16[1024,3,16,64,1]{0,3,2,1,4:T(8,128)(2,1)S(1)} %bitcast.197, f32[1024]{0:T(1024)S(1)} %get-tuple-element.114, f32[1024]{0:T(1024)S(1)} %get-tuple-element.115, f32[16,50]{1,0:T(8,128)S(1)} %add_rsqrt_fusion.1, ...), kind=kOutput, calls=%fused_computation.4 | convolution fusion | flops 5046272000 | bytes 14524928 | tf_op jit(solution)/shard_map/btw,wchd->btchd/dot_general | solution.py:18
  173.1 5.4 fusion.60
  178.5 11.9 %fusion.94 = (f32[16,16,50]{2,1,0:T(8,128)S(1)}, f32[16,16,50,50]{2,3,1,0:T(8,128)S(1)}) fusion(f32[16,16,50,50]{2,3,1,0:T(8,128)S(1)} %fusion.60), kind=kOutput, calls=%fused_computation.193 | output fusion | flops 2560049 | bytes 5171200 | tf_op jit(solution)/shard_map/sub | solution.py:55
  190.4 3.0 copy-done.8
  193.4 6.2 fusion.61
  199.7 4.6 fusion.95
  204.8 20.4 %fusion.34 = (u16[50,4096]{1,0:T(8,128)(2,1)S(1)}, u16[50,4096]{1,0:T(8,128)(2,1)S(1)}, f32[16,50,4096]{2,1,0:T(8,128)}) fusion(f32[4096]{0:T(1024)S(1)} %reshape.241, bf16[1024,4096]{1,0:T(8,128)(2,1)} %get-tuple-element.32, f32[16,50,1024]{2,1,0:T(8,128)S(1)} %get-tuple-element.137, f32[1024]{0:T(1024)S(1)} %get-tuple-element.112, ...), kind=kOutput, calls=%fused_computation.53 | convolution fusion | flops 6760448000 | bytes 25622784 | tf_op jit(solution)/shard_map/btw,wf->btf/dot_general | solution.py:18
  225.2 36.0 %fusion.4 = bf16[16,50,4096]{2,1,0:T(8,128)(2,1)} fusion(f32[16,50,4096]{2,1,0:T(8,128)} %get-tuple-element.138, f32[4096]{0:T(1024)S(1)} %reshape.241, u16[50,4096]{1,0:T(8,128)(2,1)S(1)} %get-tuple-element.97, u16[50,4096]{1,0:T(8,128)(2,1)S(1)} %get-tuple-element.96), kind=kLoop, calls=%fused_computation.8 | loop fusion | flops 232652800 | bytes 20496384 | tf_op jit(solution)/shard_map/convert_element_type | solution.py:62
  261.2 18.4 %fusion.96 = (f32[4096]{0:T(1024)S(1)}, bf16[16,50,4096]{2,1,0:T(8,128)(2,1)}) fusion(f32[16,50,4096]{2,1,0:T(8,128)S(1)} %copy-done.7, f32[4096]{0:T(1024)S(1)} %reshape.241, bf16[16,50,1024]{2,0,1:T(8,128)(2,1)S(1)} %copy-done.18, bf16[4096,1024]{1,0:T(8,128)(2,1)} %get-tuple-element.33), kind=kOutput, calls=%fused_computation.195 | convolution fusion | flops 6750203904 | bytes 29720576 | tf_op jit(solution)/shard_map/btw,fw->btf/dot_general | solution.py:18
  279.6 12.5 %add_convert_fusion.1 = bf16[16,50,1024]{2,1,0:T(8,128)(2,1)S(1)} fusion(f32[16,50,1024]{2,1,0:T(8,128)S(1)} %get-tuple-element.137, f32[1024]{0:T(1024)S(1)} %get-tuple-element.111, bf16[16,50,4096]{2,1,0:T(8,128)(2,1)} %fusion.4, bf16[4096,1024]{1,0:T(8,128)(2,1)} %get-tuple-element.33), kind=kOutput, calls=%fused_computation.86 | convolution fusion | flops 6713344000 | bytes 19861504 | tf_op jit(solution)/shard_map/btf,fw->btw/dot_general | solution.py:18
  292.1 2.1 copy.139
  294.2 13.4 %multiply_reduce_fusion.2 = (f32[1024]{0:T(1024)S(1)}, f32[16,50]{1,0:T(8,128)S(1)}, f32[16,50]{1,0:T(8,128)S(1)}, f32[1024]{0:T(1024)S(1)}, f32[16,50,1024]{2,1,0:T(8,128)S(1)}) fusion(f32[16,50,1024]{2,1,0:T(8,128)S(1)} %get-tuple-element.137, f32[16,50]{1,0:T(8,128)S(1)} %add_rsqrt_fusion, f32[16,50]{1,0:T(8,128)S(1)} %broadcast_multiply_fusion.6, ...), kind=kOutput, calls=%fused_computation.77 | convolution fusion | flops 6718255104 | bytes 21520896 | tf_op jit(solution)/shard_map/btf,wf->btw/dot_general | solution.py:18
  307.6 4.1 fusion.93
  316.1 7.8 %fusion.44 = f32[16,64,1024,1]{2,1,0,3:T(8,128)} fusion(bf16[16,16,64,50]{2,3,1,0:T(8,128)(2,1)} %fusion.61, f32[16,50,1024]{2,1,0:T(8,128)} %get-tuple-element.131), kind=kOutput, calls=%fused_computation.73 | convolution fusion | flops 1678540800 | bytes 9109504 | tf_op jit(solution)/shard_map/bqhd,bqw->hdw/dot_general | solution.py:18
  325.0 6.5 convolution_convert_fusion
  331.6 12.6 %convolution_bitcast_fusion.1.refs_0_ = f32[1024,4096]{1,0:T(8,128)} fusion(bf16[16,50,4096]{2,1,0:T(8,128)(2,1)S(1)} %bitcast.193, f32[16,50,1024]{2,1,0:T(8,128)S(1)} %copy-done.6, f32[1024]{0:T(1024)S(1)} %get-tuple-element.112, f32[1024]{0:T(1024)S(1)} %get-tuple-element.110, f32[16,50]{1,0:T(8,128)S(1)} %add_rsqrt_fusion, ...), kind=kOutput, calls=%fused_computation.39 | convolution fusion | flops 6714982400 | bytes 26622208 | tf_op jit(solution)/shard_map/btw,btf->wf/dot_general | solution.py:18
  344.2 7.1 fusion.58
  351.4 4.1 fusion.66
  355.5 3.8 copy.178
  359.3 17.0 %fusion.55 = f32[16,16,64,50]{2,3,1,0:T(8,128)} fusion(f32[16,16,50,50]{2,3,1,0:T(8,128)} %fusion.58, bf16[16,50,3,16,64]{4,1,3,2,0:T(8,128)(2,1)} %add_convert_fusion, f32[16,16,50,50]{2,3,1,0:T(8,128)} %copy-done.8, f32[16,16,50]{2,1,0:T(8,128)S(1)} %get-tuple-element.134), kind=kOutput, calls=%fused_computation.92 | convolution fusion | flops 86412848 | bytes 36569088 | tf_op jit(solution)/shard_map/bhqk,bkhd->bqhd/dot_general | solution.py:18
  376.3 16.1 %fusion.52 = f32[16,16,64,50]{2,3,1,0:T(8,128)} fusion(f32[16,16,50,50]{2,3,1,0:T(8,128)} %fusion.58, bf16[16,50,3,16,64]{4,1,3,2,0:T(8,128)(2,1)} %add_convert_fusion, f32[16,16,50,50]{2,3,1,0:T(8,128)} %copy-done.8, f32[16,16,50]{2,1,0:T(8,128)S(1)} %get-tuple-element.134), kind=kOutput, calls=%fused_computation.91 | convolution fusion | flops 86412848 | bytes 36569088 | tf_op jit(solution)/shard_map/bhqk,bqhd->bkhd/dot_general | solution.py:18
  392.4 4.4 copy.179
  396.8 4.5 copy.180
  401.3 2.6 copy-done.2
  404.0 2.4 fusion.16
  406.5 8.7 %fusion.17 = bf16[16,50,3,16,64]{4,3,2,1,0:T(8,128)(2,1)} fusion(f32[16,50,1,16,64]{4,3,2,1,0:T(8,128)S(1)} %bitcast.183, f32[16,50,1,16,64]{4,3,2,1,0:T(8,128)S(1)} %bitcast.185, f32[16,50,1,16,64]{4,3,2,1,0:T(8,128)} %bitcast.187), kind=kLoop, calls=%fused_computation.33 | loop fusion | flops 4915200 | bytes 14745600 | tf_op jit(solution)/shard_map/convert_element_type | solution.py:91
  415.3 15.7 %fusion.42 = (f32[1024]{0:T(1024)S(1)}, f32[16,50]{1,0:T(8,128)S(1)}, f32[16,50]{1,0:T(8,128)S(1)}, f32[1024]{0:T(1024)S(1)}, f32[16,50,1024,1,1]{2,1,4,3,0:T(8,128)S(1)}) fusion(f32[16,50]{1,0:T(8,128)S(1)} %copy-done.33, f32[16,50]{1,0:T(8,128)S(1)} %copy-done.27, f32[1024]{0:T(1024)S(1)} %copy-done.31, f32[1024]{0:T(1024)S(1)} %copy-done.25, ...), kind=kOutput, calls=%fused_computation.70 | convolution fusion | flops 5044629504 | bytes 17799936 | tf_op jit(solution)/shard_map/btchd,wchd->btw/dot_general | solution.py:18
  431.0 4.1 multiply_reduce_fusion.3
  435.2 2.8 subtract_multiply_fusion
  438.0 17.4 %fusion.20 = f32[1024,3,16,64,1]{0,3,4,2,1:T(8,128)} fusion(bf16[16,50,3,16,64]{4,3,2,1,0:T(8,128)(2,1)} %fusion.17, f32[1024]{0:T(1024)S(1)} %copy-done.37, f32[1024]{0:T(1024)S(1)} %copy-done.35, f32[16,50]{1,0:T(8,128)S(1)} %copy-done.33, f32[16,50]{1,0:T(8,128)S(1)} %copy-done.27, f32[1024]{0:T(1024)S(1)} %copy-done.31, f32[1024]{0:T(1024)S(1)} %copy-done.25, ...), kind=kOutput, calls=%fused_computation.36 | convolution fusion | flops 5041356800 | bytes 20804096 | tf_op jit(solution)/shard_map/btw,btchd->wchd/dot_general | solution.py:18
  455.4 12.9 %copy.138.refs_2_ = f32[1024,3072]{1,0:T(8,128)} copy(f32[1024,3072]{0,1:T(8,128)} %bitcast.189) | data formatting | bytes 25165824 | tf_op jit(solution)/shard_map/reshape | solution.py:412
  469.4 2.5 slice_reduce_fusion
  480.4 3.3 convolution_bitcast_fusion.3
  483.7 5.1 convolution_bitcast_fusion.2
  489.2 8.0 %concatenate.15 = f32[1024,982]{1,0:T(8,128)} concatenate(f32[1024,768]{1,0:T(8,128)} %convolution_bitcast_fusion.2, f32[1024,197]{1,0:T(8,128)S(1)} %maximum_bitcast_fusion, f32[1024,1]{1,0:T(8,128)} %copy.128, f32[1024,1]{1,0:T(8,128)} %copy.129, f32[1024,1]{1,0:T(8,128)} %copy.130, f32[1024,1]{1,0:T(8,128)} %copy.131, f32[1024,1]{1,0:T(8,128)} %copy.132, f32[1024,1]{1,0:T(8,128)} %copy.133, ...), dimensions={1} | concatenate | bytes 8044544 | tf_op jit(solution)/shard_map/concatenate | solution.py:389
  497.1 4.9 pad.9.refs_4_
  502.0 15.8 %convolution_bitcast_fusion.refs_1_ = f32[4096,1024]{1,0:T(8,128)} fusion(bf16[16,50,4096]{2,1,0:T(8,128)(2,1)} %fusion.4, bf16[16,50,1024]{2,0,1:T(8,128)(2,1)S(1)} %copy-done.19), kind=kOutput, calls=%fused_computation.38 | convolution fusion | flops 6710886400 | bytes 24969216 | tf_op jit(solution)/shard_map/btf,btw->fw/dot_general | solution.py:18
  517.8 199.4 %reduce_all.1 = (f32[32,4096]{1,0:T(8,128)}, f32[128,1024]{1,0:T(8,128)}, f32[32,3072]{1,0:T(8,128)}, f32[32,1024]{1,0:T(8,128)}, f32[32,1024]{1,0:T(8,128)}) custom-call(f32[1024,4096]{1,0:T(8,128)} %convolution_bitcast_fusion.1.refs_0_, f32[4096,1024]{1,0:T(8,128)} %convolution_bitcast_fusion.refs_1_, f32[1024,3072]{1,0:T(8,128)} %copy.138.refs_2_, ...), custom_call_target="tpu_custom_call" | custom-call | tf_op jit(solution)/shard_map/reduce_all/pallas_call | solution.py:361
  717.2 2.3 slice_reduce_fusion.2
  725.2 2.1 reshape.227
  728.9 1.9 copy.185
  730.7 1.9 copy.186
  (175 shorter events, 46.4 us)
Async XLA Ops:
  0.7 18.8 %copy-start.28 = (s32[16,49]{1,0:T(8,128)S(1)}, s32[16,49]{1,0:T(8,128)}, u32[]{:S(2)}) copy-start(s32[16,49]{1,0:T(8,128)} %param.22) | copy-start | bytes 9412
  134.9 8.7 %copy-start.9 = (bf16[1024,1024]{1,0:T(8,128)(2,1)S(1)}, bf16[1024,1024]{1,0:T(8,128)(2,1)}, u32[]{:S(2)}) copy-start(bf16[1024,1024]{1,0:T(8,128)(2,1)} %get-tuple-element.29) | copy-start | bytes 6291460
  145.2 9.1 %copy-start.34 = (f32[1024]{0:T(1024)}, f32[1024]{0:T(1024)S(1)}, u32[]{:S(2)}) copy-start(f32[1024]{0:T(1024)S(1)} %get-tuple-element.115) | copy-start | bytes 12292
  145.2 9.1 %copy-start.36 = (f32[1024]{0:T(1024)}, f32[1024]{0:T(1024)S(1)}, u32[]{:S(2)}) copy-start(f32[1024]{0:T(1024)S(1)} %get-tuple-element.114) | copy-start | bytes 12292
  145.2 54.4 %copy-start.24 = (f32[1024]{0:T(1024)}, f32[1024]{0:T(1024)S(1)}, u32[]{:S(2)}) copy-start(f32[1024]{0:T(1024)S(1)} %get-tuple-element.117) | copy-start | bytes 12292
  145.2 54.4 %copy-start.30 = (f32[1024]{0:T(1024)}, f32[1024]{0:T(1024)S(1)}, u32[]{:S(2)}) copy-start(f32[1024]{0:T(1024)S(1)} %get-tuple-element.116) | copy-start | bytes 12292
  145.5 54.1 %copy-start.11 = (f32[16,1,1024]{2,1,0:T(1,128)}, f32[16,1,1024]{2,1,0:T(1,128)S(1)}, u32[]{:S(2)}) copy-start(f32[16,1,1024]{2,1,0:T(1,128)S(1)} %broadcast_in_dim.105) | copy-start | bytes 196612
  150.2 49.4 %copy-start = (f32[16,49,1024]{2,1,0:T(8,128)}, f32[16,49,1024]{2,1,0:T(8,128)S(1)}, u32[]{:S(2)}) copy-start(f32[16,49,1024]{2,1,0:T(8,128)S(1)} %add_add_fusion) | copy-start | bytes 9633796
  150.7 48.9 %copy-start.20 = (f32[16,50]{1,0:T(8,128)}, f32[16,50]{1,0:T(8,128)S(1)}, u32[]{:S(2)}) copy-start(f32[16,50]{1,0:T(8,128)S(1)} %broadcast_multiply_fusion.8) | copy-start | bytes 9604
  150.7 3.6 slice-start.6
  151.5 48.1 %copy-start.22 = (f32[16,50]{1,0:T(8,128)}, f32[16,50]{1,0:T(8,128)S(1)}, u32[]{:S(2)}) copy-start(f32[16,50]{1,0:T(8,128)S(1)} %add_rsqrt_fusion.2) | copy-start | bytes 9604
  151.6 2.8 slice-start.7
  152.8 20.3 %copy-start.26 = (f32[16,50]{1,0:T(8,128)}, f32[16,50]{1,0:T(8,128)S(1)}, u32[]{:S(2)}) copy-start(f32[16,50]{1,0:T(8,128)S(1)} %broadcast_multiply_fusion.7) | copy-start | bytes 9604
  154.4 18.7 %copy-start.32 = (f32[16,50]{1,0:T(8,128)}, f32[16,50]{1,0:T(8,128)S(1)}, u32[]{:S(2)}) copy-start(f32[16,50]{1,0:T(8,128)S(1)} %add_rsqrt_fusion.1) | copy-start | bytes 9604
  190.4 3.0 copy-start.8
  193.4 6.2 copy-start.38
  204.3 103.3 %copy-start.5 = (f32[16,50,1024]{2,1,0:T(8,128)}, f32[16,50,1024]{2,1,0:T(8,128)S(1)}, u32[]{:S(2)}) copy-start(f32[16,50,1024]{2,1,0:T(8,128)S(1)} %get-tuple-element.137) | copy-start | bytes 9830404
  225.2 36.0 %copy-start.7 = (f32[16,50,4096]{2,1,0:T(8,128)S(1)}, f32[16,50,4096]{2,1,0:T(8,128)}, u32[]{:S(2)}) copy-start(f32[16,50,4096]{2,1,0:T(8,128)} %get-tuple-element.138) | copy-start | bytes 39321604
  225.2 36.0 %copy-start.18 = (bf16[16,50,1024]{2,0,1:T(8,128)(2,1)S(1)}, bf16[16,50,1024]{2,0,1:T(8,128)(2,1)}, u32[]{:S(2)}) copy-start(bf16[16,50,1024]{2,0,1:T(8,128)(2,1)} %param.41) | copy-start | bytes 4915204
  316.1 15.4 %slice-start.4 = ((s8[7340032]{0:T(1024)(128)(4,1)}), s8[3145728]{0:T(1024)(128)(4,1)S(1)}, s32[]{:S(2)}) async-start(s8[7340032]{0:T(1024)(128)(4,1)} %bitcast.192), calls=%async_computation.4 | async-start | bytes 6291456
  325.0 6.5 copy-start.6
  325.0 6.5 slice-start.5
  325.0 26.4 %slice-start.2 = ((s8[7340032]{0:T(1024)(128)(4,1)}), s8[4194304]{0:T(1024)(128)(4,1)S(1)}, s32[]{:S(2)}) async-start(s8[7340032]{0:T(1024)(128)(4,1)} %bitcast.190), calls=%async_computation.2 | async-start | bytes 8388608
  331.5 12.7 %copy-start.10 = (bf16[16,50,16,64]{3,1,2,0:T(8,128)(2,1)}, bf16[16,50,16,64]{3,1,2,0:T(8,128)(2,1)S(1)}, u32[]{:S(2)}) copy-start(bf16[16,50,16,64]{3,1,2,0:T(8,128)(2,1)S(1)} %convolution_convert_fusion) | copy-start | bytes 4915204
  331.6 19.8 %slice-start.3 = ((s8[7340032]{0:T(1024)(128)(4,1)}), s8[3145728]{0:T(1024)(128)(4,1)S(1)}, s32[]{:S(2)}) async-start(s8[7340032]{0:T(1024)(128)(4,1)} %bitcast.190), calls=%async_computation.3 | async-start | bytes 6291456
  392.4 11.6 %slice-start = ((s8[6553600]{0:T(1024)(128)(4,1)}), s8[4194304]{0:T(1024)(128)(4,1)S(1)}, s32[]{:S(2)}) async-start(s8[6553600]{0:T(1024)(128)(4,1)} %bitcast.180), calls=%async_computation | async-start | bytes 8388608
  396.8 7.2 slice-start.1
  401.3 2.7 copy-start.2
  406.4 8.8 %copy-start.1 = (f32[16,49,1024]{2,1,0:T(8,128)S(1)}, f32[16,49,1024]{2,1,0:T(8,128)}, u32[]{:S(2)}) copy-start(f32[16,49,1024]{2,1,0:T(8,128)} %copy-done) | copy-start | bytes 9633796
  406.4 8.8 %copy-start.12 = (f32[16,1,1024]{2,1,0:T(1,128)S(1)}, f32[16,1,1024]{2,1,0:T(1,128)}, u32[]{:S(2)}) copy-start(f32[16,1,1024]{2,1,0:T(1,128)} %copy-done.11) | copy-start | bytes 196612
  406.4 8.8 %copy-start.21 = (f32[16,50]{1,0:T(8,128)S(1)}, f32[16,50]{1,0:T(8,128)}, u32[]{:S(2)}) copy-start(f32[16,50]{1,0:T(8,128)} %copy-done.20) | copy-start | bytes 9604
  406.4 8.8 %copy-start.23 = (f32[16,50]{1,0:T(8,128)S(1)}, f32[16,50]{1,0:T(8,128)}, u32[]{:S(2)}) copy-start(f32[16,50]{1,0:T(8,128)} %copy-done.22) | copy-start | bytes 9604
  406.5 8.8 %copy-start.25 = (f32[1024]{0:T(1024)S(1)}, f32[1024]{0:T(1024)}, u32[]{:S(2)}) copy-start(f32[1024]{0:T(1024)} %copy-done.24) | copy-start | bytes 12292
  406.5 8.8 %copy-start.27 = (f32[16,50]{1,0:T(8,128)S(1)}, f32[16,50]{1,0:T(8,128)}, u32[]{:S(2)}) copy-start(f32[16,50]{1,0:T(8,128)} %copy-done.26) | copy-start | bytes 9604
  406.5 8.8 %copy-start.31 = (f32[1024]{0:T(1024)S(1)}, f32[1024]{0:T(1024)}, u32[]{:S(2)}) copy-start(f32[1024]{0:T(1024)} %copy-done.30) | copy-start | bytes 12292
  406.5 8.8 %copy-start.33 = (f32[16,50]{1,0:T(8,128)S(1)}, f32[16,50]{1,0:T(8,128)}, u32[]{:S(2)}) copy-start(f32[16,50]{1,0:T(8,128)} %copy-done.32) | copy-start | bytes 9604
  406.5 8.8 %copy-start.35 = (f32[1024]{0:T(1024)S(1)}, f32[1024]{0:T(1024)}, u32[]{:S(2)}) copy-start(f32[1024]{0:T(1024)} %copy-done.34) | copy-start | bytes 12292
  415.3 15.7 %copy-start.4 = (f32[16,50,1024]{2,1,0:T(8,128)S(1)}, f32[16,50,1024]{2,1,0:T(8,128)}, u32[]{:S(2)}) copy-start(f32[16,50,1024]{2,1,0:T(8,128)} %get-tuple-element.131) | copy-start | bytes 9830404
  435.1 2.8 copy-start.37
  469.4 11.0 %copy-start.29 = (s32[16,49]{1,0:T(8,128)S(1)}, s32[16,49]{1,0:T(8,128)}, u32[]{:S(2)}) copy-start(s32[16,49]{1,0:T(8,128)} %param.22) | copy-start | bytes 9412
  480.4 3.3 copy-start.3
  483.7 5.1 copy-start.17
  483.7 5.4 copy-start.13
  483.7 5.4 copy-start.14
  483.7 5.4 copy-start.15
  483.7 5.4 copy-start.16
  497.1 4.9 copy-start.19

commit v2 on v1

--- a/solution.py
+++ b/solution.py
@@ -10,95 +10,7 @@
 INV_SQRT2 = 0.7071067811865476
 INV_SQRT_2PI = 0.3989422804014327
 PARAM_NAMES = ('w_patch', 'b_patch', 'pos_table', 'cls_tok', 'lnp_g', 'lnp_b', 'ln1_g', 'ln1_b', 'w_qkv', 'b_qkv', 'w_out', 'b_out', 'ln2_g', 'ln2_b', 'w_fc', 'b_fc', 'w_proj', 'b_proj')
-VECTOR_NAMES = ('b_patch', 'cls_tok', 'lnp_g', 'lnp_b', 'ln1_g', 'ln1_b', 'b_qkv', 'b_out', 'ln2_g', 'ln2_b', 'b_fc', 'b_proj')
 LAST_SPLIT = ('w_patch', 'pos_table')
-
-
-def product(einsum_form, left_op, right_op):
-    return jnp.einsum(einsum_form, left_op, right_op, preferred_element_type=jnp.float32)
-
-
-def norm_forward(x_in, gain_f, shift_f):
-    centered = x_in - jnp.mean(x_in, axis=-1, keepdims=True)
-    inv_std = lax.rsqrt(jnp.mean(centered * centered, axis=-1, keepdims=True) + LN_EPS)
-    x_hat = centered * inv_std
-    return x_hat * gain_f + shift_f, x_hat, inv_std
-
-
-def norm_backward(d_norm, x_hat, inv_std, gain_f):
-    d_hat = d_norm * gain_f
-    d_in = inv_std * (d_hat - jnp.mean(d_hat, axis=-1, keepdims=True) - x_hat * jnp.mean(d_hat * x_hat, axis=-1, keepdims=True))
-    return d_in, jnp.sum(d_norm * x_hat, axis=(0, 1)), jnp.sum(d_norm, axis=(0, 1))
-
-
-def gelu_slope(pre_act):
-    return 0.5 * (1.0 + lax.erf(pre_act * INV_SQRT2)) + pre_act * jnp.exp(-0.5 * pre_act * pre_act) * INV_SQRT_2PI
-
-
-def forward(full_w, patches, keep):
-    n_img, n_patch = patches.shape[0], patches.shape[1]
-    d_model = full_w['w_out'].shape[0]
-    n_heads, head_dim = full_w['w_qkv'].shape[2], full_w['w_qkv'].shape[3]
-    logit_scale = head_dim ** -0.5
-    as_f32 = {name: full_w[name].astype(jnp.float32) for name in VECTOR_NAMES}
-    onehot_keep = (keep[:, :, None] == lax.broadcasted_iota(jnp.int32, (1, 1, n_patch), 2)).astype(jnp.bfloat16)
-    kept_rows = product('bkp,bpq->bkq', onehot_keep, patches).astype(jnp.bfloat16)
-    embed_rows = (product('bkq,qw->bkw', kept_rows, full_w['w_patch']) + as_f32['b_patch']
-                  + product('bkp,pw->bkw', onehot_keep, full_w['pos_table'][1:]))
-    head_row = as_f32['cls_tok'] + full_w['pos_table'][0].astype(jnp.float32)
-    x_zero = jnp.concatenate([jnp.broadcast_to(head_row, (n_img, 1, d_model)), embed_rows], axis=1)
-    h_zero, hat_p, inv_p = norm_forward(x_zero, as_f32['lnp_g'], as_f32['lnp_b'])
-    y_one, hat_1, inv_1 = norm_forward(h_zero, as_f32['ln1_g'], as_f32['ln1_b'])
-    a_in = y_one.astype(jnp.bfloat16)
-    qkv_all = (product('btw,wchd->btchd', a_in, full_w['w_qkv']) + as_f32['b_qkv'].reshape(3, n_heads, head_dim)).astype(jnp.bfloat16)
-    q_heads, k_heads, v_heads = qkv_all[:, :, 0], qkv_all[:, :, 1], qkv_all[:, :, 2]
-    attn_prob = jax.nn.softmax(product('bqhd,bkhd->bhqk', q_heads, k_heads) * logit_scale, axis=-1)
-    prob_b = attn_prob.astype(jnp.bfloat16)
-    context = product('bhqk,bkhd->bqhd', prob_b, v_heads).astype(jnp.bfloat16)
-    h_mid = h_zero + product('bqhd,hdw->bqw', context, full_w['w_out'].reshape(n_heads, head_dim, d_model)) + as_f32['b_out']
-    y_two, hat_2, inv_2 = norm_forward(h_mid, as_f32['ln2_g'], as_f32['ln2_b'])
-    c_in = y_two.astype(jnp.bfloat16)
-    pre_act = product('btw,wf->btf', c_in, full_w['w_fc']) + as_f32['b_fc']
-    gelu_out = jax.nn.gelu(pre_act, approximate=False).astype(jnp.bfloat16)
-    h_one = (h_mid + product('btf,fw->btw', gelu_out, full_w['w_proj']) + as_f32['b_proj']).astype(jnp.bfloat16)
-    saved = dict(onehot_keep=onehot_keep, kept_rows=kept_rows, hat_p=hat_p, inv_p=inv_p, hat_1=hat_1, inv_1=inv_1, a_in=a_in, q_heads=q_heads, k_heads=k_heads, v_heads=v_heads, attn_prob=attn_prob, prob_b=prob_b, context=context, hat_2=hat_2, inv_2=inv_2, c_in=c_in, pre_act=pre_act, gelu_out=gelu_out)
-    return h_one, saved
-
-
-def backward(weights, saved, grad_h1):
-    d_model = weights['w_out'].shape[0]
-    n_heads, head_dim = weights['w_qkv'].shape[2], weights['w_qkv'].shape[3]
-    logit_scale = head_dim ** -0.5
-    w_out3 = weights['w_out'].reshape(n_heads, head_dim, d_model)
-    d_h = grad_h1.astype(jnp.float32)
-    g_w_proj = product('btf,btw->fw', saved['gelu_out'], grad_h1)
-    d_pre = product('btw,fw->btf', grad_h1, weights['w_proj']) * gelu_slope(saved['pre_act'])
-    d_pre_b = d_pre.astype(jnp.bfloat16)
-    g_w_fc = product('btw,btf->wf', saved['c_in'], d_pre_b)
-    d_c = product('btf,wf->btw', d_pre_b, weights['w_fc'])
-    d_norm2, g_ln2_g, g_ln2_b = norm_backward(d_c, saved['hat_2'], saved['inv_2'], weights['ln2_g'].astype(jnp.float32))
-    d_mid = d_norm2 + d_h
-    d_mid_b = d_mid.astype(jnp.bfloat16)
-    g_w_out = product('bqhd,bqw->hdw', saved['context'], d_mid_b).reshape(d_model, d_model)
-    d_ctx = product('bqw,hdw->bqhd', d_mid_b, w_out3).astype(jnp.bfloat16)
-    g_v = product('bhqk,bqhd->bkhd', saved['prob_b'], d_ctx)
-    d_prob = product('bqhd,bkhd->bhqk', d_ctx, saved['v_heads'])
-    attn_prob = saved['attn_prob']
-    d_logit = (attn_prob * (d_prob - jnp.sum(attn_prob * d_prob, axis=-1, keepdims=True)) * logit_scale).astype(jnp.bfloat16)
-    g_q = product('bhqk,bkhd->bqhd', d_logit, saved['k_heads'])
-    g_k = product('bhqk,bqhd->bkhd', d_logit, saved['q_heads'])
-    d_qkv = jnp.stack([g_q, g_k, g_v], axis=2)
-    d_qkv_b = d_qkv.astype(jnp.bfloat16)
-    g_w_qkv = product('btw,btchd->wchd', saved['a_in'], d_qkv_b)
-    d_a = product('btchd,wchd->btw', d_qkv_b, weights['w_qkv'])
-    d_norm1, g_ln1_g, g_ln1_b = norm_backward(d_a, saved['hat_1'], saved['inv_1'], weights['ln1_g'].astype(jnp.float32))
-    d_zero = d_norm1 + d_mid
-    d_x, g_lnp_g, g_lnp_b = norm_backward(d_zero, saved['hat_p'], saved['inv_p'], weights['lnp_g'].astype(jnp.float32))
-    d_head = jnp.sum(d_x[:, 0], axis=0)
-    d_emb = d_x[:, 1:]
-    d_emb_b = d_emb.astype(jnp.bfloat16)
-    g_pos = jnp.concatenate([d_head[None], product('bkp,bkw->pw', saved['onehot_keep'], d_emb_b)], axis=0)
-    return dict(w_patch=product('bkq,bkw->qw', saved['kept_rows'], d_emb_b), b_patch=jnp.sum(d_emb, axis=(0, 1)), pos_table=g_pos, cls_tok=d_head, lnp_g=g_lnp_g, lnp_b=g_lnp_b, ln1_g=g_ln1_g, ln1_b=g_ln1_b, w_qkv=g_w_qkv, b_qkv=jnp.sum(d_qkv, axis=(0, 1)).reshape(-1), w_out=g_w_out, b_out=jnp.sum(d_mid, axis=(0, 1)), ln2_g=g_ln2_g, ln2_b=g_ln2_b, w_fc=g_w_fc, b_fc=jnp.sum(d_pre, axis=(0, 1)), w_proj=g_w_proj, b_proj=jnp.sum(d_h, axis=(0, 1)))
 
 
 RINGS = (
@@ -372,28 +284,232 @@
         name='reduce_all',
     )(*grads)
 
-
-ROW_VECTORS = ('b_patch', 'cls_tok', 'lnp_g', 'lnp_b', 'ln1_g', 'ln1_b', 'b_out', 'ln2_g', 'ln2_b', 'b_proj')
+HEAD_GROUP, HEAD_DIM, SEQ, N_TOKEN = 256, 64, 64, 50
+ROWS = 256
+LOGIT_SCALE = HEAD_DIM ** -0.5
+VEC_NAMES = ('b_patch', 'cls_tok', 'lnp_g', 'lnp_b', 'ln1_g', 'ln1_b', 'b_out', 'ln2_g', 'ln2_b', 'b_proj')
+VEC_AT = {name: place for place, name in enumerate(VEC_NAMES)}
+VEC_QKV, VEC_FC, VEC_ROWS = 10, 13, 24
+
+
+def dot_nn(left, right):
+    return lax.dot_general(left, right, (((1,), (0,)), ((), ())), preferred_element_type=jnp.float32)
+
+
+def dot_nt(left, right):
+    return lax.dot_general(left, right, (((1,), (1,)), ((), ())), preferred_element_type=jnp.float32)
+
+
+def dot_tn(left, right):
+    return lax.dot_general(left, right, (((0,), (0,)), ((), ())), preferred_element_type=jnp.float32)
+
+
+def normalize(x_in):
+    centered = x_in - jnp.mean(x_in, axis=-1, keepdims=True)
+    inv_std = lax.rsqrt(jnp.mean(centered * centered, axis=-1, keepdims=True) + LN_EPS)
+    return centered * inv_std, inv_std
+
+
+def normalize_back(d_norm, x_hat, inv_std, gain):
+    d_hat = d_norm * gain
+    return inv_std * (d_hat - jnp.mean(d_hat, axis=-1, keepdims=True) - x_hat * jnp.mean(d_hat * x_hat, axis=-1, keepdims=True))
+
+
+def lane_ids(shape):
+    return lax.broadcasted_iota(jnp.int32, shape, 1)
+
+
+def stack_heads(block):
+    head = lane_ids((1, HEAD_GROUP)) // HEAD_DIM
+    return jnp.concatenate([block * (head == h).astype(jnp.bfloat16) for h in range(4)], axis=0)
+
+
+def unstack_heads(stacked):
+    head = lane_ids((1, HEAD_GROUP)) // HEAD_DIM
+    total = jnp.where(head == 0, stacked[:SEQ], 0.0)
+    for h in range(1, 4):
+        total = jnp.where(head == h, stacked[h * SEQ:(h + 1) * SEQ], total)
+    return total
+
+
+def per_head(block, reducer, neutral):
+    halves = []
+    for j in range(2):
+        half = block[:, 128 * j:128 * (j + 1)]
+        low = lane_ids(half.shape) < HEAD_DIM
+        first = reducer(jnp.where(low, half, neutral), axis=1, keepdims=True)
+        second = reducer(jnp.where(low, neutral, half), axis=1, keepdims=True)
+        halves.append(jnp.where(low, first, second))
+    return jnp.concatenate(halves, axis=1)
+
+
+def probabilities(q_block, k_stack):
+    logits = dot_nt(q_block, k_stack) * LOGIT_SCALE
+    logits = jnp.where(lane_ids(logits.shape) % HEAD_DIM < N_TOKEN, logits, -jnp.inf)
+    powers = jnp.exp(logits - per_head(logits, jnp.max, -jnp.inf))
+    return powers / per_head(powers, jnp.sum, 0.0)
+
+
+def row_of(vecs, name):
+    place = VEC_AT[name]
+    return vecs[place:place + 1, :]
+
+
+def is_cls():
+    return lax.broadcasted_iota(jnp.int32, (ROWS, 1), 0) % SEQ == 0
+
+
+def stage_one(x_in, misc, w_qkv, w_out, vecs, x_zero, a_out, qkv, ctx, h_mid, c_out):
+    start = jnp.where(is_cls(), row_of(vecs, 'cls_tok'), row_of(vecs, 'b_patch'))
+    x_sum = dot_nt(x_in[...], misc[...]) + start
+    x_zero[...] = x_sum
+    h_zero = normalize(x_sum)[0] * row_of(vecs, 'lnp_g') + row_of(vecs, 'lnp_b')
+    a_in = (normalize(h_zero)[0] * row_of(vecs, 'ln1_g') + row_of(vecs, 'ln1_b')).astype(jnp.bfloat16)
+    a_out[...] = a_in
+    for s in range(3):
+        cols = pl.ds(1024 * s, 1024)
+        qkv[:, cols] = (dot_nn(a_in, w_qkv[:, cols]) + vecs[VEC_QKV + s:VEC_QKV + s + 1, :]).astype(jnp.bfloat16)
+
+    def image(b, carry):
+        rows = pl.ds(pl.multiple_of(b * SEQ, SEQ), SEQ)
+        for g in range(4):
+            q_block, k_block, v_block = [qkv[rows, pl.ds(1024 * s + HEAD_GROUP * g, HEAD_GROUP)] for s in range(3)]
+            prob = probabilities(q_block, stack_heads(k_block)).astype(jnp.bfloat16)
+            ctx[rows, pl.ds(HEAD_GROUP * g, HEAD_GROUP)] = dot_nn(prob, stack_heads(v_block)).astype(jnp.bfloat16)
+        return carry
+
+    lax.fori_loop(0, ROWS // SEQ, image, 0)
+    mid = h_zero + dot_nn(ctx[...], w_out[...]) + row_of(vecs, 'b_out')
+    h_mid[...] = mid
+    c_out[...] = (normalize(mid)[0] * row_of(vecs, 'ln2_g') + row_of(vecs, 'ln2_b')).astype(jnp.bfloat16)
+
+
+def add_row(sums, place, value):
+    sums[place:place + 1, :] += jnp.sum(value, axis=0, keepdims=True)
+
+
+def clear_first(sums):
+    @pl.when(pl.program_id(0) == 0)
+    def _():
+        sums[...] = jnp.zeros_like(sums)
+
+
+def stage_two(c_in, h_mid, grad_h1, w_fc, w_proj, vecs, gelu_out, d_pre_out, h_one, d_mid, d_mid_b, sums, h_acc, d_c_acc):
+    clear_first(sums)
+    c_block, g_block = c_in[...], grad_h1[...]
+    tile = 1024
+    for f in range(4096 // tile):
+        cols = pl.ds(tile * f, tile)
+        pre_act = dot_nn(c_block, w_fc[:, cols]) + vecs[VEC_FC + f:VEC_FC + f + 1, :]
+        normal_cdf = 0.5 * (1.0 + lax.erf(pre_act * INV_SQRT2))
+        gelu = (pre_act * normal_cdf).astype(jnp.bfloat16)
+        gelu_out[:, cols] = gelu
+        slope = normal_cdf + pre_act * jnp.exp(-0.5 * pre_act * pre_act) * INV_SQRT_2PI
+        d_pre = dot_nt(g_block, w_proj[cols, :]) * slope
+        add_row(sums, VEC_FC + f, d_pre)
+        d_pre_b = d_pre.astype(jnp.bfloat16)
+        d_pre_out[:, cols] = d_pre_b
+        h_part = dot_nn(gelu, w_proj[cols, :])
+        d_part = dot_nt(d_pre_b, w_fc[:, cols])
+        if f == 0:
+            h_acc[...] = h_part
+            d_c_acc[...] = d_part
+        else:
+            h_acc[...] += h_part
+            d_c_acc[...] += d_part
+    mid = h_mid[...]
+    h_one[...] = (mid + h_acc[...] + row_of(vecs, 'b_proj')).astype(jnp.bfloat16)
+    d_c = d_c_acc[...]
+    x_hat, inv_std = normalize(mid)
+    d_h = g_block.astype(jnp.float32)
+    d_sum = normalize_back(d_c, x_hat, inv_std, row_of(vecs, 'ln2_g')) + d_h
+    d_mid[...] = d_sum
+    d_mid_b[...] = d_sum.astype(jnp.bfloat16)
+    add_row(sums, VEC_AT['ln2_g'], d_c * x_hat)
+    add_row(sums, VEC_AT['ln2_b'], d_c)
+    add_row(sums, VEC_AT['b_proj'], d_h)
+    add_row(sums, VEC_AT['b_out'], d_sum)
+
+
+def stage_three(x_zero, d_mid, d_mid_b, qkv, w_qkv, w_out, vecs, d_qkv_out, d_emb_out, sums, d_ctx, d_part):
+    clear_first(sums)
+    d_ctx[...] = dot_nt(d_mid_b[...], w_out[...]).astype(jnp.bfloat16)
+    d_part[...] = jnp.zeros_like(d_part)
+
+    def image(b, carry):
+        rows = pl.ds(pl.multiple_of(b * SEQ, SEQ), SEQ)
+        for g in range(4):
+            places = [pl.ds(1024 * s + HEAD_GROUP * g, HEAD_GROUP) for s in range(3)]
+            q_block, k_block, v_block = [qkv[rows, place] for place in places]
+            d_block = d_ctx[rows, pl.ds(HEAD_GROUP * g, HEAD_GROUP)]
+            k_stack = stack_heads(k_block)
+            prob = probabilities(q_block, k_stack)
+            d_prob = dot_nt(d_block, stack_heads(v_block))
+            d_logit = (prob * (d_prob - per_head(prob * d_prob, jnp.sum, 0.0)) * LOGIT_SCALE).astype(jnp.bfloat16)
+            g_q = dot_nn(d_logit, k_stack)
+            g_k = unstack_heads(dot_tn(d_logit, q_block))
+            g_v = unstack_heads(dot_tn(prob.astype(jnp.bfloat16), d_block))
+            for place, grad in zip(places, (g_q, g_k, g_v)):
+                d_qkv_out[rows, place] = grad.astype(jnp.bfloat16)
+                d_part[:, place] += jnp.sum(grad.reshape(SEQ // 8, 8, HEAD_GROUP), axis=0)
+        return carry
+
+    lax.fori_loop(0, ROWS // SEQ, image, 0)
+    for s in range(3):
+        add_row(sums, VEC_QKV + s, d_part[:, pl.ds(1024 * s, 1024)])
+    d_a = dot_nt(d_qkv_out[...], w_qkv[...])
+    hat_p, inv_p = normalize(x_zero[...])
+    h_zero = hat_p * row_of(vecs, 'lnp_g') + row_of(vecs, 'lnp_b')
+    hat_1, inv_1 = normalize(h_zero)
+    add_row(sums, VEC_AT['ln1_g'], d_a * hat_1)
+    add_row(sums, VEC_AT['ln1_b'], d_a)
+    d_zero = normalize_back(d_a, hat_1, inv_1, row_of(vecs, 'ln1_g')) + d_mid[...]
+    add_row(sums, VEC_AT['lnp_g'], d_zero * hat_p)
+    add_row(sums, VEC_AT['lnp_b'], d_zero)
+    d_x = normalize_back(d_zero, hat_p, inv_p, row_of(vecs, 'lnp_g'))
+    d_emb = jnp.where(is_cls(), 0.0, d_x)
+    add_row(sums, VEC_AT['cls_tok'], jnp.where(is_cls(), d_x, 0.0))
+    add_row(sums, VEC_AT['b_patch'], d_emb)
+    d_emb_out[...] = d_emb.astype(jnp.bfloat16)
+
+
+def whole(shape):
+    return pl.BlockSpec(shape, lambda i: (0, 0), pipeline_mode=pl.Buffered(1))
+
+
+def rows_of(width):
+    return pl.BlockSpec((ROWS, width), lambda i: (i, 0))
+
+
+def stage_call(body, name, n_rows, ins, outs, scratch=()):
+    in_specs = [rows_of(a.shape[1]) if a.shape[0] == n_rows and not held else whole(a.shape) for a, held in ins]
+    out_specs = [pl.BlockSpec((VEC_ROWS, 1024), lambda i: (0, 0)) if dtype is None else rows_of(width) for width, dtype in outs]
+    out_shape = [jax.ShapeDtypeStruct((VEC_ROWS, 1024), jnp.float32) if dtype is None else jax.ShapeDtypeStruct((n_rows, width), dtype) for width, dtype in outs]
+    return pl.pallas_call(body, grid=(n_rows // ROWS,), in_specs=in_specs, out_specs=out_specs, out_shape=out_shape, scratch_shapes=list(scratch),
+                          compiler_params=pltpu.CompilerParams(vmem_limit_bytes=62 * 1024 * 1024, dimension_semantics=('arbitrary',)), name=name)(*[a for a, _ in ins])
+
 N_PIXEL, N_POS = 768, 197
-MISC_USED = N_PIXEL + N_POS + len(ROW_VECTORS) + 3 + 4
+MISC_USED = N_PIXEL + N_POS + len(VEC_NAMES) + 3 + 4
 
 
 def solution(mesh):
     def spec_of(name):
         return P(None, MESH_AXIS) if name in LAST_SPLIT else P(MESH_AXIS)
 
+    def vector_columns(part, rows):
+        columns = [part[name].reshape(rows, 1) for name in VEC_NAMES] + [part['b_qkv'].reshape(rows, 3), part['b_fc'].reshape(rows, 4)]
+        return jnp.pad(jnp.concatenate(columns, axis=1), ((0, 0), (0, 1024 - MISC_USED)))
+
     def pack_misc(part):
         rows = part['w_patch'].shape[1]
-        columns = [part['w_patch'].T, part['pos_table'].T] + [part[name][:, None] for name in ROW_VECTORS]
-        columns += [part['b_qkv'].reshape(rows, 3), part['b_fc'].reshape(rows, 4)]
-        return jnp.pad(jnp.concatenate(columns, axis=1), ((0, 0), (0, 1024 - MISC_USED)))
+        return jnp.concatenate([part['w_patch'].T, part['pos_table'].T, vector_columns(part, rows)], axis=1)
 
     def unpack_misc(misc):
         part = {'w_patch': misc[:, :N_PIXEL].T, 'pos_table': misc[:, N_PIXEL:N_PIXEL + N_POS].T}
         first = N_PIXEL + N_POS
-        for name in ROW_VECTORS:
-            part[name] = misc[:, first]
-            first += 1
+        for place, name in enumerate(VEC_NAMES):
+            part[name] = misc[:, first + place]
+        first += len(VEC_NAMES)
         part['b_qkv'] = misc[:, first:first + 3].reshape(-1)
         part['b_fc'] = misc[:, first + 3:first + 7].reshape(-1)
         return part
@@ -401,17 +517,47 @@
     def local_step(patches, keep, *rest):
         shards = dict(zip(PARAM_NAMES, rest[:-1]))
         grad_h1 = rest[-1]
-        n_rows, _, n_heads, head_dim = shards['w_qkv'].shape
+        n_img, n_patch, _ = patches.shape
+        n_token, d_model = grad_h1.shape[1:]
+        n_shard, _, n_heads, head_dim = shards['w_qkv'].shape
+        n_rows = n_img * SEQ
         casts = {name: shards[name].astype(jnp.bfloat16) for name in PARAM_NAMES}
-        w_fc, w_proj, w_qkv, w_out, misc = gather_all((casts['w_fc'], casts['w_proj'], casts['w_qkv'].reshape(n_rows, -1), casts['w_out'], pack_misc(casts)))
-        full_w = unpack_misc(misc)
-        full_w.update(w_fc=w_fc, w_proj=w_proj, w_qkv=w_qkv.reshape(-1, 3, n_heads, head_dim), w_out=w_out)
-        h_one, saved = forward(full_w, patches, keep)
-        grad_map = backward(full_w, saved, grad_h1)
-        d_model = w_out.shape[0]
-        sums = reduce_all((grad_map['w_fc'], grad_map['w_proj'], grad_map['w_qkv'].reshape(d_model, -1), grad_map['w_out'], pack_misc(grad_map)))
-        own = unpack_misc(sums[MISC])
-        own.update(w_fc=sums[FC], w_proj=sums[PROJ], w_qkv=sums[QKV].reshape(n_rows, 3, n_heads, head_dim), w_out=sums[OUT])
+        w_fc, w_proj, w_qkv, w_out, misc = gather_all((casts['w_fc'], casts['w_proj'], casts['w_qkv'].reshape(n_shard, -1), casts['w_out'], pack_misc(casts)))
+        position = jnp.pad(keep + 1, ((0, 0), (1, 0)))
+        position = jnp.pad(position, ((0, 0), (0, SEQ - n_token)), constant_values=-1)[:, :, None]
+        onehot_patch = (position == 1 + lax.broadcasted_iota(jnp.int32, (1, 1, n_patch), 2)).astype(jnp.bfloat16)
+        onehot_pos = (position == lax.broadcasted_iota(jnp.int32, (1, 1, 1024 - N_PIXEL), 2)).astype(jnp.bfloat16)
+        kept_rows = jnp.einsum('bkp,bpq->bkq', onehot_patch, patches, preferred_element_type=jnp.float32).astype(jnp.bfloat16)
+        x_in = jnp.concatenate([kept_rows, onehot_pos], axis=2).reshape(n_rows, 1024)
+        grad_rows = jnp.pad(grad_h1, ((0, 0), (0, SEQ - n_token), (0, 0))).reshape(n_rows, d_model)
+
+        vec_part = misc[:, N_PIXEL + N_POS:MISC_USED].astype(jnp.float32)
+        n_vec = len(VEC_NAMES)
+        vecs = jnp.concatenate([vec_part[:, :n_vec].T, vec_part[:, n_vec:n_vec + 3].reshape(3, 1024), vec_part[:, n_vec + 3:].reshape(4, 1024)], axis=0)
+        vecs = jnp.pad(vecs, ((0, VEC_ROWS - vecs.shape[0]), (0, 0)))
+
+        bf, f32 = jnp.bfloat16, jnp.float32
+        x_zero, a_in, qkv, ctx, h_mid, c_in = stage_call(
+            stage_one, 'stage_one', n_rows, [(x_in, False), (misc, True), (w_qkv, True), (w_out, True), (vecs, True)],
+            [(1024, f32), (1024, bf), (3072, bf), (1024, bf), (1024, f32), (1024, bf)])
+        gelu, d_pre, h_one, d_mid, d_mid_b, sums_two = stage_call(
+            stage_two, 'stage_two', n_rows, [(c_in, False), (h_mid, False), (grad_rows, False), (w_fc, True), (w_proj, True), (vecs, True)],
+            [(4096, bf), (4096, bf), (1024, bf), (1024, f32), (1024, bf), (0, None)],
+            [pltpu.VMEM((ROWS, 1024), f32), pltpu.VMEM((ROWS, 1024), f32)])
+        d_qkv, d_emb, sums_three = stage_call(
+            stage_three, 'stage_three', n_rows, [(x_zero, False), (d_mid, False), (d_mid_b, False), (qkv, False), (w_qkv, True), (w_out, True), (vecs, True)],
+            [(3072, bf), (1024, bf), (0, None)],
+            [pltpu.VMEM((ROWS, 1024), bf), pltpu.VMEM((8, 3072), f32)])
+        h_one = h_one.reshape(n_img, SEQ, d_model)[:, :n_token]
+        outer = lambda left, right: lax.dot_general(left, right, (((0,), (0,)), ((), ())), preferred_element_type=f32)
+        sums = sums_two + sums_three
+        totals = {name: sums[place] for name, place in VEC_AT.items()}
+        totals.update(b_qkv=sums[VEC_QKV:VEC_QKV + 3], b_fc=sums[VEC_FC:VEC_FC + 4])
+        g_vec = jnp.concatenate([totals['cls_tok'].reshape(1024, 1), jnp.zeros((1024, N_POS - 1), f32), vector_columns(totals, 1024)], axis=1)
+        g_misc = outer(d_emb, x_in) + jnp.pad(g_vec, ((0, 0), (N_PIXEL, 0)))
+        reduced = reduce_all((outer(c_in, d_pre), outer(gelu, grad_rows), outer(a_in, d_qkv), outer(ctx, d_mid_b), g_misc))
+        own = unpack_misc(reduced[MISC])
+        own.update(w_fc=reduced[FC], w_proj=reduced[PROJ], w_qkv=reduced[QKV].reshape(n_shard, 3, n_heads, head_dim), w_out=reduced[OUT])
         return (h_one,) + tuple(own[name] for name in PARAM_NAMES)
 
     batch_spec = P(MESH_AXIS)

time: 738 us -> 570 us (0.77)
  matrix products: 238 us -> 48.9 us
  Pallas kernels: 308 us -> 464 us
  other arithmetic: 96.3 us -> 9.04 us
  local copies, waits for them, and re-layouts: 88.2 us -> 36.4 us
    dot_general x23 -> x6, matrix products: 238 us -> 48.9 us  [the longest x5 43.5 us: local_step(): lax.dot_general(left, right, (((0,), (0,)), ((), ())), preferred_element_...]
    pallas_call x0 -> x3, Pallas kernels: none -> 156 us  [stage_call(): pl.pallas_call(body, grid=(n_rows // ROWS,), in_specs=in_specs, out_specs...]
    convert_element_type x6 -> x2, other arithmetic: 46.7 us -> 0.22 us  [the longest x1 0.21 us: local_step(): (position == lax.broadcasted_iota(jnp.int32, (1, 1, 1024 - N_PIXEL), 2))....]
    reduce_sum x10 -> x0, other arithmetic: 18.7 us -> none  [the longest x1 4.1 us: backward(): jnp.sum(d_mid, axis=(0, 1))]
    dot_general x3 -> x0, local copies, waits for them, and re-layouts: 12.7 us -> none  [product(): jnp.einsum(einsum_form, left_op, right_op, preferred_element_type=jnp.flo...]
    broadcast_in_dim x22 -> x1, local copies, waits for them, and re-layouts: 12.5 us -> 0.01 us  [local_step(): jnp.zeros((1024, N_POS - 1), f32)]
    sub x1 -> x0, other arithmetic: 11.9 us -> none  [forward(): jax.nn.softmax(product('bqhd,bkhd->bhqk', q_heads, k_heads) * logit_scale...]
    reshape x6 -> x18, local copies, waits for them, and re-layouts: 17.5 us -> 7.45 us  [the longest x1 2.09 us: local_step(): reduced[QKV].reshape(n_shard, 3, n_heads, head_dim)]
where the time goes in v2:
time: 570 us; the launch traced here: 560 us
  Pallas kernels  464 us (81%)
  matrix products  48.9 us (9%)
  local copies, waits for them, and re-layouts  36.4 us (6%)
  other arithmetic  9.04 us (2%)
    pallas_call x1, Pallas kernels, reduce_all(): pl.pallas_call(reduce_kernel, out_shape=[jax.ShapeDtypeStruct((rows, cols...  199 us
    pallas_call x3, Pallas kernels, stage_call(): pl.pallas_call(body, grid=(n_rows // ROWS,), in_specs=in_specs, out_specs...  156 us
    pallas_call x1, Pallas kernels, gather_all(): pl.pallas_call(gather_kernel, out_shape=[jax.ShapeDtypeStruct((2 * N_CHIP...  109 us
    dot_general x5, matrix products, local_step(): lax.dot_general(left, right, (((0,), (0,)), ((), ())), preferred_element_...  43.5 us

profile of v2, /device:TPU:0, one launch (start us, length us, event | category | flops | bytes accessed | tf_op | source)
XLA Modules:
  0.0 559.9 jit_solution(698772353024715095)
XLA Ops:
  0.8 1.3 convert_element_type.78
  2.1 1.0 reshape.114.refs_2_
  3.1 0.7 convert_element_type.76.refs_0_
  3.8 0.7 convert_element_type.77.refs_1_
  6.1 0.7 fusion.10.refs_4_
  6.8 0.6 convert_element_type.79.refs_3_
  7.4 108.9 %gather_all.1 = (bf16[1024,4096]{1,0:T(8,128)(2,1)}, bf16[4096,1024]{1,0:T(8,128)(2,1)}, bf16[1024,3072]{1,0:T(8,128)(2,1)}, bf16[1024,1024]{1,0:T(8,128)(2,1)}, bf16[1024,1024]{1,0:T(8,128)(2,1)}) custom-call(bf16[32,4096]{1,0:T(8,128)(2,1)} %convert_element_type.76.refs_0_, bf16[128,1024]{1,0:T(8,128)(2,1)} %convert_element_type.77.refs_1_, ...), custom_call_target="tpu_custom_call" | custom-call | tf_op jit(solution)/shard_map/gather_all/pallas_call | solution.py:138
  116.3 2.9 copy.114
  119.4 0.4 reshape.127
  120.0 0.3 reshape.128
  120.4 0.7 select_maximum_fusion.1.vecs
  121.1 5.5 fusion.2
  126.8 1.6 pad_maximum_fusion
  128.4 49.6 %stage_one.1 = (f32[1024,1024]{1,0:T(8,128)}, bf16[1024,1024]{1,0:T(8,128)(2,1)}, bf16[1024,3072]{1,0:T(8,128)(2,1)}, bf16[1024,1024]{1,0:T(8,128)(2,1)}, f32[10...) custom-call(bf16[1024,1024]{1,0:T(8,128)(2,1)} %bitcast.67, bf16[1024,1024]{1,0:T(8,128)(2,1)} %get-tuple-element.44.misc, ...), custom_call_target="tpu_custom_call" | custom-call | tf_op jit(solution)/shard_map/stage_one/pallas_call | solution.py:488
  178.0 0.9 copy.131
  178.9 1.6 pad.32.clone
  180.5 49.0 %stage_two.1 = (bf16[1024,4096]{1,0:T(8,128)(2,1)}, bf16[1024,4096]{1,0:T(8,128)(2,1)}, bf16[1024,1024]{1,0:T(8,128)(2,1)}, f32[1024,1024]{1,0:T(8,128)}, bf16[1...) custom-call(bf16[1024,1024]{1,0:T(8,128)(2,1)} %get-tuple-element.47.c_in, f32[1024,1024]{1,0:T(8,128)} %get-tuple-element.48.h_mid, ...), custom_call_target="tpu_custom_call" | custom-call | tf_op jit(solution)/shard_map/stage_two/pallas_call | solution.py:488
  229.6 57.0 %stage_three.1 = (bf16[1024,3072]{1,0:T(8,128)(2,1)}, bf16[1024,1024]{1,0:T(8,128)(2,1)}, f32[24,1024]{1,0:T(8,128)}) custom-call(f32[1024,1024]{1,0:T(8,128)} %get-tuple-element.55.x_zero, f32[1024,1024]{1,0:T(8,128)} %get-tuple-element.56.d_mid, bf16[1024,1024]{1,0:T(8,128)(2,1)} %get-tuple-element.57.d_mid_b, bf16[1024,3072]{1,0:T(8,128)(2,1)} %get-tuple-element.58.qkv, ...), custom_call_target="tpu_custom_call" | custom-call | tf_op jit(solution)/shard_map/stage_three/pallas_call | solution.py:488
  286.6 0.9 add.41
  287.8 0.2 copy.121
  288.5 0.2 copy.124
  288.7 1.0 copy.125
  289.8 1.0 copy.126
  290.8 1.0 copy.127
  291.8 1.0 copy.128
  293.1 1.2 reshape.131
  294.3 1.3 reshape.132
  295.6 4.6 concatenate.22
  300.3 1.4 select_maximum_fusion
  301.7 0.3 copy-done.1
  301.9 6.3 %pad_add_fusion.refs_4_ = f32[1024,1024]{1,0:T(8,128)} fusion(f32[1024,256]{1,0:T(8,128)S(1)} %select_maximum_fusion, bf16[1024,1024]{1,0:T(8,128)(2,1)} %get-tuple-element.61, bf16[1024,1024]{1,0:T(8,128)(2,1)S(1)} %bitcast.68), kind=kOutput, calls=%fused_computation.2 | convolution fusion | flops 2148532224 | bytes 9437184 | tf_op jit(solution)/shard_map/dot_general | solution.py:552
  308.3 4.5 fusion.14.refs_3_
  312.8 9.6 %fusion.13.refs_2_ = f32[1024,3072]{1,0:T(8,128)} fusion(bf16[1024,1024]{1,0:T(8,128)(2,1)S(1)} %copy-done.16, bf16[1024,3072]{1,0:T(8,128)(2,1)S(1)} %bitcast.75), kind=kOutput, calls=%fused_computation.60 | convolution fusion | flops 6442450944 | bytes 20971520 | tf_op jit(solution)/shard_map/dot_general | solution.py:552
  322.5 11.5 %fusion.11.refs_0_ = f32[1024,4096]{1,0:T(8,128)} fusion(bf16[1024,1024]{1,0:T(8,128)(2,1)S(1)} %copy-done.2, bf16[1024,4096]{1,0:T(8,128)(2,1)S(1)} %bitcast.73), kind=kOutput, calls=%fused_computation.58 | convolution fusion | flops 8589934592 | bytes 27262976 | tf_op jit(solution)/shard_map/dot_general | solution.py:552
  334.0 11.6 %fusion.12.refs_1_ = f32[4096,1024]{1,0:T(8,128)} fusion(bf16[1024,4096]{1,0:T(8,128)(2,1)S(1)} %bitcast.71, bf16[1024,1024]{1,0:T(8,128)(2,1)S(1)} %bitcast.66), kind=kOutput, calls=%fused_computation.59 | convolution fusion | flops 8589934592 | bytes 27262976 | tf_op jit(solution)/shard_map/dot_general | solution.py:552
  345.5 199.4 %reduce_all.1 = (f32[32,4096]{1,0:T(8,128)}, f32[128,1024]{1,0:T(8,128)}, f32[32,3072]{1,0:T(8,128)}, f32[32,1024]{1,0:T(8,128)}, f32[32,1024]{1,0:T(8,128)}) custom-call(f32[1024,4096]{1,0:T(8,128)} %fusion.11.refs_0_, f32[4096,1024]{1,0:T(8,128)} %fusion.12.refs_1_, f32[1024,3072]{1,0:T(8,128)} %fusion.13.refs_2_, f32[1024,1024]{1,0:T(8,128)} %fusion.14.refs_3_, ...), custom_call_target="tpu_custom_call" | custom-call | tf_op jit(solution)/shard_map/reduce_all/pallas_call | solution.py:273
  544.9 2.1 reshape.133
  547.0 1.5 slice_bitcast_fusion
  548.6 1.4 slice_bitcast_fusion.2
  549.9 0.8 slice.118
  550.7 0.6 reshape.134
  551.3 0.8 slice.122
  552.1 0.6 reshape.135
  552.7 2.2 slice_reduce_fusion
  555.2 2.1 copy.130
  557.2 0.7 copy.139
  557.9 0.8 copy.140
  558.7 0.8 copy.141
  (121 shorter events, 3.5 us)
Async XLA Ops:
  0.7 2.4 copy-start.6
  0.7 3.1 copy-start.7
  0.7 3.9 copy-start.18
  0.7 4.0 copy-start.19
  0.7 4.1 copy-start.20
  0.7 4.2 copy-start.21
  0.7 4.3 copy-start.22
  0.7 4.4 copy-start.23
  0.7 4.5 copy-start.24
  0.8 4.6 copy-start.25
  0.8 4.7 copy-start.26
  0.8 4.8 copy-start.27
  0.8 4.9 copy-start.28
  0.8 5.0 copy-start.29
  0.8 5.2 copy-start.12
  0.8 5.3 copy-start.14
  0.8 6.0 %copy-start.10 = (f32[32,1024]{1,0:T(8,128)S(1)}, f32[32,1024]{1,0:T(8,128)}, u32[]{:S(2)}) copy-start(f32[32,1024]{1,0:T(8,128)} %param.33) | copy-start | bytes 393220
  119.2 1.9 copy-start.15
  128.4 49.6 %copy-start.4 = (bf16[16,50,1024]{2,0,1:T(8,128)(2,1)S(1)}, bf16[16,50,1024]{2,0,1:T(8,128)(2,1)}, u32[]{:S(2)}) copy-start(bf16[16,50,1024]{2,0,1:T(8,128)(2,1)} %param.41) | copy-start | bytes 4915204
  229.6 57.1 %copy-start.13 = (f32[24,1024]{1,0:T(8,128)S(1)}, f32[24,1024]{1,0:T(8,128)}, u32[]{:S(2)}) copy-start(f32[24,1024]{1,0:T(8,128)} %get-tuple-element.62) | copy-start | bytes 294916
  300.2 1.7 copy-start.1
  300.3 12.5 %slice-start.4 = ((s8[6291456]{0:T(1024)(128)(4,1)}), s8[4194304]{0:T(1024)(128)(4,1)S(1)}, s32[]{:S(2)}) async-start(s8[6291456]{0:T(1024)(128)(4,1)} %bitcast.74), calls=%async_computation.4 | async-start | bytes 8388608
  301.9 6.3 %copy-start.3 = (bf16[1024,1024]{1,0:T(8,128)(2,1)S(1)}, bf16[1024,1024]{1,0:T(8,128)(2,1)}, u32[]{:S(2)}) copy-start(bf16[1024,1024]{1,0:T(8,128)(2,1)} %get-tuple-element.57.d_mid_b) | copy-start | bytes 6291460
  301.9 6.3 %copy-start.17 = (bf16[1024,1024]{1,0:T(8,128)(2,1)S(1)}, bf16[1024,1024]{1,0:T(8,128)(2,1)}, u32[]{:S(2)}) copy-start(bf16[1024,1024]{1,0:T(8,128)(2,1)} %get-tuple-element.60) | copy-start | bytes 6291460
  301.9 10.9 %slice-start.5 = ((s8[6291456]{0:T(1024)(128)(4,1)}), s8[2097152]{0:T(1024)(128)(4,1)S(1)}, s32[]{:S(2)}) async-start(s8[6291456]{0:T(1024)(128)(4,1)} %bitcast.74), calls=%async_computation.5 | async-start | bytes 4194304
  308.3 4.5 copy-start.16
  308.3 14.1 %slice-start.2 = ((s8[8388608]{0:T(1024)(128)(4,1)}), s8[4194304]{0:T(1024)(128)(4,1)S(1)}, s32[]{:S(2)}) async-start(s8[8388608]{0:T(1024)(128)(4,1)} %bitcast.72), calls=%async_computation.2 | async-start | bytes 8388608
  312.8 9.6 %copy-start.2 = (bf16[1024,1024]{1,0:T(8,128)(2,1)S(1)}, bf16[1024,1024]{1,0:T(8,128)(2,1)}, u32[]{:S(2)}) copy-start(bf16[1024,1024]{1,0:T(8,128)(2,1)} %get-tuple-element.47.c_in) | copy-start | bytes 6291460
  312.8 9.6 %slice-start.3 = ((s8[8388608]{0:T(1024)(128)(4,1)}), s8[4194304]{0:T(1024)(128)(4,1)S(1)}, s32[]{:S(2)}) async-start(s8[8388608]{0:T(1024)(128)(4,1)} %bitcast.72), calls=%async_computation.3 | async-start | bytes 8388608
  312.8 21.1 %slice-start = ((s8[8388608]{0:T(1024)(128)(4,1)}), s8[4194304]{0:T(1024)(128)(4,1)S(1)}, s32[]{:S(2)}) async-start(s8[8388608]{0:T(1024)(128)(4,1)} %bitcast.70), calls=%async_computation | async-start | bytes 8388608
  322.4 11.5 %copy-start = (bf16[16,64,1024]{2,1,0:T(8,128)(2,1)S(1)}, bf16[16,64,1024]{2,1,0:T(8,128)(2,1)}, u32[]{:S(2)}) copy-start(bf16[16,64,1024]{2,1,0:T(8,128)(2,1)} %pad.32.clone) | copy-start | bytes 6291460
  322.4 11.5 %slice-start.1 = ((s8[8388608]{0:T(1024)(128)(4,1)}), s8[4194304]{0:T(1024)(128)(4,1)S(1)}, s32[]{:S(2)}) async-start(s8[8388608]{0:T(1024)(128)(4,1)} %bitcast.70), calls=%async_computation.1 | async-start | bytes 8388608
  345.5 209.5 %copy-start.5 = (bf16[1024,1024]{1,0:T(8,128)(2,1)S(1)}, bf16[1024,1024]{1,0:T(8,128)(2,1)}, u32[]{:S(2)}) copy-start(bf16[1024,1024]{1,0:T(8,128)(2,1)} %get-tuple-element.51) | copy-start | bytes 6291460
  555.1 2.1 copy-start.11
  555.2 2.7 copy-start.9
  555.2 3.5 copy-start.8

commit v3 on v2

--- a/solution.py
+++ b/solution.py
@@ -30,11 +30,11 @@
     (QKV, 0, 32, 0, 2048, 4), (QKV, 0, 32, 2048, 1024, 5), (OUT, 0, 32, 0, 1024, 5),
     (FC, 0, 32, 0, 2048, 0), (FC, 0, 32, 2048, 2048, 1), (PROJ, 0, 64, 0, 1024, 2), (PROJ, 64, 64, 0, 1024, 3),
 )
-REDUCE_STREAMS = (
-    (FC, 0, 64, 0, 1024, 0), (FC, 0, 64, 1024, 1024, 1), (PROJ, 0, 128, 0, 512, 2), (PROJ, 128, 128, 0, 512, 3),
-    (QKV, 0, 64, 0, 1024, 4), (QKV, 0, 64, 1024, 512, 5), (OUT, 0, 64, 0, 512, 5),
-    (MISC, 0, 64, 0, 128, 0), (MISC, 0, 64, 128, 128, 1), (MISC, 0, 64, 256, 128, 2), (MISC, 0, 64, 384, 128, 3),
-)
+MLP_STREAMS = tuple((FC, 0, 64, 384 * k, 384, k) for k in range(4)) + ((FC, 0, 64, 1536, 256, 4), (FC, 0, 64, 1792, 256, 5)) + tuple(
+    (PROJ, 128 * (place % 2), 128, 128 * (place // 2), 128, ring) for place, ring in enumerate((0, 1, 2, 3, 4, 5, 4, 5)))
+REST_STREAMS = tuple((QKV, 0, 64, 256 * k, 256, k) for k in range(6)) + tuple((OUT, 0, 64, 128 * k, 128, k) for k in range(4)) + (
+    (MISC, 0, 64, 0, 128, 4), (MISC, 0, 64, 128, 128, 5), (MISC, 0, 32, 256, 128, 0), (MISC, 32, 32, 256, 128, 1),
+    (MISC, 0, 32, 384, 128, 2), (MISC, 32, 32, 384, 128, 3))
 
 
 def pick(table, index):
@@ -146,143 +146,139 @@
     )(*shards)
 
 
-def reduce_kernel(*refs):
-    grads, outs = refs[:5], refs[5:10]
-    accs, owns, twins = refs[10:15], refs[15:20], refs[20:25]
-    own_sem, twin_send, twin_recv, send_sem, recv_sem, ring_free, twin_free, end_own, end_send, end_recv = refs[25:]
-    place = Place()
-    n_streams = len(REDUCE_STREAMS)
-
-    def part(i, ref, slot):
-        _, row, rows, col, cols, _ = REDUCE_STREAMS[i]
-        return ref.at[slot, pl.ds(row, rows), pl.ds(col, cols)]
-
-    def source(i, chip, core):
-        arr, row, rows, col, cols, _ = REDUCE_STREAMS[i]
+class RingSum:
+    def __init__(self, place, arrays, streams, accs, owns, gives, twins, sems, term):
+        self.place, self.streams, self.term, self.arrays = place, streams, term, arrays
+        self.accs, self.owns, self.gives, self.twins = [dict(zip(arrays, refs)) for refs in (accs, owns, gives, twins)]
+        (self.twin_send, self.twin_recv, self.send_sem, self.recv_sem, self.ring_free, self.twin_free,
+         self.end_own, self.end_send, self.end_recv) = sems
+
+    def part(self, i, ref, *slot):
+        _, row, rows, col, cols, _ = self.streams[i]
+        return ref.at[(*slot, pl.ds(row, rows), pl.ds(col, cols))]
+
+    def push(self, i, slot):
+        arr = self.streams[i][0]
+        return pltpu.make_async_remote_copy(src_ref=self.part(i, self.gives[arr]), dst_ref=self.part(i, self.twins[arr], slot),
+                                            send_sem=self.twin_send.at[i], recv_sem=self.twin_recv.at[i, slot],
+                                            device_id=(self.place.sibling,), device_id_type=MESH_ID)
+
+    def pass_on(self, i, slot, slot_next):
+        arr, k = self.streams[i][0], self.streams[i][5]
+        return pltpu.make_async_remote_copy(src_ref=self.part(i, self.accs[arr], slot), dst_ref=self.part(i, self.accs[arr], slot_next),
+                                            send_sem=self.send_sem.at[i, slot], recv_sem=self.recv_sem.at[i, slot_next],
+                                            device_id=(self.place.after[k],), device_id_type=MESH_ID)
+
+    def compute(self, group, step, first):
+        chips = self.place.chips_back(step + 1)
+        slot = lax.rem(jnp.int32(step), 2)
+        for i in group:
+            arr, k = self.streams[i][0], self.streams[i][5]
+            if not first:
+                self.push(i, slot).wait_send()
+            self.part(i, self.gives[arr])[...] = self.term(i, chips[k], 1 - self.place.core)
+            if not first:
+                @pl.when(step >= 2)
+                def _():
+                    pl.semaphore_wait(self.twin_free.at[i], 1)
+            self.push(i, slot).start()
+            self.part(i, self.owns[arr])[...] = self.term(i, chips[k], self.place.core)
+
+    def advance(self, group, step):
+        slot, slot_next, slot_last, pair = lax.rem(step, 3), lax.rem(step + 1, 3), lax.rem(step + 2, 3), lax.rem(step, 2)
+        for i in group:
+            arr, row, rows, col, cols, k = self.streams[i]
+            acc, own, twin = self.part(i, self.accs[arr], slot), self.part(i, self.owns[arr]), self.part(i, self.twins[arr], pair)
+            self.push(i, pair).wait_recv()
+
+            @pl.when(step == 0)
+            def _():
+                acc[...] = own[...] + twin[...]
+
+            @pl.when(step > 0)
+            def _():
+                self.pass_on(i, slot, slot).wait_recv()
+                acc[...] = acc[...] + (own[...] + twin[...])
+
+            @pl.when(jnp.logical_and(step >= 2, step < N_CHIP - 1))
+            def _():
+                pl.semaphore_wait(self.ring_free.at[i], 1)
+
+            @pl.when(step < N_CHIP - 1)
+            def _():
+                self.pass_on(i, slot, slot_next).start()
+
+            @pl.when(step < N_CHIP - 2)
+            def _():
+                pl.semaphore_signal(self.twin_free.at[i], inc=1, device_id=(self.place.sibling,), device_id_type=MESH_ID)
+
+        for i in group:
+            k = self.streams[i][5]
+
+            @pl.when(step >= 1)
+            def _():
+                self.pass_on(i, slot_last, slot).wait_send()
+
+            @pl.when(jnp.logical_and(step >= 1, step < N_CHIP - 2))
+            def _():
+                pl.semaphore_signal(self.ring_free.at[i], inc=1, device_id=(self.place.before[k],), device_id_type=MESH_ID)
+
+    def run(self, groups, hook):
+        for group in groups:
+            self.compute(group, 0, True)
+
+        def ring_step(step, carry):
+            for place, group in enumerate(groups):
+                self.advance(group, step)
+
+                @pl.when(step < N_CHIP - 1)
+                def _():
+                    self.compute(group, step + 1, False)
+
+                hook(place, step)
+            return carry
+
+        lax.fori_loop(0, N_CHIP, ring_step, 0)
+
+    def finish(self, outs):
+        for i in range(len(self.streams)):
+            self.push(i, (N_CHIP - 1) % 2).wait_send()
+        last = (N_CHIP - 1) % 3
+        ends = []
+        for place, arr in enumerate(self.arrays):
+            rows, half, core = ARRAYS[arr][0], ARRAYS[arr][1] // 2, self.place.core
+            target = outs[place].at[:, pl.ds(pl.multiple_of(core * half, 128), half)]
+            keep_rows = self.accs[arr].at[last, pl.ds(pl.multiple_of(core * rows, 32), rows), :]
+            give_rows = self.accs[arr].at[last, pl.ds(pl.multiple_of((1 - core) * rows, 32), rows), :]
+            ends.append(pltpu.make_async_copy(keep_rows, target, self.end_own.at[place]))
+            ends.append(pltpu.make_async_remote_copy(src_ref=give_rows, dst_ref=target, send_sem=self.end_send.at[place], recv_sem=self.end_recv.at[place],
+                                                     device_id=(self.place.sibling,), device_id_type=MESH_ID))
+        for end in ends:
+            end.start()
+        for end in ends:
+            end.wait()
+
+
+def ring_scratch(arrays, streams):
+    shapes = [(2 * ARRAYS[arr][0], ARRAYS[arr][1] // 2) for arr in arrays]
+    buffers = [pltpu.VMEM((*lead, *shape), jnp.float32) for lead in ((3,), (), (), (2,)) for shape in shapes]
+    dma, regular, n = pltpu.SemaphoreType.DMA, pltpu.SemaphoreType.REGULAR, len(streams)
+    return buffers + [dma((n,)), dma((n, 2)), dma((n, 3)), dma((n, 3)), regular((n,)), regular((n,))] + [dma((len(arrays),))] * 3
+
+
+def split_scratch(refs, n_arrays):
+    buffers, sems = refs[:4 * n_arrays], refs[4 * n_arrays:4 * n_arrays + 9]
+    return [buffers[n_arrays * b:n_arrays * (b + 1)] for b in range(4)], sems
+
+
+def term_of(streams, lefts, rights):
+    def term(i, chip, core):
+        arr, row, rows, col, cols, _ = streams[i]
         half = ARRAYS[arr][1] // 2
-        first = pl.multiple_of(2 * chip * ARRAYS[arr][0] + row, 64)
-        return grads[arr].at[pl.ds(first, rows), pl.ds(pl.multiple_of(core * half + col, 128), cols)]
-
-    def load(i, chip, slot):
-        return pltpu.make_async_copy(source(i, chip, place.core), part(i, owns[REDUCE_STREAMS[i][0]], slot), own_sem.at[i, slot])
-
-    def push(i, chip, slot):
-        return pltpu.make_async_remote_copy(src_ref=source(i, chip, 1 - place.core), dst_ref=part(i, twins[REDUCE_STREAMS[i][0]], slot),
-                                            send_sem=twin_send.at[i, slot], recv_sem=twin_recv.at[i, slot],
-                                            device_id=(place.sibling,), device_id_type=MESH_ID)
-
-    def pass_on(i, slot, slot_next):
-        arr, k = REDUCE_STREAMS[i][0], REDUCE_STREAMS[i][5]
-        return pltpu.make_async_remote_copy(src_ref=part(i, accs[arr], slot), dst_ref=part(i, accs[arr], slot_next),
-                                            send_sem=send_sem.at[i, slot], recv_sem=recv_sem.at[i, slot_next],
-                                            device_id=(place.after[k],), device_id_type=MESH_ID)
-
-    place.meet()
-    for step in range(2):
-        chips = place.chips_back(step + 1)
-        for i in range(n_streams):
-            load(i, chips[REDUCE_STREAMS[i][5]], step).start()
-            push(i, chips[REDUCE_STREAMS[i][5]], step).start()
-
-    def ring_step(step, carry):
-        slot, pair = lax.rem(step, 3), lax.rem(step, 2)
-        slot_next, slot_last = lax.rem(step + 1, 3), lax.rem(step + 2, 3)
-        chips = place.chips_back(step + 3)
-        for i in range(n_streams):
-            arr, row, rows, col, cols, k = REDUCE_STREAMS[i]
-            load(i, chips[k], pair).wait()
-            push(i, chips[k], pair).wait_recv()
-
-            @pl.when(step == 0)
-            def _():
-                def add_two(r, c):
-                    at = pl.ds(pl.multiple_of(row + 8 * r, 8), 8)
-                    lanes = pl.ds(col, cols)
-                    accs[arr][slot, at, lanes] = owns[arr][pair, at, lanes] + twins[arr][pair, at, lanes]
-                    return c
-                lax.fori_loop(0, rows // 8, add_two, 0)
-
-            @pl.when(step > 0)
-            def _():
-                pass_on(i, slot, slot).wait_recv()
-
-                def add_three(r, c):
-                    at = pl.ds(pl.multiple_of(row + 8 * r, 8), 8)
-                    lanes = pl.ds(col, cols)
-                    accs[arr][slot, at, lanes] = accs[arr][slot, at, lanes] + (owns[arr][pair, at, lanes] + twins[arr][pair, at, lanes])
-                    return c
-                lax.fori_loop(0, rows // 8, add_three, 0)
-
-            @pl.when(jnp.logical_and(step >= 2, step < N_CHIP - 1))
-            def _():
-                pl.semaphore_wait(ring_free.at[i], 1)
-
-            @pl.when(step < N_CHIP - 1)
-            def _():
-                pass_on(i, slot, slot_next).start()
-
-            @pl.when(step < N_CHIP - 2)
-            def _():
-                pl.semaphore_signal(twin_free.at[i], inc=1, device_id=(place.sibling,), device_id_type=MESH_ID)
-                load(i, chips[k], pair).start()
-
-        for i in range(n_streams):
-            k = REDUCE_STREAMS[i][5]
-            push(i, chips[k], pair).wait_send()
-
-            @pl.when(step < N_CHIP - 2)
-            def _():
-                pl.semaphore_wait(twin_free.at[i], 1)
-                push(i, chips[k], pair).start()
-
-            @pl.when(step >= 1)
-            def _():
-                pass_on(i, slot_last, slot).wait_send()
-
-            @pl.when(jnp.logical_and(step >= 1, step < N_CHIP - 2))
-            def _():
-                pl.semaphore_signal(ring_free.at[i], inc=1, device_id=(place.before[k],), device_id_type=MESH_ID)
-        return carry
-
-    lax.fori_loop(0, N_CHIP, ring_step, 0)
-    last = (N_CHIP - 1) % 3
-
-    def end_copies(arr):
-        rows, half = ARRAYS[arr][0], ARRAYS[arr][1] // 2
-        target = outs[arr].at[:, pl.ds(pl.multiple_of(place.core * half, 128), half)]
-        keep_rows = accs[arr].at[last, pl.ds(pl.multiple_of(place.core * rows, 32), rows), :]
-        give_rows = accs[arr].at[last, pl.ds(pl.multiple_of((1 - place.core) * rows, 32), rows), :]
-        return (pltpu.make_async_copy(keep_rows, target, end_own.at[arr]),
-                pltpu.make_async_remote_copy(src_ref=give_rows, dst_ref=target, send_sem=end_send.at[arr], recv_sem=end_recv.at[arr],
-                                             device_id=(place.sibling,), device_id_type=MESH_ID))
-
-    for arr in range(5):
-        local, cross = end_copies(arr)
-        local.start()
-        cross.start()
-    for arr in range(5):
-        local, cross = end_copies(arr)
-        local.wait()
-        cross.wait()
-
-
-def reduce_all(grads):
-    n_streams = len(REDUCE_STREAMS)
-    slots = lambda n: [pltpu.VMEM((n, 2 * rows, cols // 2), jnp.float32) for rows, cols in ARRAYS]
-    sems = lambda n: pltpu.SemaphoreType.DMA((n_streams, n))
-    return pl.pallas_call(
-        reduce_kernel,
-        out_shape=[jax.ShapeDtypeStruct((rows, cols), jnp.float32) for rows, cols in ARRAYS],
-        in_specs=[pl.BlockSpec(memory_space=pl.ANY)] * 5,
-        out_specs=[pl.BlockSpec(memory_space=pl.ANY)] * 5,
-        scratch_shapes=slots(3) + slots(2) + slots(2) + [
-            sems(2), sems(2), sems(2), sems(3), sems(3),
-            pltpu.SemaphoreType.REGULAR((n_streams,)), pltpu.SemaphoreType.REGULAR((n_streams,)),
-            pltpu.SemaphoreType.DMA((5,)), pltpu.SemaphoreType.DMA((5,)), pltpu.SemaphoreType.DMA((5,)),
-        ],
-        compiler_params=pltpu.CompilerParams(collective_id=1, has_side_effects=True),
-        name='reduce_all',
-    )(*grads)
+        first = pl.multiple_of(2 * chip * ARRAYS[arr][0] + row, 16)
+        return dot_nn(lefts[arr][pl.ds(first, rows), :], rights[arr][:, pl.ds(pl.multiple_of(core * half + col, 128), cols)])
+    return term
+
 
 HEAD_GROUP, HEAD_DIM, SEQ, N_TOKEN = 256, 64, 64, 50
 ROWS = 256
@@ -355,17 +351,17 @@
     return vecs[place:place + 1, :]
 
 
-def is_cls():
-    return lax.broadcasted_iota(jnp.int32, (ROWS, 1), 0) % SEQ == 0
-
-
-def stage_one(x_in, misc, w_qkv, w_out, vecs, x_zero, a_out, qkv, ctx, h_mid, c_out):
-    start = jnp.where(is_cls(), row_of(vecs, 'cls_tok'), row_of(vecs, 'b_patch'))
+def is_cls(rows):
+    return lax.broadcasted_iota(jnp.int32, (rows, 1), 0) % SEQ == 0
+
+
+def stage_one(x_in, misc, w_qkv, w_out, vecs, x_zero, a_turned, qkv, ctx_turned, h_mid, c_out, c_turned, ctx):
+    start = jnp.where(is_cls(ROWS), row_of(vecs, 'cls_tok'), row_of(vecs, 'b_patch'))
     x_sum = dot_nt(x_in[...], misc[...]) + start
     x_zero[...] = x_sum
     h_zero = normalize(x_sum)[0] * row_of(vecs, 'lnp_g') + row_of(vecs, 'lnp_b')
     a_in = (normalize(h_zero)[0] * row_of(vecs, 'ln1_g') + row_of(vecs, 'ln1_b')).astype(jnp.bfloat16)
-    a_out[...] = a_in
+    a_turned[...] = a_in.T
     for s in range(3):
         cols = pl.ds(1024 * s, 1024)
         qkv[:, cols] = (dot_nn(a_in, w_qkv[:, cols]) + vecs[VEC_QKV + s:VEC_QKV + s + 1, :]).astype(jnp.bfloat16)
@@ -379,9 +375,13 @@
         return carry
 
     lax.fori_loop(0, ROWS // SEQ, image, 0)
-    mid = h_zero + dot_nn(ctx[...], w_out[...]) + row_of(vecs, 'b_out')
+    context = ctx[...]
+    ctx_turned[...] = context.T
+    mid = h_zero + dot_nn(context, w_out[...]) + row_of(vecs, 'b_out')
     h_mid[...] = mid
-    c_out[...] = (normalize(mid)[0] * row_of(vecs, 'ln2_g') + row_of(vecs, 'ln2_b')).astype(jnp.bfloat16)
+    c_in = (normalize(mid)[0] * row_of(vecs, 'ln2_g') + row_of(vecs, 'ln2_b')).astype(jnp.bfloat16)
+    c_out[...] = c_in
+    c_turned[...] = c_in.T
 
 
 def add_row(sums, place, value):
@@ -394,7 +394,7 @@
         sums[...] = jnp.zeros_like(sums)
 
 
-def stage_two(c_in, h_mid, grad_h1, w_fc, w_proj, vecs, gelu_out, d_pre_out, h_one, d_mid, d_mid_b, sums, h_acc, d_c_acc):
+def stage_two(c_in, h_mid, grad_h1, w_fc, w_proj, vecs, gelu_turned, d_pre_out, h_one, d_mid, d_mid_b, sums, h_acc, d_c_acc):
     clear_first(sums)
     c_block, g_block = c_in[...], grad_h1[...]
     tile = 1024
@@ -403,7 +403,7 @@
         pre_act = dot_nn(c_block, w_fc[:, cols]) + vecs[VEC_FC + f:VEC_FC + f + 1, :]
         normal_cdf = 0.5 * (1.0 + lax.erf(pre_act * INV_SQRT2))
         gelu = (pre_act * normal_cdf).astype(jnp.bfloat16)
-        gelu_out[:, cols] = gelu
+        gelu_turned[cols, :] = gelu.T
         slope = normal_cdf + pre_act * jnp.exp(-0.5 * pre_act * pre_act) * INV_SQRT_2PI
         d_pre = dot_nt(g_block, w_proj[cols, :]) * slope
         add_row(sums, VEC_FC + f, d_pre)
@@ -431,46 +431,161 @@
     add_row(sums, VEC_AT['b_out'], d_sum)
 
 
-def stage_three(x_zero, d_mid, d_mid_b, qkv, w_qkv, w_out, vecs, d_qkv_out, d_emb_out, sums, d_ctx, d_part):
-    clear_first(sums)
-    d_ctx[...] = dot_nt(d_mid_b[...], w_out[...]).astype(jnp.bfloat16)
-    d_part[...] = jnp.zeros_like(d_part)
-
-    def image(b, carry):
-        rows = pl.ds(pl.multiple_of(b * SEQ, SEQ), SEQ)
-        for g in range(4):
-            places = [pl.ds(1024 * s + HEAD_GROUP * g, HEAD_GROUP) for s in range(3)]
-            q_block, k_block, v_block = [qkv[rows, place] for place in places]
-            d_block = d_ctx[rows, pl.ds(HEAD_GROUP * g, HEAD_GROUP)]
-            k_stack = stack_heads(k_block)
-            prob = probabilities(q_block, k_stack)
-            d_prob = dot_nt(d_block, stack_heads(v_block))
-            d_logit = (prob * (d_prob - per_head(prob * d_prob, jnp.sum, 0.0)) * LOGIT_SCALE).astype(jnp.bfloat16)
-            g_q = dot_nn(d_logit, k_stack)
-            g_k = unstack_heads(dot_tn(d_logit, q_block))
-            g_v = unstack_heads(dot_tn(prob.astype(jnp.bfloat16), d_block))
-            for place, grad in zip(places, (g_q, g_k, g_v)):
-                d_qkv_out[rows, place] = grad.astype(jnp.bfloat16)
-                d_part[:, place] += jnp.sum(grad.reshape(SEQ // 8, 8, HEAD_GROUP), axis=0)
-        return carry
-
-    lax.fori_loop(0, ROWS // SEQ, image, 0)
-    for s in range(3):
-        add_row(sums, VEC_QKV + s, d_part[:, pl.ds(1024 * s, 1024)])
-    d_a = dot_nt(d_qkv_out[...], w_qkv[...])
-    hat_p, inv_p = normalize(x_zero[...])
+def context_back(b, qkv, d_ctx, d_qkv, d_part):
+    for g in range(4):
+        places = [pl.ds(1024 * s + HEAD_GROUP * g, HEAD_GROUP) for s in range(3)]
+        q_block, k_block, v_block = [qkv[b, :, place] for place in places]
+        d_block = d_ctx[:, HEAD_GROUP * g:HEAD_GROUP * (g + 1)]
+        k_stack = stack_heads(k_block)
+        prob = probabilities(q_block, k_stack)
+        d_prob = dot_nt(d_block, stack_heads(v_block))
+        d_logit = (prob * (d_prob - per_head(prob * d_prob, jnp.sum, 0.0)) * LOGIT_SCALE).astype(jnp.bfloat16)
+        g_q = dot_nn(d_logit, k_stack)
+        g_k = unstack_heads(dot_tn(d_logit, q_block))
+        g_v = unstack_heads(dot_tn(prob.astype(jnp.bfloat16), d_block))
+        for place, grad in zip(places, (g_q, g_k, g_v)):
+            d_qkv[b, :, place] = grad.astype(jnp.bfloat16)
+            d_part[:, place] += jnp.sum(grad.reshape(SEQ // 8, 8, HEAD_GROUP), axis=0)
+
+
+def entry_back(x_sum, d_mid, d_a, vecs, sums):
+    hat_p, inv_p = normalize(x_sum)
     h_zero = hat_p * row_of(vecs, 'lnp_g') + row_of(vecs, 'lnp_b')
     hat_1, inv_1 = normalize(h_zero)
     add_row(sums, VEC_AT['ln1_g'], d_a * hat_1)
     add_row(sums, VEC_AT['ln1_b'], d_a)
-    d_zero = normalize_back(d_a, hat_1, inv_1, row_of(vecs, 'ln1_g')) + d_mid[...]
+    d_zero = normalize_back(d_a, hat_1, inv_1, row_of(vecs, 'ln1_g')) + d_mid
     add_row(sums, VEC_AT['lnp_g'], d_zero * hat_p)
     add_row(sums, VEC_AT['lnp_b'], d_zero)
     d_x = normalize_back(d_zero, hat_p, inv_p, row_of(vecs, 'lnp_g'))
-    d_emb = jnp.where(is_cls(), 0.0, d_x)
-    add_row(sums, VEC_AT['cls_tok'], jnp.where(is_cls(), d_x, 0.0))
+    cls = is_cls(SEQ)
+    d_emb = jnp.where(cls, 0.0, d_x)
+    add_row(sums, VEC_AT['cls_tok'], jnp.where(cls, d_x, 0.0))
     add_row(sums, VEC_AT['b_patch'], d_emb)
-    d_emb_out[...] = d_emb.astype(jnp.bfloat16)
+    return d_emb.astype(jnp.bfloat16)
+
+
+def mlp_sums_kernel(*refs):
+    (c_hbm, pre_hbm, gelu_hbm, rows_hbm, qkv_w_hbm, out_w_hbm, vecs, x_hbm, mid_hbm, mid_b_hbm, qkv_hbm) = refs[:11]
+    fc_out, proj_out, d_qkv_out, d_emb_out, sums = refs[11:16]
+    (c_turned, d_pre, gelu_turned, grad_rows, w_qkv, w_out, x_zero, d_mid, d_mid_b, qkv, d_qkv, d_emb, d_part,
+     load_sem, in_sem, out_sem) = refs[16:32]
+    (accs, owns, gives, twins), sems = split_scratch(refs[32:], 2)
+    place = Place()
+    loads = [pltpu.make_async_copy(src, dst, load_sem.at[n]) for n, (src, dst) in enumerate(
+        ((c_hbm, c_turned), (pre_hbm, d_pre), (gelu_hbm, gelu_turned), (rows_hbm, grad_rows), (qkv_w_hbm, w_qkv), (out_w_hbm, w_out)))]
+    for load in loads:
+        load.start()
+    n_img = x_hbm.shape[0] // SEQ
+
+    def image_in(b, slot):
+        rows = pl.ds(pl.multiple_of(b * SEQ, SEQ), SEQ)
+        return [pltpu.make_async_copy(src.at[rows, :], dst.at[slot], in_sem.at[n, slot]) for n, (src, dst) in enumerate(
+            ((x_hbm, x_zero), (mid_hbm, d_mid), (mid_b_hbm, d_mid_b), (qkv_hbm, qkv)))]
+
+    def image_out(b, slot):
+        rows = pl.ds(pl.multiple_of(b * SEQ, SEQ), SEQ)
+        return [pltpu.make_async_copy(src.at[slot], dst.at[rows, :], out_sem.at[n, slot]) for n, (src, dst) in enumerate(
+            ((d_qkv, d_qkv_out), (d_emb, d_emb_out)))]
+
+    for copy in image_in(0, 0):
+        copy.start()
+    sums[...] = jnp.zeros_like(sums)
+    d_part[...] = jnp.zeros_like(d_part)
+    place.meet()
+    term = term_of(MLP_STREAMS, {FC: c_turned, PROJ: gelu_turned}, {FC: d_pre, PROJ: grad_rows})
+    ring = RingSum(place, (FC, PROJ), MLP_STREAMS, accs, owns, gives, twins, sems, term)
+    for load in loads:
+        load.wait()
+
+    def hook(half, step):
+        slot = lax.rem(step, 2)
+        if half == 0:
+            @pl.when(step < n_img - 1)
+            def _():
+                for copy in image_in(step + 1, 1 - slot):
+                    copy.start()
+
+            for copy in image_in(step, slot):
+                copy.wait()
+
+            @pl.when(step >= 2)
+            def _():
+                for copy in image_out(step - 2, slot):
+                    copy.wait()
+
+            d_ctx = dot_nt(d_mid_b[slot], w_out[...]).astype(jnp.bfloat16)
+            context_back(slot, qkv, d_ctx, d_qkv, d_part)
+        else:
+            d_a = dot_nt(d_qkv[slot], w_qkv[...])
+            d_emb[slot] = entry_back(x_zero[slot], d_mid[slot], d_a, vecs, sums)
+            for copy in image_out(step, slot):
+                copy.start()
+
+    ring.run((tuple(range(6)), tuple(range(6, len(MLP_STREAMS)))), hook)
+    for step in (n_img - 2, n_img - 1):
+        for copy in image_out(step, step % 2):
+            copy.wait()
+    for s in range(3):
+        add_row(sums, VEC_QKV + s, d_part[:, pl.ds(1024 * s, 1024)])
+    ring.finish((fc_out, proj_out))
+
+
+def mlp_sums(c_turned, d_pre, gelu_turned, grad_rows, w_qkv, w_out, vecs, x_zero, d_mid, d_mid_b, qkv):
+    bf, f32, dma = jnp.bfloat16, jnp.float32, pltpu.SemaphoreType.DMA
+    n_rows = x_zero.shape[0]
+    assert n_rows // SEQ == N_CHIP
+    out_shape = [jax.ShapeDtypeStruct(ARRAYS[FC], f32), jax.ShapeDtypeStruct(ARRAYS[PROJ], f32), jax.ShapeDtypeStruct((n_rows, 3072), bf),
+                 jax.ShapeDtypeStruct((n_rows, 1024), bf), jax.ShapeDtypeStruct((VEC_ROWS, 1024), f32)]
+    anywhere, vmem = pl.BlockSpec(memory_space=pl.ANY), pl.BlockSpec(memory_space=pltpu.VMEM)
+    scratch = [pltpu.VMEM(a.shape, bf) for a in (c_turned, d_pre, gelu_turned, grad_rows, w_qkv, w_out)]
+    scratch += [pltpu.VMEM((2, SEQ, 1024), f32), pltpu.VMEM((2, SEQ, 1024), f32), pltpu.VMEM((2, SEQ, 1024), bf), pltpu.VMEM((2, SEQ, 3072), bf),
+                pltpu.VMEM((2, SEQ, 3072), bf), pltpu.VMEM((2, SEQ, 1024), bf), pltpu.VMEM((8, 3072), f32), dma((6,)), dma((4, 2)), dma((2, 2))]
+    return pl.pallas_call(
+        mlp_sums_kernel, out_shape=out_shape, in_specs=[anywhere] * 6 + [vmem] + [anywhere] * 4, out_specs=[anywhere] * 4 + [vmem],
+        scratch_shapes=scratch + ring_scratch((FC, PROJ), MLP_STREAMS),
+        compiler_params=pltpu.CompilerParams(collective_id=1, has_side_effects=True, vmem_limit_bytes=62 * 1024 * 1024), name='mlp_sums',
+    )(c_turned, d_pre, gelu_turned, grad_rows, w_qkv, w_out, vecs, x_zero, d_mid, d_mid_b, qkv)
+
+
+def rest_sums_kernel(*refs):
+    (a_hbm, dqkv_hbm, ctx_hbm, mid_hbm, emb_hbm, in_hbm, vec_hbm) = refs[:7]
+    outs = refs[7:10]
+    (a_turned, d_qkv, ctx_turned, d_mid_b, emb_turned, x_in, g_vec, load_sem) = refs[10:18]
+    (accs, owns, gives, twins), sems = split_scratch(refs[18:], 3)
+    place = Place()
+    loads = [pltpu.make_async_copy(src, dst, load_sem.at[n]) for n, (src, dst) in enumerate(
+        ((a_hbm, a_turned), (dqkv_hbm, d_qkv), (ctx_hbm, ctx_turned), (mid_hbm, d_mid_b), (emb_hbm, emb_turned), (in_hbm, x_in), (vec_hbm, g_vec)))]
+    for load in loads:
+        load.start()
+    place.meet()
+    product = term_of(REST_STREAMS, {QKV: a_turned, OUT: ctx_turned, MISC: emb_turned}, {QKV: d_qkv, OUT: d_mid_b, MISC: x_in})
+
+    def term(i, chip, core):
+        arr, row, rows, col, cols, _ = REST_STREAMS[i]
+        block = product(i, chip, core)
+        if arr == MISC and col >= 256:
+            first = pl.multiple_of(2 * chip * ARRAYS[arr][0] + row, 16)
+            block = block + jnp.where(core == 1, g_vec[pl.ds(first, rows), pl.ds(col - 256, cols)], 0.0)
+        return block
+
+    ring = RingSum(place, (QKV, OUT, MISC), REST_STREAMS, accs, owns, gives, twins, sems, term)
+    for load in loads:
+        load.wait()
+    ring.run((tuple(range(6)), tuple(range(6, len(REST_STREAMS)))), lambda half, step: None)
+    ring.finish(outs)
+
+
+def rest_sums(a_turned, d_qkv, ctx_turned, d_mid_b, emb_turned, x_in, g_vec):
+    arrays = (QKV, OUT, MISC)
+    operands = (a_turned, d_qkv, ctx_turned, d_mid_b, emb_turned, x_in, g_vec)
+    anywhere = pl.BlockSpec(memory_space=pl.ANY)
+    return pl.pallas_call(
+        rest_sums_kernel, out_shape=[jax.ShapeDtypeStruct(ARRAYS[arr], jnp.float32) for arr in arrays],
+        in_specs=[anywhere] * 7, out_specs=[anywhere] * 3,
+        scratch_shapes=[pltpu.VMEM(a.shape, a.dtype) for a in operands] + [pltpu.SemaphoreType.DMA((7,))] + ring_scratch(arrays, REST_STREAMS),
+        compiler_params=pltpu.CompilerParams(collective_id=2, has_side_effects=True, vmem_limit_bytes=62 * 1024 * 1024), name='rest_sums',
+    )(*operands)
 
 
 def whole(shape):
@@ -483,8 +598,17 @@
 
 def stage_call(body, name, n_rows, ins, outs, scratch=()):
     in_specs = [rows_of(a.shape[1]) if a.shape[0] == n_rows and not held else whole(a.shape) for a, held in ins]
-    out_specs = [pl.BlockSpec((VEC_ROWS, 1024), lambda i: (0, 0)) if dtype is None else rows_of(width) for width, dtype in outs]
-    out_shape = [jax.ShapeDtypeStruct((VEC_ROWS, 1024), jnp.float32) if dtype is None else jax.ShapeDtypeStruct((n_rows, width), dtype) for width, dtype in outs]
+    out_specs, out_shape = [], []
+    for width, dtype in outs:
+        if dtype is None:
+            out_specs.append(pl.BlockSpec((VEC_ROWS, 1024), lambda i: (0, 0)))
+            out_shape.append(jax.ShapeDtypeStruct((VEC_ROWS, 1024), jnp.float32))
+        elif width < 0:
+            out_specs.append(pl.BlockSpec((-width, ROWS), lambda i: (0, i)))
+            out_shape.append(jax.ShapeDtypeStruct((-width, n_rows), dtype))
+        else:
+            out_specs.append(rows_of(width))
+            out_shape.append(jax.ShapeDtypeStruct((n_rows, width), dtype))
     return pl.pallas_call(body, grid=(n_rows // ROWS,), in_specs=in_specs, out_specs=out_specs, out_shape=out_shape, scratch_shapes=list(scratch),
                           compiler_params=pltpu.CompilerParams(vmem_limit_bytes=62 * 1024 * 1024, dimension_semantics=('arbitrary',)), name=name)(*[a for a, _ in ins])
 
@@ -537,27 +661,22 @@
         vecs = jnp.pad(vecs, ((0, VEC_ROWS - vecs.shape[0]), (0, 0)))
 
         bf, f32 = jnp.bfloat16, jnp.float32
-        x_zero, a_in, qkv, ctx, h_mid, c_in = stage_call(
+        x_zero, a_turned, qkv, ctx_turned, h_mid, c_in, c_turned = stage_call(
             stage_one, 'stage_one', n_rows, [(x_in, False), (misc, True), (w_qkv, True), (w_out, True), (vecs, True)],
-            [(1024, f32), (1024, bf), (3072, bf), (1024, bf), (1024, f32), (1024, bf)])
-        gelu, d_pre, h_one, d_mid, d_mid_b, sums_two = stage_call(
+            [(1024, f32), (-1024, bf), (3072, bf), (-1024, bf), (1024, f32), (1024, bf), (-1024, bf)], [pltpu.VMEM((ROWS, 1024), bf)])
+        gelu_turned, d_pre, h_one, d_mid, d_mid_b, sums_two = stage_call(
             stage_two, 'stage_two', n_rows, [(c_in, False), (h_mid, False), (grad_rows, False), (w_fc, True), (w_proj, True), (vecs, True)],
-            [(4096, bf), (4096, bf), (1024, bf), (1024, f32), (1024, bf), (0, None)],
+            [(-4096, bf), (4096, bf), (1024, bf), (1024, f32), (1024, bf), (0, None)],
             [pltpu.VMEM((ROWS, 1024), f32), pltpu.VMEM((ROWS, 1024), f32)])
-        d_qkv, d_emb, sums_three = stage_call(
-            stage_three, 'stage_three', n_rows, [(x_zero, False), (d_mid, False), (d_mid_b, False), (qkv, False), (w_qkv, True), (w_out, True), (vecs, True)],
-            [(3072, bf), (1024, bf), (0, None)],
-            [pltpu.VMEM((ROWS, 1024), bf), pltpu.VMEM((8, 3072), f32)])
         h_one = h_one.reshape(n_img, SEQ, d_model)[:, :n_token]
-        outer = lambda left, right: lax.dot_general(left, right, (((0,), (0,)), ((), ())), preferred_element_type=f32)
+        fc_sum, proj_sum, d_qkv, d_emb, sums_three = mlp_sums(c_turned, d_pre, gelu_turned, grad_rows, w_qkv, w_out, vecs, x_zero, d_mid, d_mid_b, qkv)
         sums = sums_two + sums_three
-        totals = {name: sums[place] for name, place in VEC_AT.items()}
-        totals.update(b_qkv=sums[VEC_QKV:VEC_QKV + 3], b_fc=sums[VEC_FC:VEC_FC + 4])
-        g_vec = jnp.concatenate([totals['cls_tok'].reshape(1024, 1), jnp.zeros((1024, N_POS - 1), f32), vector_columns(totals, 1024)], axis=1)
-        g_misc = outer(d_emb, x_in) + jnp.pad(g_vec, ((0, 0), (N_PIXEL, 0)))
-        reduced = reduce_all((outer(c_in, d_pre), outer(gelu, grad_rows), outer(a_in, d_qkv), outer(ctx, d_mid_b), g_misc))
-        own = unpack_misc(reduced[MISC])
-        own.update(w_fc=reduced[FC], w_proj=reduced[PROJ], w_qkv=reduced[QKV].reshape(n_shard, 3, n_heads, head_dim), w_out=reduced[OUT])
+        vec_rows = jnp.concatenate([sums[:n_vec], sums[VEC_QKV:VEC_QKV + 3].reshape(1024, 3).T, sums[VEC_FC:VEC_FC + 4].reshape(1024, 4).T], axis=0)
+        g_rows = jnp.concatenate([sums[VEC_AT['cls_tok']][None], jnp.zeros((N_POS - 1, 1024), f32), vec_rows], axis=0)
+        g_vec = jnp.pad(g_rows, ((0, 1024 - N_PIXEL - g_rows.shape[0]), (0, 0))).T
+        qkv_sum, out_sum, misc_sum = rest_sums(a_turned, d_qkv, ctx_turned, d_mid_b, d_emb.T, x_in, g_vec)
+        own = unpack_misc(misc_sum)
+        own.update(w_fc=fc_sum, w_proj=proj_sum, w_qkv=qkv_sum.reshape(n_shard, 3, n_heads, head_dim), w_out=out_sum)
         return (h_one,) + tuple(own[name] for name in PARAM_NAMES)
 
     batch_spec = P(MESH_AXIS)

time: 570 us -> 643 us (1.13)
  Pallas kernels: 464 us -> 583 us
  matrix products: 48.9 us -> 5.49 us
    pallas_call x1 -> x2, Pallas kernels: 199 us -> 372 us  [the longest x1 231 us: mlp_sums(): pl.pallas_call(mlp_sums_kernel, out_shape=out_shape, in_specs=[anywhere]...]
    pallas_call x3 -> x2, Pallas kernels: 156 us -> 102 us  [stage_call(): pl.pallas_call(body, grid=(n_rows // ROWS,), in_specs=in_specs, out_specs...]
    dot_general x5 -> x0, matrix products: 43.5 us -> none  [local_step(): lax.dot_general(left, right, (((0,), (0,)), ((), ())), preferred_element_...]
where the time goes in v3:
time: 643 us; the launch traced here: 634 us
  Pallas kernels  583 us (91%)
  local copies, waits for them, and re-layouts  37.1 us (6%)
  other arithmetic  6.79 us (1%)
    pallas_call x1, Pallas kernels, mlp_sums(): pl.pallas_call(mlp_sums_kernel, out_shape=out_shape, in_specs=[anywhere]...  231 us
    pallas_call x1, Pallas kernels, rest_sums(): pl.pallas_call(rest_sums_kernel, out_shape=[jax.ShapeDtypeStruct(ARRAYS[a...  142 us
    pallas_call x1, Pallas kernels, gather_all(): pl.pallas_call(gather_kernel, out_shape=[jax.ShapeDtypeStruct((2 * N_CHIP...  109 us
    pallas_call x2, Pallas kernels, stage_call(): pl.pallas_call(body, grid=(n_rows // ROWS,), in_specs=in_specs, out_specs...  102 us

profile of v3, /device:TPU:0, one launch (start us, length us, event | category | flops | bytes accessed | tf_op | source)
XLA Modules:
  0.0 633.6 jit_solution(14442095539508945029)
XLA Ops:
  0.8 1.3 convert_element_type.76
  2.1 1.0 reshape.114.refs_2_
  3.1 0.7 convert_element_type.74.refs_0_
  3.8 0.7 convert_element_type.75.refs_1_
  5.9 0.1 concatenate.16
  6.1 0.7 fusion.10.refs_4_
  6.8 0.6 convert_element_type.77.refs_3_
  7.4 108.9 %gather_all.1 = (bf16[1024,4096]{1,0:T(8,128)(2,1)}, bf16[4096,1024]{1,0:T(8,128)(2,1)}, bf16[1024,3072]{1,0:T(8,128)(2,1)}, bf16[1024,1024]{1,0:T(8,128)(2,1)}, bf16[1024,1024]{1,0:T(8,128)(2,1)}) custom-call(bf16[32,4096]{1,0:T(8,128)(2,1)} %convert_element_type.74.refs_0_, bf16[128,1024]{1,0:T(8,128)(2,1)} %convert_element_type.75.refs_1_, ...), custom_call_target="tpu_custom_call" | custom-call | tf_op jit(solution)/shard_map/gather_all/pallas_call | solution.py:138
  116.3 2.9 copy.72
  119.2 0.2 copy.73
  119.4 0.4 reshape.127
  119.8 0.2 copy.74
  120.0 0.3 reshape.128
  120.4 0.7 select_maximum_fusion.vecs.refs_6_
  121.1 5.5 fusion.2
  126.6 0.2 fusion.5
  126.8 1.6 pad_maximum_fusion
  128.4 50.7 %stage_one.1 = (f32[1024,1024]{1,0:T(8,128)}, bf16[1024,1024]{1,0:T(8,128)(2,1)}, bf16[1024,3072]{1,0:T(8,128)(2,1)}, bf16[1024,1024]{1,0:T(8,128)(2,1)}, f32[10...) custom-call(bf16[1024,1024]{1,0:T(8,128)(2,1)} %bitcast.43, ...), custom_call_target="tpu_custom_call" | custom-call | tf_op jit(solution)/shard_map/stage_one/pallas_call | solution.py:612
  179.1 0.9 copy.83
  180.0 1.6 pad.28.clone
  181.6 51.0 %stage_two.1 = (bf16[4096,1024]{1,0:T(8,128)(2,1)}, bf16[1024,4096]{1,0:T(8,128)(2,1)}, bf16[1024,1024]{1,0:T(8,128)(2,1)}, f32[1024,1024]{1,0:T(8,128)}, bf16[1...) custom-call(bf16[1024,1024]{1,0:T(8,128)(2,1)} %get-tuple-element.48.c_in, f32[1024,1024]{1,0:T(8,128)} %get-tuple-element.49.h_mid, ...), custom_call_target="tpu_custom_call" | custom-call | tf_op jit(solution)/shard_map/stage_two/pallas_call | solution.py:612
  232.6 230.9 %mlp_sums.1 = (f32[32,4096]{1,0:T(8,128)}, f32[128,1024]{1,0:T(8,128)}, bf16[1024,3072]{1,0:T(8,128)(2,1)}, bf16[1024,1024]{1,0:T(8,128)(2,1)}, f32[24,1024]{1,0:T(8,128)}) custom-call(bf16[1024,1024]{1,0:T(8,128)(2,1)} %get-tuple-element.54.refs_0_, bf16[1024,4096]{1,0:T(8,128)(2,1)} %get-tuple-element.55.refs_1_, ...), custom_call_target="tpu_custom_call" | custom-call | tf_op jit(solution)/shard_map/mlp_sums/pallas_call | solution.py:544
  463.5 1.1 copy.79
  464.6 0.2 copy.78
  464.9 0.2 slice.99
  465.1 0.2 copy.80
  465.3 0.4 reshape.131
  465.7 0.2 slice.100
  465.9 0.2 copy.81
  466.1 1.4 reshape.132
  467.4 1.0 slice.97
  468.5 2.0 concatenate.19
  470.5 1.0 pad_bitcast_fusion.refs_6_
  471.5 4.3 copy.77
  475.9 141.5 %rest_sums.1 = (f32[32,3072]{1,0:T(8,128)}, f32[32,1024]{1,0:T(8,128)}, f32[32,1024]{1,0:T(8,128)}) custom-call(bf16[1024,1024]{1,0:T(8,128)(2,1)} %get-tuple-element.53.refs_0_, bf16[1024,3072]{1,0:T(8,128)(2,1)} %get-tuple-element.61.refs_1_, bf16[1024,1024]{1,0:T(8,128)(2,1)} %get-tuple-element.62.refs_2_, ...), custom_call_target="tpu_custom_call" | custom-call | tf_op jit(solution)/shard_map/rest_sums/pallas_call | solution.py:583
  617.4 2.1 reshape.133
  619.5 1.5 slice_bitcast_fusion
  621.0 1.4 slice_bitcast_fusion.2
  622.4 0.8 slice.86
  623.2 0.6 reshape.134
  623.8 0.8 slice.90
  624.6 0.6 reshape.135
  625.2 2.3 slice_reduce_fusion
  627.5 1.6 slice.96
  629.2 2.1 copy.82
  631.2 0.7 copy.91
  631.9 0.8 copy.92
  632.7 0.8 copy.93
  (81 shorter events, 1.6 us)
Async XLA Ops:
  0.7 2.4 copy-start.1
  0.7 3.1 copy-start.2
  0.7 3.9 copy-start.11
  0.7 4.0 copy-start.12
  0.7 4.1 copy-start.13
  0.7 4.2 copy-start.14
  0.7 4.3 copy-start.15
  0.7 4.4 copy-start.16
  0.7 4.5 copy-start.17
  0.8 4.6 copy-start.18
  0.8 4.7 copy-start.19
  0.8 4.8 copy-start.20
  0.8 4.9 copy-start.21
  0.8 5.0 copy-start.22
  0.8 5.2 copy-start.8
  0.8 5.3 copy-start.9
  0.8 6.0 copy-start.5
  119.2 1.9 copy-start.10
  128.4 50.7 %copy-start = (bf16[16,50,1024]{2,0,1:T(8,128)(2,1)S(1)}, bf16[16,50,1024]{2,0,1:T(8,128)(2,1)}, u32[]{:S(2)}) copy-start(bf16[16,50,1024]{2,0,1:T(8,128)(2,1)} %param.41) | copy-start | bytes 4915204
  232.6 232.0 %copy-start.7 = (f32[24,1024]{1,0:T(8,128)S(1)}, f32[24,1024]{1,0:T(8,128)}, u32[]{:S(2)}) copy-start(f32[24,1024]{1,0:T(8,128)} %get-tuple-element.64) | copy-start | bytes 294916
  629.1 2.1 copy-start.6
  629.1 2.7 copy-start.4
  629.1 3.5 copy-start.3

commit v4 on v3

--- a/solution.py
+++ b/solution.py
@@ -25,11 +25,13 @@
 MESH_ID = pl.DeviceIdType.MESH
 ARRAYS = ((32, 4096), (128, 1024), (32, 3072), (32, 1024), (32, 1024))
 FC, PROJ, QKV, OUT, MISC = range(5)
-GATHER_STREAMS = (
-    (MISC, 0, 32, 0, 256, 0), (MISC, 0, 32, 256, 256, 1), (MISC, 0, 32, 512, 256, 2), (MISC, 0, 32, 768, 256, 3),
-    (QKV, 0, 32, 0, 2048, 4), (QKV, 0, 32, 2048, 1024, 5), (OUT, 0, 32, 0, 1024, 5),
-    (FC, 0, 32, 0, 2048, 0), (FC, 0, 32, 2048, 2048, 1), (PROJ, 0, 64, 0, 1024, 2), (PROJ, 64, 64, 0, 1024, 3),
-)
+FIRST_STREAMS = tuple((QKV, 0, 32, 512 * k, 512, k) for k in range(6)) + (
+    (OUT, 0, 32, 0, 384, 0), (OUT, 0, 32, 384, 384, 1), (OUT, 0, 32, 768, 256, 4),
+    (MISC, 0, 32, 0, 384, 2), (MISC, 0, 32, 384, 384, 3), (MISC, 0, 32, 768, 256, 5))
+SECOND_STREAMS = (
+    (FC, 0, 32, 0, 896, 0), (FC, 0, 32, 896, 896, 1), (FC, 0, 32, 1792, 384, 2), (FC, 0, 32, 2176, 384, 3),
+    (FC, 0, 32, 2560, 768, 4), (FC, 0, 32, 3328, 768, 5), (PROJ, 0, 128, 0, 128, 0), (PROJ, 0, 128, 128, 128, 1),
+    (PROJ, 0, 128, 256, 256, 2), (PROJ, 0, 128, 512, 256, 3), (PROJ, 0, 128, 768, 128, 4), (PROJ, 0, 128, 896, 128, 5))
 MLP_STREAMS = tuple((FC, 0, 64, 384 * k, 384, k) for k in range(4)) + ((FC, 0, 64, 1536, 256, 4), (FC, 0, 64, 1792, 256, 5)) + tuple(
     (PROJ, 128 * (place % 2), 128, 128 * (place // 2), 128, ring) for place, ring in enumerate((0, 1, 2, 3, 4, 5, 4, 5)))
 REST_STREAMS = tuple((QKV, 0, 64, 256 * k, 256, k) for k in range(6)) + tuple((OUT, 0, 64, 128 * k, 128, k) for k in range(4)) + (
@@ -67,82 +69,102 @@
         pl.semaphore_wait(barrier, 2 * len(RINGS) + 1)
 
 
-def gather_kernel(*refs):
-    shards, wholes = refs[:5], refs[5:10]
-    own_sem, send_sem, recv_sem, twin_send, twin_recv = refs[10:]
+class RingGather:
+    def __init__(self, place, arrays, streams, shards, wholes, sems):
+        self.place, self.arrays, self.streams = place, arrays, streams
+        self.shards, self.wholes = dict(zip(arrays, shards)), dict(zip(arrays, wholes))
+        self.own_sem, self.send_sem, self.recv_sem, self.twin_send, self.twin_recv = sems
+
+    def block(self, i, chip, core):
+        arr, row, rows, col, cols, _ = self.streams[i]
+        first = (2 * chip + core) * ARRAYS[arr][0] + row
+        return self.wholes[arr].at[pl.ds(pl.multiple_of(first, 32), rows), pl.ds(col, cols)]
+
+    def ring_copy(self, i, src, dst, step):
+        return pltpu.make_async_remote_copy(src_ref=src, dst_ref=dst, send_sem=self.send_sem.at[i, step], recv_sem=self.recv_sem.at[i, step],
+                                            device_id=(self.place.after[self.streams[i][5]],), device_id_type=MESH_ID)
+
+    def twin_copy(self, i, src, dst, step):
+        return pltpu.make_async_remote_copy(src_ref=src, dst_ref=dst, send_sem=self.twin_send.at[i, step], recv_sem=self.twin_recv.at[i, step],
+                                            device_id=(self.place.sibling,), device_id_type=MESH_ID)
+
+    def own_copies(self):
+        for place, arr in enumerate(self.arrays):
+            rows = ARRAYS[arr][0]
+            first = pl.multiple_of((2 * self.place.chip + self.place.core) * rows, 32)
+            yield pltpu.make_async_copy(self.shards[arr], self.wholes[arr].at[pl.ds(first, rows), :], self.own_sem.at[place])
+
+    def run(self, hook):
+        place = self.place
+        for i in range(len(self.streams)):
+            arr, row, rows, col, cols, _ = self.streams[i]
+            mine = self.shards[arr].at[pl.ds(row, rows), pl.ds(col, cols)]
+            here = self.block(i, place.chip, place.core)
+            self.ring_copy(i, mine, here, 0).start()
+            self.twin_copy(i, mine, here, 0).start()
+        for copy in self.own_copies():
+            copy.start()
+        hook(jnp.int32(0))
+
+        def ring_step(step, carry):
+            chips = place.chips_back(step)
+            for i in range(len(self.streams)):
+                here = self.block(i, chips[self.streams[i][5]], place.core)
+                self.ring_copy(i, here, here, step - 1).wait_recv()
+
+                @pl.when(step < N_CHIP - 1)
+                def _():
+                    self.ring_copy(i, here, here, step).start()
+
+                self.twin_copy(i, here, here, step).start()
+            hook(step)
+            return carry
+
+        lax.fori_loop(1, N_CHIP, ring_step, 0)
+
+        def drain(step, carry):
+            chips = place.chips_back(step)
+            for i in range(len(self.streams)):
+                k = self.streams[i][5]
+                here, there = self.block(i, chips[k], place.core), self.block(i, chips[k], 1 - place.core)
+
+                @pl.when(step < N_CHIP - 1)
+                def _():
+                    self.ring_copy(i, here, here, step).wait_send()
+
+                self.twin_copy(i, here, here, step).wait_send()
+                self.twin_copy(i, there, there, step).wait_recv()
+            return carry
+
+        lax.fori_loop(0, N_CHIP, drain, 0)
+        for copy in self.own_copies():
+            copy.wait()
+
+
+def gather_sems(arrays, streams):
+    ring, twin = pltpu.SemaphoreType.DMA((len(streams), N_CHIP - 1)), pltpu.SemaphoreType.DMA((len(streams), N_CHIP))
+    return [pltpu.SemaphoreType.DMA((len(arrays),)), ring, ring, twin, twin]
+
+
+def gathered_shapes(arrays):
+    return [jax.ShapeDtypeStruct((2 * N_CHIP * ARRAYS[arr][0], ARRAYS[arr][1]), jnp.bfloat16) for arr in arrays]
+
+
+FIRST_ARRAYS, SECOND_ARRAYS = (QKV, OUT, MISC), (FC, PROJ)
+
+
+def gather_first_kernel(*refs):
     place = Place()
-
-    def block(i, chip, core):
-        arr, row, rows, col, cols, _ = GATHER_STREAMS[i]
-        first = (2 * chip + core) * ARRAYS[arr][0] + row
-        return wholes[arr].at[pl.ds(pl.multiple_of(first, 32), rows), pl.ds(col, cols)]
-
-    def remote(src, dst, sems, i, step, device):
-        return pltpu.make_async_remote_copy(src_ref=src, dst_ref=dst, send_sem=sems[0].at[i, step], recv_sem=sems[1].at[i, step],
-                                            device_id=(device,), device_id_type=MESH_ID)
-
     place.meet()
-    n_streams = len(GATHER_STREAMS)
-    for i in range(n_streams):
-        arr, row, rows, col, cols, k = GATHER_STREAMS[i]
-        mine = shards[arr].at[pl.ds(row, rows), pl.ds(col, cols)]
-        here = block(i, place.chip, place.core)
-        remote(mine, here, (send_sem, recv_sem), i, 0, place.after[k]).start()
-        remote(mine, here, (twin_send, twin_recv), i, 0, place.sibling).start()
-    for arr in range(5):
-        rows = ARRAYS[arr][0]
-        first = pl.multiple_of((2 * place.chip + place.core) * rows, 32)
-        pltpu.make_async_copy(shards[arr], wholes[arr].at[pl.ds(first, rows), :], own_sem.at[arr]).start()
-
-    def ring_step(step, carry):
-        chips = place.chips_back(step)
-        for i in range(n_streams):
-            k = GATHER_STREAMS[i][5]
-            here = block(i, chips[k], place.core)
-            remote(here, here, (send_sem, recv_sem), i, step - 1, place.after[k]).wait_recv()
-
-            @pl.when(step < N_CHIP - 1)
-            def _():
-                remote(here, here, (send_sem, recv_sem), i, step, place.after[k]).start()
-
-            remote(here, here, (twin_send, twin_recv), i, step, place.sibling).start()
-        return carry
-
-    lax.fori_loop(1, N_CHIP, ring_step, 0)
-
-    def drain(step, carry):
-        chips = place.chips_back(step)
-        for i in range(n_streams):
-            k = GATHER_STREAMS[i][5]
-            here = block(i, chips[k], place.core)
-            there = block(i, chips[k], 1 - place.core)
-
-            @pl.when(step < N_CHIP - 1)
-            def _():
-                remote(here, here, (send_sem, recv_sem), i, step, place.after[k]).wait_send()
-
-            remote(here, here, (twin_send, twin_recv), i, step, place.sibling).wait_send()
-            remote(there, there, (twin_send, twin_recv), i, step, place.sibling).wait_recv()
-        return carry
-
-    lax.fori_loop(0, N_CHIP, drain, 0)
-    for arr in range(5):
-        rows = ARRAYS[arr][0]
-        first = pl.multiple_of((2 * place.chip + place.core) * rows, 32)
-        pltpu.make_async_copy(shards[arr], wholes[arr].at[pl.ds(first, rows), :], own_sem.at[arr]).wait()
-
-
-def gather_all(shards):
-    n_streams = len(GATHER_STREAMS)
-    ring_sems, twin_sems = pltpu.SemaphoreType.DMA((n_streams, N_CHIP - 1)), pltpu.SemaphoreType.DMA((n_streams, N_CHIP))
+    RingGather(place, FIRST_ARRAYS, FIRST_STREAMS, refs[:3], refs[3:6], refs[6:]).run(lambda step: None)
+
+
+def gather_first(shards):
     return pl.pallas_call(
-        gather_kernel,
-        out_shape=[jax.ShapeDtypeStruct((2 * N_CHIP * rows, cols), jnp.bfloat16) for rows, cols in ARRAYS],
-        in_specs=[pl.BlockSpec(memory_space=pltpu.VMEM)] * 5,
-        out_specs=[pl.BlockSpec(memory_space=pl.ANY)] * 5,
-        scratch_shapes=[pltpu.SemaphoreType.DMA((5,)), ring_sems, ring_sems, twin_sems, twin_sems],
-        compiler_params=pltpu.CompilerParams(collective_id=0, has_side_effects=True),
-        name='gather_all',
+        gather_first_kernel, out_shape=gathered_shapes(FIRST_ARRAYS),
+        in_specs=[pl.BlockSpec(memory_space=pltpu.VMEM)] * 3, out_specs=[pl.BlockSpec(memory_space=pl.ANY)] * 3,
+        scratch_shapes=gather_sems(FIRST_ARRAYS, FIRST_STREAMS),
+        compiler_params=pltpu.CompilerParams(collective_id=0, has_side_effects=True), name='gather_first',
     )(*shards)
 
 
@@ -159,8 +181,8 @@
 
     def push(self, i, slot):
         arr = self.streams[i][0]
-        return pltpu.make_async_remote_copy(src_ref=self.part(i, self.gives[arr]), dst_ref=self.part(i, self.twins[arr], slot),
-                                            send_sem=self.twin_send.at[i], recv_sem=self.twin_recv.at[i, slot],
+        return pltpu.make_async_remote_copy(src_ref=self.part(i, self.gives[arr], slot), dst_ref=self.part(i, self.twins[arr], slot),
+                                            send_sem=self.twin_send.at[i, slot], recv_sem=self.twin_recv.at[i, slot],
                                             device_id=(self.place.sibling,), device_id_type=MESH_ID)
 
     def pass_on(self, i, slot, slot_next):
@@ -169,20 +191,27 @@
                                             send_sem=self.send_sem.at[i, slot], recv_sem=self.recv_sem.at[i, slot_next],
                                             device_id=(self.place.after[k],), device_id_type=MESH_ID)
 
-    def compute(self, group, step, first):
+    def make_own(self, group, step):
         chips = self.place.chips_back(step + 1)
-        slot = lax.rem(jnp.int32(step), 2)
         for i in group:
             arr, k = self.streams[i][0], self.streams[i][5]
-            if not first:
-                self.push(i, slot).wait_send()
-            self.part(i, self.gives[arr])[...] = self.term(i, chips[k], 1 - self.place.core)
-            if not first:
-                @pl.when(step >= 2)
-                def _():
-                    pl.semaphore_wait(self.twin_free.at[i], 1)
-            self.push(i, slot).start()
             self.part(i, self.owns[arr])[...] = self.term(i, chips[k], self.place.core)
+
+    def make_give(self, group, step):
+        chips, slot = self.place.chips_back(step + 1), lax.rem(jnp.int32(step), 2)
+        for i in group:
+            arr, k = self.streams[i][0], self.streams[i][5]
+            self.part(i, self.gives[arr], slot)[...] = self.term(i, chips[k], 1 - self.place.core)
+
+    def push_next(self, group, step):
+        slot, slot_next = lax.rem(step, 2), lax.rem(step + 1, 2)
+        for i in group:
+            self.push(i, slot).wait_send()
+
+            @pl.when(step >= 1)
+            def _():
+                pl.semaphore_wait(self.twin_free.at[i], 1)
+            self.push(i, slot_next).start()
 
     def advance(self, group, step):
         slot, slot_next, slot_last, pair = lax.rem(step, 3), lax.rem(step + 1, 3), lax.rem(step + 2, 3), lax.rem(step, 2)
@@ -225,7 +254,11 @@
 
     def run(self, groups, hook):
         for group in groups:
-            self.compute(group, 0, True)
+            self.make_give(group, 0)
+            for i in group:
+                self.push(i, 0).start()
+            self.make_own(group, 0)
+            self.make_give(group, 1)
 
         def ring_step(step, carry):
             for place, group in enumerate(groups):
@@ -233,7 +266,12 @@
 
                 @pl.when(step < N_CHIP - 1)
                 def _():
-                    self.compute(group, step + 1, False)
+                    self.push_next(group, step)
+                    self.make_own(group, step + 1)
+
+                @pl.when(step < N_CHIP - 2)
+                def _():
+                    self.make_give(group, step + 2)
 
                 hook(place, step)
             return carry
@@ -261,9 +299,9 @@
 
 def ring_scratch(arrays, streams):
     shapes = [(2 * ARRAYS[arr][0], ARRAYS[arr][1] // 2) for arr in arrays]
-    buffers = [pltpu.VMEM((*lead, *shape), jnp.float32) for lead in ((3,), (), (), (2,)) for shape in shapes]
+    buffers = [pltpu.VMEM((*lead, *shape), jnp.float32) for lead in ((3,), (), (2,), (2,)) for shape in shapes]
     dma, regular, n = pltpu.SemaphoreType.DMA, pltpu.SemaphoreType.REGULAR, len(streams)
-    return buffers + [dma((n,)), dma((n, 2)), dma((n, 3)), dma((n, 3)), regular((n,)), regular((n,))] + [dma((len(arrays),))] * 3
+    return buffers + [dma((n, 2)), dma((n, 2)), dma((n, 3)), dma((n, 3)), regular((n,)), regular((n,))] + [dma((len(arrays),))] * 3
 
 
 def split_scratch(refs, n_arrays):
@@ -355,33 +393,102 @@
     return lax.broadcasted_iota(jnp.int32, (rows, 1), 0) % SEQ == 0
 
 
-def stage_one(x_in, misc, w_qkv, w_out, vecs, x_zero, a_turned, qkv, ctx_turned, h_mid, c_out, c_turned, ctx):
-    start = jnp.where(is_cls(ROWS), row_of(vecs, 'cls_tok'), row_of(vecs, 'b_patch'))
-    x_sum = dot_nt(x_in[...], misc[...]) + start
-    x_zero[...] = x_sum
-    h_zero = normalize(x_sum)[0] * row_of(vecs, 'lnp_g') + row_of(vecs, 'lnp_b')
-    a_in = (normalize(h_zero)[0] * row_of(vecs, 'ln1_g') + row_of(vecs, 'ln1_b')).astype(jnp.bfloat16)
-    a_turned[...] = a_in.T
-    for s in range(3):
-        cols = pl.ds(1024 * s, 1024)
-        qkv[:, cols] = (dot_nn(a_in, w_qkv[:, cols]) + vecs[VEC_QKV + s:VEC_QKV + s + 1, :]).astype(jnp.bfloat16)
-
-    def image(b, carry):
-        rows = pl.ds(pl.multiple_of(b * SEQ, SEQ), SEQ)
-        for g in range(4):
-            q_block, k_block, v_block = [qkv[rows, pl.ds(1024 * s + HEAD_GROUP * g, HEAD_GROUP)] for s in range(3)]
-            prob = probabilities(q_block, stack_heads(k_block)).astype(jnp.bfloat16)
-            ctx[rows, pl.ds(HEAD_GROUP * g, HEAD_GROUP)] = dot_nn(prob, stack_heads(v_block)).astype(jnp.bfloat16)
-        return carry
-
-    lax.fori_loop(0, ROWS // SEQ, image, 0)
-    context = ctx[...]
-    ctx_turned[...] = context.T
-    mid = h_zero + dot_nn(context, w_out[...]) + row_of(vecs, 'b_out')
-    h_mid[...] = mid
-    c_in = (normalize(mid)[0] * row_of(vecs, 'ln2_g') + row_of(vecs, 'ln2_b')).astype(jnp.bfloat16)
-    c_out[...] = c_in
-    c_turned[...] = c_in.T
+PAIR = 2 * SEQ
+
+
+def gather_second_kernel(*refs):
+    fc_shard, proj_shard, in_hbm, misc_hbm, qkv_w_hbm, out_w_hbm, vecs = refs[:7]
+    fc_whole, proj_whole = refs[7:9]
+    results = refs[9:16]
+    x_in, misc, w_qkv, w_out, h_zero, ctx = refs[16:22]
+    buffers = refs[22:29]
+    x_zero, a_turned, qkv, ctx_turned, h_mid, c_out, c_turned = buffers
+    load_sem, out_sem = refs[29:31]
+    place = Place()
+    loads = [pltpu.make_async_copy(src, dst, load_sem.at[n]) for n, (src, dst) in enumerate(
+        ((in_hbm, x_in), (misc_hbm, misc), (qkv_w_hbm, w_qkv), (out_w_hbm, w_out)))]
+    for load in loads:
+        load.start()
+    place.meet()
+
+    def pair_out(p, slot):
+        span = pl.ds(pl.multiple_of(p * PAIR, PAIR), PAIR)
+        for n, (src, dst) in enumerate(zip(buffers, results)):
+            target = dst.at[:, span] if n in (1, 3, 6) else dst.at[span, :]
+            yield pltpu.make_async_copy(src.at[slot], target, out_sem.at[n, slot])
+
+    def enter(p, slot):
+        rows = pl.ds(pl.multiple_of(p * PAIR, PAIR), PAIR)
+        start = jnp.where(is_cls(PAIR), row_of(vecs, 'cls_tok'), row_of(vecs, 'b_patch'))
+        x_sum = dot_nt(x_in[rows, :], misc[...]) + start
+        x_zero[slot] = x_sum
+        h_sum = normalize(x_sum)[0] * row_of(vecs, 'lnp_g') + row_of(vecs, 'lnp_b')
+        h_zero[...] = h_sum
+        a_in = (normalize(h_sum)[0] * row_of(vecs, 'ln1_g') + row_of(vecs, 'ln1_b')).astype(jnp.bfloat16)
+        a_turned[slot] = a_in.T
+        for s in range(3):
+            cols = pl.ds(1024 * s, 1024)
+            qkv[slot, :, cols] = (dot_nn(a_in, w_qkv[:, cols]) + vecs[VEC_QKV + s:VEC_QKV + s + 1, :]).astype(jnp.bfloat16)
+
+    def attend(slot):
+        for b in range(2):
+            rows = pl.ds(b * SEQ, SEQ)
+            for g in range(4):
+                q_block, k_block, v_block = [qkv[slot, rows, pl.ds(1024 * s + HEAD_GROUP * g, HEAD_GROUP)] for s in range(3)]
+                prob = probabilities(q_block, stack_heads(k_block)).astype(jnp.bfloat16)
+                ctx[rows, pl.ds(HEAD_GROUP * g, HEAD_GROUP)] = dot_nn(prob, stack_heads(v_block)).astype(jnp.bfloat16)
+        context = ctx[...]
+        ctx_turned[slot] = context.T
+        mid = h_zero[...] + dot_nn(context, w_out[...]) + row_of(vecs, 'b_out')
+        h_mid[slot] = mid
+        c_in = (normalize(mid)[0] * row_of(vecs, 'ln2_g') + row_of(vecs, 'ln2_b')).astype(jnp.bfloat16)
+        c_out[slot] = c_in
+        c_turned[slot] = c_in.T
+
+    def hook(step):
+        p = lax.div(step, 2)
+        slot = lax.rem(p, 2)
+
+        @pl.when(step == 0)
+        def _():
+            for load in loads:
+                load.wait()
+
+        @pl.when(lax.rem(step, 2) == 0)
+        def _():
+            @pl.when(p >= 2)
+            def _():
+                for copy in pair_out(p - 2, slot):
+                    copy.wait()
+            enter(p, slot)
+
+        @pl.when(lax.rem(step, 2) == 1)
+        def _():
+            attend(slot)
+            for copy in pair_out(p, slot):
+                copy.start()
+
+    RingGather(place, SECOND_ARRAYS, SECOND_STREAMS, (fc_shard, proj_shard), (fc_whole, proj_whole), refs[31:]).run(hook)
+    for p in (N_CHIP // 2 - 2, N_CHIP // 2 - 1):
+        for copy in pair_out(p, p % 2):
+            copy.wait()
+
+
+def gather_second(fc_shard, proj_shard, x_in, misc, w_qkv, w_out, vecs):
+    bf, f32, dma = jnp.bfloat16, jnp.float32, pltpu.SemaphoreType.DMA
+    n_rows = x_in.shape[0]
+    assert n_rows // SEQ == N_CHIP
+    anywhere, vmem = pl.BlockSpec(memory_space=pl.ANY), pl.BlockSpec(memory_space=pltpu.VMEM)
+    kinds = ((1024, f32), (-1024, bf), (3072, bf), (-1024, bf), (1024, f32), (1024, bf), (-1024, bf))
+    out_shape = gathered_shapes(SECOND_ARRAYS) + [jax.ShapeDtypeStruct((n_rows, width) if width > 0 else (-width, n_rows), dtype) for width, dtype in kinds]
+    scratch = [pltpu.VMEM(a.shape, bf) for a in (x_in, misc, w_qkv, w_out)] + [pltpu.VMEM((PAIR, 1024), f32), pltpu.VMEM((PAIR, 1024), bf)]
+    scratch += [pltpu.VMEM((2, PAIR, width) if width > 0 else (2, -width, PAIR), dtype) for width, dtype in kinds]
+    scratch += [dma((4,)), dma((7, 2))]
+    return pl.pallas_call(
+        gather_second_kernel, out_shape=out_shape, in_specs=[vmem, vmem] + [anywhere] * 4 + [vmem], out_specs=[anywhere] * len(out_shape),
+        scratch_shapes=scratch + gather_sems(SECOND_ARRAYS, SECOND_STREAMS),
+        compiler_params=pltpu.CompilerParams(collective_id=3, has_side_effects=True, vmem_limit_bytes=62 * 1024 * 1024), name='gather_second',
+    )(fc_shard, proj_shard, x_in, misc, w_qkv, w_out, vecs)
 
 
 def add_row(sums, place, value):
@@ -646,7 +753,7 @@
         n_shard, _, n_heads, head_dim = shards['w_qkv'].shape
         n_rows = n_img * SEQ
         casts = {name: shards[name].astype(jnp.bfloat16) for name in PARAM_NAMES}
-        w_fc, w_proj, w_qkv, w_out, misc = gather_all((casts['w_fc'], casts['w_proj'], casts['w_qkv'].reshape(n_shard, -1), casts['w_out'], pack_misc(casts)))
+        w_qkv, w_out, misc = gather_first((casts['w_qkv'].reshape(n_shard, -1), casts['w_out'], pack_misc(casts)))
         position = jnp.pad(keep + 1, ((0, 0), (1, 0)))
         position = jnp.pad(position, ((0, 0), (0, SEQ - n_token)), constant_values=-1)[:, :, None]
         onehot_patch = (position == 1 + lax.broadcasted_iota(jnp.int32, (1, 1, n_patch), 2)).astype(jnp.bfloat16)
@@ -661,9 +768,7 @@
         vecs = jnp.pad(vecs, ((0, VEC_ROWS - vecs.shape[0]), (0, 0)))
 
         bf, f32 = jnp.bfloat16, jnp.float32
-        x_zero, a_turned, qkv, ctx_turned, h_mid, c_in, c_turned = stage_call(
-            stage_one, 'stage_one', n_rows, [(x_in, False), (misc, True), (w_qkv, True), (w_out, True), (vecs, True)],
-            [(1024, f32), (-1024, bf), (3072, bf), (-1024, bf), (1024, f32), (1024, bf), (-1024, bf)], [pltpu.VMEM((ROWS, 1024), bf)])
+        w_fc, w_proj, x_zero, a_turned, qkv, ctx_turned, h_mid, c_in, c_turned = gather_second(casts['w_fc'], casts['w_proj'], x_in, misc, w_qkv, w_out, vecs)
         gelu_turned, d_pre, h_one, d_mid, d_mid_b, sums_two = stage_call(
             stage_two, 'stage_two', n_rows, [(c_in, False), (h_mid, False), (grad_rows, False), (w_fc, True), (w_proj, True), (vecs, True)],
             [(-4096, bf), (4096, bf), (1024, bf), (1024, f32), (1024, bf), (0, None)],

time: 643 us -> 523 us (0.81)
  Pallas kernels: 583 us -> 456 us
  other arithmetic: 6.79 us -> 15.5 us
    pallas_call x1, Pallas kernels: 231 us -> 164 us  [mlp_sums(): pl.pallas_call(mlp_sums_kernel, out_shape=out_shape, in_specs=[anywhere]...]
    pallas_call x1, Pallas kernels: 142 us -> 89.4 us  [rest_sums(): pl.pallas_call(rest_sums_kernel, out_shape=[jax.ShapeDtypeStruct(ARRAYS[a...]
    pallas_call x2 -> x1, Pallas kernels: 102 us -> 51.2 us  [stage_call(): pl.pallas_call(body, grid=(n_rows // ROWS,), in_specs=in_specs, out_specs...]
    pallas_call x1 -> x2, Pallas kernels: 109 us -> 152 us  [the longest x1 89.4 us: gather_second(): pl.pallas_call(gather_second_kernel, out_shape=out_shape, in_specs=[vmem,...]
    reshape x10, other arithmetic: 0.03 us -> 6.59 us  [vector_columns(): part[name].reshape(rows, 1)]
where the time goes in v4:
time: 523 us; the launch traced here: 515 us
  Pallas kernels  456 us (87%)
  local copies, waits for them, and re-layouts  36.7 us (7%)
  other arithmetic  15.5 us (3%)
  matrix products  5.48 us (1%)
    pallas_call x1, Pallas kernels, mlp_sums(): pl.pallas_call(mlp_sums_kernel, out_shape=out_shape, in_specs=[anywhere]...  164 us
    pallas_call x1, Pallas kernels, rest_sums(): pl.pallas_call(rest_sums_kernel, out_shape=[jax.ShapeDtypeStruct(ARRAYS[a...  89.4 us
    pallas_call x1, Pallas kernels, gather_second(): pl.pallas_call(gather_second_kernel, out_shape=out_shape, in_specs=[vmem,...  89.4 us
    pallas_call x1, Pallas kernels, gather_first(): pl.pallas_call(gather_first_kernel, out_shape=gathered_shapes(FIRST_ARRAY...  62.6 us
    pallas_call x1, Pallas kernels, stage_call(): pl.pallas_call(body, grid=(n_rows // ROWS,), in_specs=in_specs, out_specs...  51.2 us

profile of v4, /device:TPU:0, one launch (start us, length us, event | category | flops | bytes accessed | tf_op | source)
XLA Modules:
  0.0 515.4 jit_solution(4640411566379421560)
XLA Ops:
  0.7 1.2 convert_element_type.76
  1.9 1.0 reshape.114.refs_0_
  2.9 0.7 convert_bitcast_fusion.11
  3.6 0.7 convert_bitcast_fusion.10
  4.4 0.7 convert_bitcast_fusion.9
  5.1 0.7 convert_bitcast_fusion.8
  5.9 0.7 convert_bitcast_fusion.7
  6.7 0.7 convert_bitcast_fusion.6
  7.4 0.7 convert_bitcast_fusion.5
  8.2 0.7 convert_bitcast_fusion.4
  9.0 0.7 convert_bitcast_fusion.3
  9.7 0.7 convert_bitcast_fusion.2
  10.5 0.7 convert_element_type.90
  11.3 0.7 convert_element_type.91
  12.2 0.9 convert_bitcast_fusion
  13.1 0.7 fusion.10.refs_2_
  13.8 0.6 convert_element_type.77.refs_1_
  14.4 62.6 %gather_first.1 = (bf16[1024,3072]{1,0:T(8,128)(2,1)}, bf16[1024,1024]{1,0:T(8,128)(2,1)}, bf16[1024,1024]{1,0:T(8,128)(2,1)}) custom-call(bf16[32,3072]{1,0:T(8,128)(2,1)} %reshape.114.refs_0_, bf16[32,1024]{1,0:T(8,128)(2,1)} %convert_element_type.77.refs_1_, bf16[32,1024]{1,0:T(8,128)(2,1)} %fusion.10.refs_2_), custom_call_target="tpu_custom_call" | custom-call | tf_op jit(solution)/shard_map/gather_first/pallas_call | solution.py:163
  77.1 2.9 copy.72
  81.1 0.7 select_maximum_fusion.refs_6_.vecs
  81.9 5.5 %fusion.2 = bf16[16,64,768]{2,1,0:T(8,128)(2,1)S(1)} fusion(bf16[16,196,768]{2,0,1:T(8,128)(2,1)} %param.21, s32[196]{0:T(256)S(1)} %iota_add_fusion, s32[16,64]{1,0:T(8,128)S(1)} %pad_select_fusion), kind=kOutput, calls=%fused_computation.3 | convolution fusion | flops 309268480 | bytes 6394640 | tf_op jit(solution)/shard_map/bkp,bpq->bkq/dot_general | solution.py:761
  87.6 1.6 pad_maximum_fusion
  89.2 0.7 convert_element_type.72.refs_0_
  90.0 0.7 convert_element_type.73.refs_1_
  90.7 89.4 %gather_second.1 = (bf16[1024,4096]{1,0:T(8,128)(2,1)}, bf16[4096,1024]{1,0:T(8,128)(2,1)}, f32[1024,1024]{1,0:T(8,128)}, bf16[1024,1024]{1,0:T(8,128)(2,1)}, bf...) custom-call(bf16[32,4096]{1,0:T(8,128)(2,1)} %convert_element_type.7, ...), custom_call_target="tpu_custom_call" | custom-call | tf_op jit(solution)/shard_map/gather_second/pallas_call | solution.py:487
  180.1 0.9 copy.83
  181.0 1.6 pad.28.clone
  182.6 51.2 %stage_two.1 = (bf16[4096,1024]{1,0:T(8,128)(2,1)}, bf16[1024,4096]{1,0:T(8,128)(2,1)}, bf16[1024,1024]{1,0:T(8,128)(2,1)}, f32[1024,1024]{1,0:T(8,128)}, bf16[1...) custom-call(bf16[1024,1024]{1,0:T(8,128)(2,1)} %get-tuple-element.48.c_in, f32[1024,1024]{1,0:T(8,128)} %get-tuple-element.49.h_mid, ...), custom_call_target="tpu_custom_call" | custom-call | tf_op jit(solution)/shard_map/stage_two/pallas_call | solution.py:719
  233.8 163.7 %mlp_sums.1 = (f32[32,4096]{1,0:T(8,128)}, f32[128,1024]{1,0:T(8,128)}, bf16[1024,3072]{1,0:T(8,128)(2,1)}, bf16[1024,1024]{1,0:T(8,128)(2,1)}, f32[24,1024]{1,0:T(8,128)}) custom-call(bf16[1024,1024]{1,0:T(8,128)(2,1)} %get-tuple-element.54.refs_0_, bf16[1024,4096]{1,0:T(8,128)(2,1)} %get-tuple-element.55.refs_1_, ...), custom_call_target="tpu_custom_call" | custom-call | tf_op jit(solution)/shard_map/mlp_sums/pallas_call | solution.py:651
  397.5 1.1 copy.79
  400.0 1.4 reshape.132
  401.4 1.0 slice.97
  402.5 2.0 concatenate.19
  404.5 1.0 pad_bitcast_fusion.refs_6_
  405.5 3.9 copy.77
  409.5 89.4 %rest_sums.1 = (f32[32,3072]{1,0:T(8,128)}, f32[32,1024]{1,0:T(8,128)}, f32[32,1024]{1,0:T(8,128)}) custom-call(bf16[1024,1024]{1,0:T(8,128)(2,1)} %get-tuple-element.53.refs_0_, bf16[1024,3072]{1,0:T(8,128)(2,1)} %get-tuple-element.61.refs_1_, bf16[1024,1024]{1,0:T(8,128)(2,1)} %get-tuple-element.62.refs_2_, ...), custom_call_target="tpu_custom_call" | custom-call | tf_op jit(solution)/shard_map/rest_sums/pallas_call | solution.py:690
  498.9 2.1 reshape.133
  501.0 1.5 slice_bitcast_fusion
  502.5 1.4 slice_bitcast_fusion.2
  503.9 0.8 slice.86
  504.7 0.6 reshape.134
  505.3 0.8 slice.90
  506.7 2.3 slice_reduce_fusion
  509.0 1.6 slice.96
  510.7 2.1 copy.82
  512.7 0.7 copy.91
  513.4 0.8 copy.92
  514.2 0.8 copy.93
  (55 shorter events, 4.9 us)
Async XLA Ops:
  0.7 12.4 %copy-start.8 = (f32[197,32]{0,1:T(8,128)S(1)}, f32[197,32]{0,1:T(8,128)}, u32[]{:S(2)}) copy-start(f32[197,32]{0,1:T(8,128)} %param.25) | copy-start | bytes 75652
  0.7 13.1 %copy-start.5 = (f32[32,1024]{1,0:T(8,128)S(1)}, f32[32,1024]{1,0:T(8,128)}, u32[]{:S(2)}) copy-start(f32[32,1024]{1,0:T(8,128)} %param.33) | copy-start | bytes 393220
  79.9 1.9 copy-start.9
  87.6 1.7 copy-start.1
  87.6 2.4 copy-start.2
  90.7 89.4 %copy-start = (bf16[16,50,1024]{2,0,1:T(8,128)(2,1)S(1)}, bf16[16,50,1024]{2,0,1:T(8,128)(2,1)}, u32[]{:S(2)}) copy-start(bf16[16,50,1024]{2,0,1:T(8,128)(2,1)} %param.41) | copy-start | bytes 4915204
  233.8 164.8 %copy-start.7 = (f32[24,1024]{1,0:T(8,128)S(1)}, f32[24,1024]{1,0:T(8,128)}, u32[]{:S(2)}) copy-start(f32[24,1024]{1,0:T(8,128)} %get-tuple-element.64) | copy-start | bytes 294916
  510.6 2.1 copy-start.6
  510.7 2.7 copy-start.4
  510.7 3.5 copy-start.3

commit v5 on v4

--- a/solution.py
+++ b/solution.py
@@ -80,9 +80,10 @@
         first = (2 * chip + core) * ARRAYS[arr][0] + row
         return self.wholes[arr].at[pl.ds(pl.multiple_of(first, 32), rows), pl.ds(col, cols)]
 
-    def ring_copy(self, i, src, dst, step):
-        return pltpu.make_async_remote_copy(src_ref=src, dst_ref=dst, send_sem=self.send_sem.at[i, step], recv_sem=self.recv_sem.at[i, step],
-                                            device_id=(self.place.after[self.streams[i][5]],), device_id_type=MESH_ID)
+    def ring_copy(self, i, src, dst, step, back):
+        towards, place = (self.place.before, step + N_CHIP // 2) if back else (self.place.after, step)
+        return pltpu.make_async_remote_copy(src_ref=src, dst_ref=dst, send_sem=self.send_sem.at[i, place], recv_sem=self.recv_sem.at[i, place],
+                                            device_id=(towards[self.streams[i][5]],), device_id_type=MESH_ID)
 
     def twin_copy(self, i, src, dst, step):
         return pltpu.make_async_remote_copy(src_ref=src, dst_ref=dst, send_sem=self.twin_send.at[i, step], recv_sem=self.twin_recv.at[i, step],
@@ -94,49 +95,65 @@
             first = pl.multiple_of((2 * self.place.chip + self.place.core) * rows, 32)
             yield pltpu.make_async_copy(self.shards[arr], self.wholes[arr].at[pl.ds(first, rows), :], self.own_sem.at[place])
 
+    def pass_along(self, step, back):
+        place, far = self.place, N_CHIP // 2 - (1 if back else 0)
+        chips = place.chips_back(-step if back else step)
+        for i in range(len(self.streams)):
+            here = self.block(i, chips[self.streams[i][5]], place.core)
+            self.ring_copy(i, here, here, step - 1, back).wait_recv()
+
+            @pl.when(step < far)
+            def _():
+                self.ring_copy(i, here, here, step, back).start()
+
+            self.twin_copy(i, here, here, step + (N_CHIP // 2 if back else 0)).start()
+
     def run(self, hook):
-        place = self.place
+        place, half = self.place, N_CHIP // 2
         for i in range(len(self.streams)):
             arr, row, rows, col, cols, _ = self.streams[i]
             mine = self.shards[arr].at[pl.ds(row, rows), pl.ds(col, cols)]
             here = self.block(i, place.chip, place.core)
-            self.ring_copy(i, mine, here, 0).start()
+            self.ring_copy(i, mine, here, 0, False).start()
+            self.ring_copy(i, mine, here, 0, True).start()
             self.twin_copy(i, mine, here, 0).start()
         for copy in self.own_copies():
             copy.start()
         hook(jnp.int32(0))
 
         def ring_step(step, carry):
-            chips = place.chips_back(step)
-            for i in range(len(self.streams)):
-                here = self.block(i, chips[self.streams[i][5]], place.core)
-                self.ring_copy(i, here, here, step - 1).wait_recv()
-
-                @pl.when(step < N_CHIP - 1)
-                def _():
-                    self.ring_copy(i, here, here, step).start()
-
-                self.twin_copy(i, here, here, step).start()
-            hook(step)
+            self.pass_along(step, False)
+            hook(2 * step - 1)
+
+            @pl.when(step < half)
+            def _():
+                self.pass_along(step, True)
+                hook(2 * step)
             return carry
 
-        lax.fori_loop(1, N_CHIP, ring_step, 0)
+        lax.fori_loop(1, half + 1, ring_step, 0)
 
         def drain(step, carry):
-            chips = place.chips_back(step)
+            chips = [place.chips_back(step), place.chips_back(-step)]
             for i in range(len(self.streams)):
                 k = self.streams[i][5]
-                here, there = self.block(i, chips[k], place.core), self.block(i, chips[k], 1 - place.core)
-
-                @pl.when(step < N_CHIP - 1)
-                def _():
-                    self.ring_copy(i, here, here, step).wait_send()
-
-                self.twin_copy(i, here, here, step).wait_send()
-                self.twin_copy(i, there, there, step).wait_recv()
+                for back in (False, True):
+                    here, there = self.block(i, chips[back][k], place.core), self.block(i, chips[back][k], 1 - place.core)
+                    far = half - 1 if back else half
+
+                    @pl.when(step < far)
+                    def _():
+                        self.ring_copy(i, here, here, step, back).wait_send()
+
+                    at = step + (half if back else 0)
+
+                    @pl.when(jnp.logical_and(step >= 1, step < half) if back else step >= 0)
+                    def _():
+                        self.twin_copy(i, here, here, at).wait_send()
+                        self.twin_copy(i, there, there, at).wait_recv()
             return carry
 
-        lax.fori_loop(0, N_CHIP, drain, 0)
+        lax.fori_loop(0, half + 1, drain, 0)
         for copy in self.own_copies():
             copy.wait()
 
@@ -538,11 +555,12 @@
     add_row(sums, VEC_AT['b_out'], d_sum)
 
 
-def context_back(b, qkv, d_ctx, d_qkv, d_part):
+def context_back(slot, b, qkv, d_ctx, d_qkv, d_part):
+    rows = pl.ds(b * SEQ, SEQ)
     for g in range(4):
         places = [pl.ds(1024 * s + HEAD_GROUP * g, HEAD_GROUP) for s in range(3)]
-        q_block, k_block, v_block = [qkv[b, :, place] for place in places]
-        d_block = d_ctx[:, HEAD_GROUP * g:HEAD_GROUP * (g + 1)]
+        q_block, k_block, v_block = [qkv[slot, rows, place] for place in places]
+        d_block = d_ctx[rows, pl.ds(HEAD_GROUP * g, HEAD_GROUP)]
         k_stack = stack_heads(k_block)
         prob = probabilities(q_block, k_stack)
         d_prob = dot_nt(d_block, stack_heads(v_block))
@@ -551,7 +569,7 @@
         g_k = unstack_heads(dot_tn(d_logit, q_block))
         g_v = unstack_heads(dot_tn(prob.astype(jnp.bfloat16), d_block))
         for place, grad in zip(places, (g_q, g_k, g_v)):
-            d_qkv[b, :, place] = grad.astype(jnp.bfloat16)
+            d_qkv[slot, rows, place] = grad.astype(jnp.bfloat16)
             d_part[:, place] += jnp.sum(grad.reshape(SEQ // 8, 8, HEAD_GROUP), axis=0)
 
 
@@ -565,7 +583,7 @@
     add_row(sums, VEC_AT['lnp_g'], d_zero * hat_p)
     add_row(sums, VEC_AT['lnp_b'], d_zero)
     d_x = normalize_back(d_zero, hat_p, inv_p, row_of(vecs, 'lnp_g'))
-    cls = is_cls(SEQ)
+    cls = is_cls(PAIR)
     d_emb = jnp.where(cls, 0.0, d_x)
     add_row(sums, VEC_AT['cls_tok'], jnp.where(cls, d_x, 0.0))
     add_row(sums, VEC_AT['b_patch'], d_emb)
@@ -576,26 +594,27 @@
     (c_hbm, pre_hbm, gelu_hbm, rows_hbm, qkv_w_hbm, out_w_hbm, vecs, x_hbm, mid_hbm, mid_b_hbm, qkv_hbm) = refs[:11]
     fc_out, proj_out, d_qkv_out, d_emb_out, sums = refs[11:16]
     (c_turned, d_pre, gelu_turned, grad_rows, w_qkv, w_out, x_zero, d_mid, d_mid_b, qkv, d_qkv, d_emb, d_part,
-     load_sem, in_sem, out_sem) = refs[16:32]
-    (accs, owns, gives, twins), sems = split_scratch(refs[32:], 2)
+     d_ctx, d_a, load_sem, in_sem, out_sem) = refs[16:34]
+    (accs, owns, gives, twins), sems = split_scratch(refs[34:], 2)
     place = Place()
     loads = [pltpu.make_async_copy(src, dst, load_sem.at[n]) for n, (src, dst) in enumerate(
         ((c_hbm, c_turned), (pre_hbm, d_pre), (gelu_hbm, gelu_turned), (rows_hbm, grad_rows), (qkv_w_hbm, w_qkv), (out_w_hbm, w_out)))]
     for load in loads:
         load.start()
-    n_img = x_hbm.shape[0] // SEQ
-
-    def image_in(b, slot):
-        rows = pl.ds(pl.multiple_of(b * SEQ, SEQ), SEQ)
-        return [pltpu.make_async_copy(src.at[rows, :], dst.at[slot], in_sem.at[n, slot]) for n, (src, dst) in enumerate(
+    n_pair = x_hbm.shape[0] // PAIR
+
+    def span(p):
+        return pl.ds(pl.multiple_of(p * PAIR, PAIR), PAIR)
+
+    def pair_in(p, slot):
+        return [pltpu.make_async_copy(src.at[span(p), :], dst.at[slot], in_sem.at[n, slot]) for n, (src, dst) in enumerate(
             ((x_hbm, x_zero), (mid_hbm, d_mid), (mid_b_hbm, d_mid_b), (qkv_hbm, qkv)))]
 
-    def image_out(b, slot):
-        rows = pl.ds(pl.multiple_of(b * SEQ, SEQ), SEQ)
-        return [pltpu.make_async_copy(src.at[slot], dst.at[rows, :], out_sem.at[n, slot]) for n, (src, dst) in enumerate(
-            ((d_qkv, d_qkv_out), (d_emb, d_emb_out)))]
-
-    for copy in image_in(0, 0):
+    def pair_out(p, slot):
+        return [pltpu.make_async_copy(d_qkv.at[slot], d_qkv_out.at[span(p), :], out_sem.at[0, slot]),
+                pltpu.make_async_copy(d_emb.at[slot], d_emb_out.at[:, span(p)], out_sem.at[1, slot])]
+
+    for copy in pair_in(0, 0):
         copy.start()
     sums[...] = jnp.zeros_like(sums)
     d_part[...] = jnp.zeros_like(d_part)
@@ -606,32 +625,40 @@
         load.wait()
 
     def hook(half, step):
-        slot = lax.rem(step, 2)
-        if half == 0:
-            @pl.when(step < n_img - 1)
-            def _():
-                for copy in image_in(step + 1, 1 - slot):
+        p = lax.div(step, 2)
+        slot = lax.rem(p, 2)
+
+        @pl.when(lax.rem(step, 2) == 0)
+        def _():
+            if half == 0:
+                @pl.when(p < n_pair - 1)
+                def _():
+                    for copy in pair_in(p + 1, 1 - slot):
+                        copy.start()
+
+                for copy in pair_in(p, slot):
+                    copy.wait()
+
+                @pl.when(p >= 2)
+                def _():
+                    for copy in pair_out(p - 2, slot):
+                        copy.wait()
+
+                d_ctx[...] = dot_nt(d_mid_b[slot], w_out[...]).astype(jnp.bfloat16)
+            context_back(slot, half, qkv, d_ctx, d_qkv, d_part)
+
+        @pl.when(lax.rem(step, 2) == 1)
+        def _():
+            if half == 0:
+                d_a[...] = dot_nt(d_qkv[slot], w_qkv[...])
+            else:
+                d_emb[slot] = entry_back(x_zero[slot], d_mid[slot], d_a[...], vecs, sums).T
+                for copy in pair_out(p, slot):
                     copy.start()
 
-            for copy in image_in(step, slot):
-                copy.wait()
-
-            @pl.when(step >= 2)
-            def _():
-                for copy in image_out(step - 2, slot):
-                    copy.wait()
-
-            d_ctx = dot_nt(d_mid_b[slot], w_out[...]).astype(jnp.bfloat16)
-            context_back(slot, qkv, d_ctx, d_qkv, d_part)
-        else:
-            d_a = dot_nt(d_qkv[slot], w_qkv[...])
-            d_emb[slot] = entry_back(x_zero[slot], d_mid[slot], d_a, vecs, sums)
-            for copy in image_out(step, slot):
-                copy.start()
-
     ring.run((tuple(range(6)), tuple(range(6, len(MLP_STREAMS)))), hook)
-    for step in (n_img - 2, n_img - 1):
-        for copy in image_out(step, step % 2):
+    for p in (n_pair - 2, n_pair - 1):
+        for copy in pair_out(p, p % 2):
             copy.wait()
     for s in range(3):
         add_row(sums, VEC_QKV + s, d_part[:, pl.ds(1024 * s, 1024)])
@@ -643,11 +670,12 @@
     n_rows = x_zero.shape[0]
     assert n_rows // SEQ == N_CHIP
     out_shape = [jax.ShapeDtypeStruct(ARRAYS[FC], f32), jax.ShapeDtypeStruct(ARRAYS[PROJ], f32), jax.ShapeDtypeStruct((n_rows, 3072), bf),
-                 jax.ShapeDtypeStruct((n_rows, 1024), bf), jax.ShapeDtypeStruct((VEC_ROWS, 1024), f32)]
+                 jax.ShapeDtypeStruct((1024, n_rows), bf), jax.ShapeDtypeStruct((VEC_ROWS, 1024), f32)]
     anywhere, vmem = pl.BlockSpec(memory_space=pl.ANY), pl.BlockSpec(memory_space=pltpu.VMEM)
     scratch = [pltpu.VMEM(a.shape, bf) for a in (c_turned, d_pre, gelu_turned, grad_rows, w_qkv, w_out)]
-    scratch += [pltpu.VMEM((2, SEQ, 1024), f32), pltpu.VMEM((2, SEQ, 1024), f32), pltpu.VMEM((2, SEQ, 1024), bf), pltpu.VMEM((2, SEQ, 3072), bf),
-                pltpu.VMEM((2, SEQ, 3072), bf), pltpu.VMEM((2, SEQ, 1024), bf), pltpu.VMEM((8, 3072), f32), dma((6,)), dma((4, 2)), dma((2, 2))]
+    scratch += [pltpu.VMEM((2, PAIR, 1024), f32), pltpu.VMEM((2, PAIR, 1024), f32), pltpu.VMEM((2, PAIR, 1024), bf), pltpu.VMEM((2, PAIR, 3072), bf),
+                pltpu.VMEM((2, PAIR, 3072), bf), pltpu.VMEM((2, 1024, PAIR), bf), pltpu.VMEM((8, 3072), f32),
+                pltpu.VMEM((PAIR, 1024), bf), pltpu.VMEM((PAIR, 1024), f32), dma((6,)), dma((4, 2)), dma((2, 2))]
     return pl.pallas_call(
         mlp_sums_kernel, out_shape=out_shape, in_specs=[anywhere] * 6 + [vmem] + [anywhere] * 4, out_specs=[anywhere] * 4 + [vmem],
         scratch_shapes=scratch + ring_scratch((FC, PROJ), MLP_STREAMS),
@@ -724,26 +752,33 @@
 
 
 def solution(mesh):
+    n_dev = mesh.shape[MESH_AXIS]
+
     def spec_of(name):
         return P(None, MESH_AXIS) if name in LAST_SPLIT else P(MESH_AXIS)
 
-    def vector_columns(part, rows):
-        columns = [part[name].reshape(rows, 1) for name in VEC_NAMES] + [part['b_qkv'].reshape(rows, 3), part['b_fc'].reshape(rows, 4)]
-        return jnp.pad(jnp.concatenate(columns, axis=1), ((0, 0), (0, 1024 - MISC_USED)))
-
     def pack_misc(part):
-        rows = part['w_patch'].shape[1]
-        return jnp.concatenate([part['w_patch'].T, part['pos_table'].T, vector_columns(part, rows)], axis=1)
+        lane = part['b_patch'].shape[0]
+        rows = [part['w_patch'], part['pos_table']] + [part[name].reshape(1, lane) for name in VEC_NAMES]
+        rows += [part['b_qkv'].reshape(3, lane), part['b_fc'].reshape(4, lane), jnp.zeros((1024 - MISC_USED, lane), jnp.float32)]
+        return jnp.concatenate(rows, axis=0).astype(jnp.bfloat16).T
 
     def unpack_misc(misc):
-        part = {'w_patch': misc[:, :N_PIXEL].T, 'pos_table': misc[:, N_PIXEL:N_PIXEL + N_POS].T}
+        turned = misc.T
+        part = {'w_patch': turned[:N_PIXEL], 'pos_table': turned[N_PIXEL:N_PIXEL + N_POS]}
         first = N_PIXEL + N_POS
         for place, name in enumerate(VEC_NAMES):
-            part[name] = misc[:, first + place]
+            part[name] = turned[first + place]
         first += len(VEC_NAMES)
-        part['b_qkv'] = misc[:, first:first + 3].reshape(-1)
-        part['b_fc'] = misc[:, first + 3:first + 7].reshape(-1)
+        part['b_qkv'] = turned[first:first + 3].reshape(-1)
+        part['b_fc'] = turned[first + 3:first + 7].reshape(-1)
         return part
+
+    def flat_of(rows):
+        return rows.reshape(rows.shape[0], n_dev, -1).transpose(1, 0, 2).reshape(rows.shape)
+
+    def shards_of(rows):
+        return rows.reshape(n_dev, rows.shape[0], -1).transpose(1, 0, 2).reshape(rows.shape)
 
     def local_step(patches, keep, *rest):
         shards = dict(zip(PARAM_NAMES, rest[:-1]))
@@ -752,8 +787,8 @@
         n_token, d_model = grad_h1.shape[1:]
         n_shard, _, n_heads, head_dim = shards['w_qkv'].shape
         n_rows = n_img * SEQ
-        casts = {name: shards[name].astype(jnp.bfloat16) for name in PARAM_NAMES}
-        w_qkv, w_out, misc = gather_first((casts['w_qkv'].reshape(n_shard, -1), casts['w_out'], pack_misc(casts)))
+        casts = {name: shards[name].astype(jnp.bfloat16) for name in ('w_fc', 'w_proj', 'w_qkv', 'w_out')}
+        w_qkv, w_out, misc = gather_first((casts['w_qkv'].reshape(n_shard, -1), casts['w_out'], pack_misc(shards)))
         position = jnp.pad(keep + 1, ((0, 0), (1, 0)))
         position = jnp.pad(position, ((0, 0), (0, SEQ - n_token)), constant_values=-1)[:, :, None]
         onehot_patch = (position == 1 + lax.broadcasted_iota(jnp.int32, (1, 1, n_patch), 2)).astype(jnp.bfloat16)
@@ -762,10 +797,9 @@
         x_in = jnp.concatenate([kept_rows, onehot_pos], axis=2).reshape(n_rows, 1024)
         grad_rows = jnp.pad(grad_h1, ((0, 0), (0, SEQ - n_token), (0, 0))).reshape(n_rows, d_model)
 
-        vec_part = misc[:, N_PIXEL + N_POS:MISC_USED].astype(jnp.float32)
         n_vec = len(VEC_NAMES)
-        vecs = jnp.concatenate([vec_part[:, :n_vec].T, vec_part[:, n_vec:n_vec + 3].reshape(3, 1024), vec_part[:, n_vec + 3:].reshape(4, 1024)], axis=0)
-        vecs = jnp.pad(vecs, ((0, VEC_ROWS - vecs.shape[0]), (0, 0)))
+        packed = misc[:, 896:].T[N_PIXEL + N_POS - 896:MISC_USED - 896].astype(jnp.float32)
+        vecs = jnp.concatenate([packed[:n_vec], flat_of(packed[n_vec:n_vec + 3]), flat_of(packed[n_vec + 3:]), jnp.zeros((VEC_ROWS - packed.shape[0], 1024), jnp.float32)], axis=0)
 
         bf, f32 = jnp.bfloat16, jnp.float32
         w_fc, w_proj, x_zero, a_turned, qkv, ctx_turned, h_mid, c_in, c_turned = gather_second(casts['w_fc'], casts['w_proj'], x_in, misc, w_qkv, w_out, vecs)
@@ -774,12 +808,12 @@
             [(-4096, bf), (4096, bf), (1024, bf), (1024, f32), (1024, bf), (0, None)],
             [pltpu.VMEM((ROWS, 1024), f32), pltpu.VMEM((ROWS, 1024), f32)])
         h_one = h_one.reshape(n_img, SEQ, d_model)[:, :n_token]
-        fc_sum, proj_sum, d_qkv, d_emb, sums_three = mlp_sums(c_turned, d_pre, gelu_turned, grad_rows, w_qkv, w_out, vecs, x_zero, d_mid, d_mid_b, qkv)
+        fc_sum, proj_sum, d_qkv, emb_turned, sums_three = mlp_sums(c_turned, d_pre, gelu_turned, grad_rows, w_qkv, w_out, vecs, x_zero, d_mid, d_mid_b, qkv)
         sums = sums_two + sums_three
-        vec_rows = jnp.concatenate([sums[:n_vec], sums[VEC_QKV:VEC_QKV + 3].reshape(1024, 3).T, sums[VEC_FC:VEC_FC + 4].reshape(1024, 4).T], axis=0)
+        vec_rows = jnp.concatenate([sums[:n_vec], shards_of(sums[VEC_QKV:VEC_QKV + 3]), shards_of(sums[VEC_FC:VEC_FC + 4])], axis=0)
         g_rows = jnp.concatenate([sums[VEC_AT['cls_tok']][None], jnp.zeros((N_POS - 1, 1024), f32), vec_rows], axis=0)
         g_vec = jnp.pad(g_rows, ((0, 1024 - N_PIXEL - g_rows.shape[0]), (0, 0))).T
-        qkv_sum, out_sum, misc_sum = rest_sums(a_turned, d_qkv, ctx_turned, d_mid_b, d_emb.T, x_in, g_vec)
+        qkv_sum, out_sum, misc_sum = rest_sums(a_turned, d_qkv, ctx_turned, d_mid_b, emb_turned, x_in, g_vec)
         own = unpack_misc(misc_sum)
         own.update(w_fc=fc_sum, w_proj=proj_sum, w_qkv=qkv_sum.reshape(n_shard, 3, n_heads, head_dim), w_out=out_sum)
         return (h_one,) + tuple(own[name] for name in PARAM_NAMES)

time: 523 us -> 479 us (0.916)
  Pallas kernels: 456 us -> 415 us
    pallas_call x1, Pallas kernels: 164 us -> 148 us  [mlp_sums(): pl.pallas_call(mlp_sums_kernel, out_shape=out_shape, in_specs=[anywhere]...]
    pallas_call x1, Pallas kernels: 89.4 us -> 74.9 us  [gather_second(): pl.pallas_call(gather_second_kernel, out_shape=out_shape, in_specs=[vmem,...]
    pallas_call x1, Pallas kernels: 62.6 us -> 50.5 us  [gather_first(): pl.pallas_call(gather_first_kernel, out_shape=gathered_shapes(FIRST_ARRAY...]
where the time goes in v5:
time: 479 us; the launch traced here: 471 us
  Pallas kernels  415 us (87%)
  local copies, waits for them, and re-layouts  32.9 us (7%)
  other arithmetic  15.6 us (3%)
  matrix products  5.48 us (1%)
    pallas_call x1, Pallas kernels, mlp_sums(): pl.pallas_call(mlp_sums_kernel, out_shape=out_shape, in_specs=[anywhere]...  148 us
    pallas_call x1, Pallas kernels, rest_sums(): pl.pallas_call(rest_sums_kernel, out_shape=[jax.ShapeDtypeStruct(ARRAYS[a...  91.5 us
    pallas_call x1, Pallas kernels, gather_second(): pl.pallas_call(gather_second_kernel, out_shape=out_shape, in_specs=[vmem,...  74.9 us
    pallas_call x1, Pallas kernels, stage_call(): pl.pallas_call(body, grid=(n_rows // ROWS,), in_specs=in_specs, out_specs...  51 us
    pallas_call x1, Pallas kernels, gather_first(): pl.pallas_call(gather_first_kernel, out_shape=gathered_shapes(FIRST_ARRAY...  50.5 us

profile of v5, /device:TPU:0, one launch (start us, length us, event | category | flops | bytes accessed | tf_op | source)
XLA Modules:
  0.0 470.8 jit_solution(15593614391721795162)
XLA Ops:
  0.7 1.2 convert_element_type.31
  1.9 1.0 reshape.138.refs_0_
  2.8 0.9 convert.56
  3.7 0.8 convert.57
  4.5 0.7 convert.68
  5.4 0.7 convert.69
  6.2 0.7 convert_bitcast_fusion.9
  7.0 0.7 convert_bitcast_fusion.8
  7.7 0.7 convert_bitcast_fusion.7
  8.5 0.7 convert_bitcast_fusion.6
  9.3 0.7 convert_bitcast_fusion.5
  10.0 0.7 convert_bitcast_fusion.4
  10.8 0.7 convert_bitcast_fusion.3
  11.5 0.7 convert_bitcast_fusion.2
  12.3 0.7 convert_bitcast_fusion.1
  13.1 0.7 convert_bitcast_fusion
  13.8 0.7 concatenate.14
  14.6 0.6 convert_element_type.32.refs_1_
  15.2 50.5 %gather_first.1 = (bf16[1024,3072]{1,0:T(8,128)(2,1)}, bf16[1024,1024]{1,0:T(8,128)(2,1)}, bf16[1024,1024]{1,0:T(8,128)(2,1)}) custom-call(bf16[32,3072]{1,0:T(8,128)(2,1)} %reshape.138.refs_0_, bf16[32,1024]{1,0:T(8,128)(2,1)} %convert_element_type.32.refs_1_, bf16[32,1024]{1,0:T(8,128)(2,1)} %bitcast.59), custom_call_target="tpu_custom_call" | custom-call | tf_op jit(solution)/shard_map/gather_first/pallas_call | solution.py:180
  65.8 2.9 copy.75
  69.3 0.7 maximum_maximum_fusion.refs_6_.vecs
  70.1 5.5 %fusion.2 = bf16[16,64,768]{2,1,0:T(8,128)(2,1)S(1)} fusion(bf16[16,196,768]{2,0,1:T(8,128)(2,1)} %param.21, s32[196]{0:T(256)S(1)} %iota_add_fusion, s32[16,64]{1,0:T(8,128)S(1)} %pad_select_fusion), kind=kOutput, calls=%fused_computation.3 | convolution fusion | flops 309268480 | bytes 6394640 | tf_op jit(solution)/shard_map/bkp,bpq->bkq/dot_general | solution.py:796
  75.8 1.6 pad_maximum_fusion
  77.5 0.7 convert_element_type.27.refs_0_
  78.2 0.7 convert_element_type.28.refs_1_
  78.9 74.9 %gather_second.1 = (bf16[1024,4096]{1,0:T(8,128)(2,1)}, bf16[4096,1024]{1,0:T(8,128)(2,1)}, f32[1024,1024]{1,0:T(8,128)}, bf16[1024,1024]{1,0:T(8,128)(2,1)}, bf...) custom-call(bf16[32,4096]{1,0:T(8,128)(2,1)} %convert_element_type.2, ...), custom_call_target="tpu_custom_call" | custom-call | tf_op jit(solution)/shard_map/gather_second/pallas_call | solution.py:504
  153.8 0.9 copy.89
  154.8 1.6 pad.18.clone
  156.3 51.0 %stage_two.1 = (bf16[4096,1024]{1,0:T(8,128)(2,1)}, bf16[1024,4096]{1,0:T(8,128)(2,1)}, bf16[1024,1024]{1,0:T(8,128)(2,1)}, f32[1024,1024]{1,0:T(8,128)}, bf16[1...) custom-call(bf16[1024,1024]{1,0:T(8,128)(2,1)} %get-tuple-element.48.c_in, f32[1024,1024]{1,0:T(8,128)} %get-tuple-element.49.h_mid, ...), custom_call_target="tpu_custom_call" | custom-call | tf_op jit(solution)/shard_map/stage_two/pallas_call | solution.py:747
  207.3 147.5 %mlp_sums.1 = (f32[32,4096]{1,0:T(8,128)}, f32[128,1024]{1,0:T(8,128)}, bf16[1024,3072]{1,0:T(8,128)(2,1)}, bf16[1024,1024]{1,0:T(8,128)(2,1)}, f32[24,1024]{1,0:T(8,128)}) custom-call(bf16[1024,1024]{1,0:T(8,128)(2,1)} %get-tuple-element.54.refs_0_, bf16[1024,4096]{1,0:T(8,128)(2,1)} %get-tuple-element.55.refs_1_, ...), custom_call_target="tpu_custom_call" | custom-call | tf_op jit(solution)/shard_map/mlp_sums/pallas_call | solution.py:679
  354.9 1.1 copy.81
  357.5 1.1 copy.85
  358.6 1.0 slice.102
  359.7 2.3 concatenate.16
  361.9 1.0 pad_bitcast_fusion.refs_6_
  363.0 91.5 %rest_sums.1 = (f32[32,3072]{1,0:T(8,128)}, f32[32,1024]{1,0:T(8,128)}, f32[32,1024]{1,0:T(8,128)}) custom-call(bf16[1024,1024]{1,0:T(8,128)(2,1)} %get-tuple-element.53.refs_0_, bf16[1024,3072]{1,0:T(8,128)(2,1)} %get-tuple-element.61.refs_1_, bf16[1024,1024]{1,0:T(8,128)(2,1)} %get-tuple-element.62.refs_2_, ...), custom_call_target="tpu_custom_call" | custom-call | tf_op jit(solution)/shard_map/rest_sums/pallas_call | solution.py:718
  454.5 2.1 reshape.161
  456.5 1.5 slice.106
  458.1 1.4 slice.108
  459.5 0.8 slice.114
  460.9 0.8 slice.118
  461.8 0.6 reshape.163
  462.4 2.0 slice_reduce_fusion
  464.4 1.6 slice.101
  466.0 2.1 copy.88
  468.1 0.7 copy.101
  468.8 0.8 copy.102
  469.6 0.8 copy.103
  (63 shorter events, 4.7 us)
Async XLA Ops:
  0.7 13.9 %copy-start.5 = (f32[32,1024]{1,0:T(8,128)S(1)}, f32[32,1024]{1,0:T(8,128)}, u32[]{:S(2)}) copy-start(f32[32,1024]{1,0:T(8,128)} %param.33) | copy-start | bytes 393220
  65.8 4.3 copy-start.8
  75.8 1.7 copy-start.1
  75.8 2.4 copy-start.2
  78.9 74.9 %copy-start = (bf16[16,50,1024]{2,0,1:T(8,128)(2,1)S(1)}, bf16[16,50,1024]{2,0,1:T(8,128)(2,1)}, u32[]{:S(2)}) copy-start(bf16[16,50,1024]{2,0,1:T(8,128)(2,1)} %param.41) | copy-start | bytes 4915204
  207.3 148.6 %copy-start.7 = (f32[24,1024]{1,0:T(8,128)S(1)}, f32[24,1024]{1,0:T(8,128)}, u32[]{:S(2)}) copy-start(f32[24,1024]{1,0:T(8,128)} %get-tuple-element.64) | copy-start | bytes 294916
  466.0 2.1 copy-start.6
  466.0 2.7 copy-start.4
  466.0 3.5 copy-start.3

commit v6 on v5

--- a/solution.py
+++ b/solution.py
@@ -208,17 +208,13 @@
                                             send_sem=self.send_sem.at[i, slot], recv_sem=self.recv_sem.at[i, slot_next],
                                             device_id=(self.place.after[k],), device_id_type=MESH_ID)
 
-    def make_own(self, group, step):
-        chips = self.place.chips_back(step + 1)
-        for i in group:
-            arr, k = self.streams[i][0], self.streams[i][5]
-            self.part(i, self.owns[arr])[...] = self.term(i, chips[k], self.place.core)
-
-    def make_give(self, group, step):
+    def make(self, group, step):
         chips, slot = self.place.chips_back(step + 1), lax.rem(jnp.int32(step), 2)
         for i in group:
-            arr, k = self.streams[i][0], self.streams[i][5]
-            self.part(i, self.gives[arr], slot)[...] = self.term(i, chips[k], 1 - self.place.core)
+            arr, cols, k = self.streams[i][0], self.streams[i][4], self.streams[i][5]
+            block = self.term(i, chips[k])
+            self.part(i, self.owns[arr], slot)[...] = block[:, :cols]
+            self.part(i, self.gives[arr], slot)[...] = block[:, cols:]
 
     def push_next(self, group, step):
         slot, slot_next = lax.rem(step, 2), lax.rem(step + 1, 2)
@@ -234,7 +230,7 @@
         slot, slot_next, slot_last, pair = lax.rem(step, 3), lax.rem(step + 1, 3), lax.rem(step + 2, 3), lax.rem(step, 2)
         for i in group:
             arr, row, rows, col, cols, k = self.streams[i]
-            acc, own, twin = self.part(i, self.accs[arr], slot), self.part(i, self.owns[arr]), self.part(i, self.twins[arr], pair)
+            acc, own, twin = self.part(i, self.accs[arr], slot), self.part(i, self.owns[arr], pair), self.part(i, self.twins[arr], pair)
             self.push(i, pair).wait_recv()
 
             @pl.when(step == 0)
@@ -269,26 +265,28 @@
             def _():
                 pl.semaphore_signal(self.ring_free.at[i], inc=1, device_id=(self.place.before[k],), device_id_type=MESH_ID)
 
-    def run(self, groups, hook):
-        for group in groups:
-            self.make_give(group, 0)
+    def run(self, groups, hook, ready):
+        for place, group in enumerate(groups):
+            ready(place)
+            self.make(group, 0)
             for i in group:
                 self.push(i, 0).start()
-            self.make_own(group, 0)
-            self.make_give(group, 1)
 
         def ring_step(step, carry):
             for place, group in enumerate(groups):
                 self.advance(group, step)
 
+                @pl.when(step == 0)
+                def _():
+                    self.make(group, 1)
+
                 @pl.when(step < N_CHIP - 1)
                 def _():
                     self.push_next(group, step)
-                    self.make_own(group, step + 1)
 
                 @pl.when(step < N_CHIP - 2)
                 def _():
-                    self.make_give(group, step + 2)
+                    self.make(group, step + 2)
 
                 hook(place, step)
             return carry
@@ -316,7 +314,7 @@
 
 def ring_scratch(arrays, streams):
     shapes = [(2 * ARRAYS[arr][0], ARRAYS[arr][1] // 2) for arr in arrays]
-    buffers = [pltpu.VMEM((*lead, *shape), jnp.float32) for lead in ((3,), (), (2,), (2,)) for shape in shapes]
+    buffers = [pltpu.VMEM((*lead, *shape), jnp.float32) for lead in ((3,), (2,), (2,), (2,)) for shape in shapes]
     dma, regular, n = pltpu.SemaphoreType.DMA, pltpu.SemaphoreType.REGULAR, len(streams)
     return buffers + [dma((n, 2)), dma((n, 2)), dma((n, 3)), dma((n, 3)), regular((n,)), regular((n,))] + [dma((len(arrays),))] * 3
 
@@ -326,12 +324,13 @@
     return [buffers[n_arrays * b:n_arrays * (b + 1)] for b in range(4)], sems
 
 
-def term_of(streams, lefts, rights):
-    def term(i, chip, core):
+def term_of(streams, lefts, rights, core):
+    def term(i, chip):
         arr, row, rows, col, cols, _ = streams[i]
         half = ARRAYS[arr][1] // 2
         first = pl.multiple_of(2 * chip * ARRAYS[arr][0] + row, 16)
-        return dot_nn(lefts[arr][pl.ds(first, rows), :], rights[arr][:, pl.ds(pl.multiple_of(core * half + col, 128), cols)])
+        right = jnp.concatenate([rights[arr][:, pl.ds(pl.multiple_of(side * half + col, 128), cols)] for side in (core, 1 - core)], axis=1)
+        return dot_nn(lefts[arr][pl.ds(first, rows), :], right)
     return term
 
 
@@ -599,7 +598,7 @@
     place = Place()
     loads = [pltpu.make_async_copy(src, dst, load_sem.at[n]) for n, (src, dst) in enumerate(
         ((c_hbm, c_turned), (pre_hbm, d_pre), (gelu_hbm, gelu_turned), (rows_hbm, grad_rows), (qkv_w_hbm, w_qkv), (out_w_hbm, w_out)))]
-    for load in loads:
+    for load in loads[:2]:
         load.start()
     n_pair = x_hbm.shape[0] // PAIR
 
@@ -619,10 +618,14 @@
     sums[...] = jnp.zeros_like(sums)
     d_part[...] = jnp.zeros_like(d_part)
     place.meet()
-    term = term_of(MLP_STREAMS, {FC: c_turned, PROJ: gelu_turned}, {FC: d_pre, PROJ: grad_rows})
+    term = term_of(MLP_STREAMS, {FC: c_turned, PROJ: gelu_turned}, {FC: d_pre, PROJ: grad_rows}, place.core)
     ring = RingSum(place, (FC, PROJ), MLP_STREAMS, accs, owns, gives, twins, sems, term)
-    for load in loads:
-        load.wait()
+
+    def ready(group):
+        for load in loads[2 * group:2 * group + 2]:
+            load.wait()
+        for load in loads[2 * group + 2:2 * group + 4]:
+            load.start()
 
     def hook(half, step):
         p = lax.div(step, 2)
@@ -631,6 +634,11 @@
         @pl.when(lax.rem(step, 2) == 0)
         def _():
             if half == 0:
+                @pl.when(step == 0)
+                def _():
+                    for load in loads[4:]:
+                        load.wait()
+
                 @pl.when(p < n_pair - 1)
                 def _():
                     for copy in pair_in(p + 1, 1 - slot):
@@ -656,7 +664,7 @@
                 for copy in pair_out(p, slot):
                     copy.start()
 
-    ring.run((tuple(range(6)), tuple(range(6, len(MLP_STREAMS)))), hook)
+    ring.run((tuple(range(6)), tuple(range(6, len(MLP_STREAMS)))), hook, ready)
     for p in (n_pair - 2, n_pair - 1):
         for copy in pair_out(p, p % 2):
             copy.wait()
@@ -691,23 +699,30 @@
     place = Place()
     loads = [pltpu.make_async_copy(src, dst, load_sem.at[n]) for n, (src, dst) in enumerate(
         ((a_hbm, a_turned), (dqkv_hbm, d_qkv), (ctx_hbm, ctx_turned), (mid_hbm, d_mid_b), (emb_hbm, emb_turned), (in_hbm, x_in), (vec_hbm, g_vec)))]
-    for load in loads:
+    for load in loads[:2]:
         load.start()
     place.meet()
-    product = term_of(REST_STREAMS, {QKV: a_turned, OUT: ctx_turned, MISC: emb_turned}, {QKV: d_qkv, OUT: d_mid_b, MISC: x_in})
-
-    def term(i, chip, core):
+    product = term_of(REST_STREAMS, {QKV: a_turned, OUT: ctx_turned, MISC: emb_turned}, {QKV: d_qkv, OUT: d_mid_b, MISC: x_in}, place.core)
+
+    def term(i, chip):
         arr, row, rows, col, cols, _ = REST_STREAMS[i]
-        block = product(i, chip, core)
+        block = product(i, chip)
         if arr == MISC and col >= 256:
             first = pl.multiple_of(2 * chip * ARRAYS[arr][0] + row, 16)
-            block = block + jnp.where(core == 1, g_vec[pl.ds(first, rows), pl.ds(col - 256, cols)], 0.0)
+            extra = g_vec[pl.ds(first, rows), pl.ds(col - 256, cols)]
+            block = block + jnp.concatenate([jnp.where(place.core == side, extra, 0.0) for side in (1, 0)], axis=1)
         return block
 
     ring = RingSum(place, (QKV, OUT, MISC), REST_STREAMS, accs, owns, gives, twins, sems, term)
-    for load in loads:
-        load.wait()
-    ring.run((tuple(range(6)), tuple(range(6, len(REST_STREAMS)))), lambda half, step: None)
+
+    def ready(group):
+        for load in loads[2:] if group else loads[:2]:
+            load.wait()
+        if not group:
+            for load in loads[2:]:
+                load.start()
+
+    ring.run((tuple(range(6)), tuple(range(6, len(REST_STREAMS)))), lambda half, step: None, ready)
     ring.finish(outs)
 
 
@@ -759,9 +774,9 @@
 
     def pack_misc(part):
         lane = part['b_patch'].shape[0]
-        rows = [part['w_patch'], part['pos_table']] + [part[name].reshape(1, lane) for name in VEC_NAMES]
-        rows += [part['b_qkv'].reshape(3, lane), part['b_fc'].reshape(4, lane), jnp.zeros((1024 - MISC_USED, lane), jnp.float32)]
-        return jnp.concatenate(rows, axis=0).astype(jnp.bfloat16).T
+        flat = [part[name] for name in VEC_NAMES] + [part['b_qkv'], part['b_fc'], jnp.zeros(((1024 - MISC_USED) * lane,), jnp.float32)]
+        vectors = lax.optimization_barrier(jnp.concatenate(flat)).reshape(-1, lane)
+        return jnp.concatenate([part['w_patch'], part['pos_table'], vectors], axis=0).astype(jnp.bfloat16).T
 
     def unpack_misc(misc):
         turned = misc.T

time: 479 us -> 469 us (0.979)
  other arithmetic: 15.6 us -> 8.41 us
    reshape x10 -> x0, other arithmetic: 6.59 us -> none  [pack_misc(): part[name].reshape(1, lane)]
    pallas_call x1, Pallas kernels: 148 us -> 141 us  [mlp_sums(): pl.pallas_call(mlp_sums_kernel, out_shape=out_shape, in_specs=[anywhere]...]
    pallas_call x1, Pallas kernels: 91.5 us -> 96.6 us  [rest_sums(): pl.pallas_call(rest_sums_kernel, out_shape=[jax.ShapeDtypeStruct(ARRAYS[a...]
where the time goes in v6:
time: 469 us; the launch traced here: 461 us
  Pallas kernels  414 us (88%)
  local copies, waits for them, and re-layouts  31.8 us (7%)
  other arithmetic  8.41 us (2%)
  matrix products  5.48 us (1%)
    pallas_call x1, Pallas kernels, mlp_sums(): pl.pallas_call(mlp_sums_kernel, out_shape=out_shape, in_specs=[anywhere]...  141 us
    pallas_call x1, Pallas kernels, rest_sums(): pl.pallas_call(rest_sums_kernel, out_shape=[jax.ShapeDtypeStruct(ARRAYS[a...  96.6 us
    pallas_call x1, Pallas kernels, gather_second(): pl.pallas_call(gather_second_kernel, out_shape=out_shape, in_specs=[vmem,...  74.9 us
    pallas_call x1, Pallas kernels, stage_call(): pl.pallas_call(body, grid=(n_rows // ROWS,), in_specs=in_specs, out_specs...  51 us
    pallas_call x1, Pallas kernels, gather_first(): pl.pallas_call(gather_first_kernel, out_shape=gathered_shapes(FIRST_ARRAY...  50.5 us

profile of v6, /device:TPU:0, one launch (start us, length us, event | category | flops | bytes accessed | tf_op | source)
XLA Modules:
  0.0 461.0 jit_solution(14614757636132017364)
XLA Ops:
  0.7 1.2 convert_element_type.31
  1.9 1.0 reshape.94.refs_0_
  2.8 0.9 convert.10
  3.7 0.9 concatenate.17
  4.8 0.8 convert.11
  5.6 0.7 maximum_bitcast_fusion.refs_2_
  6.3 0.6 convert_element_type.32.refs_1_
  6.9 50.5 %gather_first.1 = (bf16[1024,3072]{1,0:T(8,128)(2,1)}, bf16[1024,1024]{1,0:T(8,128)(2,1)}, bf16[1024,1024]{1,0:T(8,128)(2,1)}) custom-call(bf16[32,3072]{1,0:T(8,128)(2,1)} %reshape.94.refs_0_, bf16[32,1024]{1,0:T(8,128)(2,1)} %convert_element_type.32.refs_1_, bf16[32,1024]{1,0:T(8,128)(2,1)} %maximum_bitcast_fusion.refs_2_), custom_call_target="tpu_custom_call" | custom-call | tf_op jit(solution)/shard_map/gather_first/pallas_call | solution.py:180
  57.5 2.9 copy.52
  60.5 0.1 reshape.99
  61.0 0.7 maximum_maximum_fusion.refs_6_.vecs
  61.8 5.5 %fusion.2 = bf16[16,64,768]{2,1,0:T(8,128)(2,1)S(1)} fusion(bf16[16,196,768]{2,0,1:T(8,128)(2,1)} %param.21, s32[196]{0:T(256)S(1)} %iota_add_fusion, s32[16,64]{1,0:T(8,128)S(1)} %pad_select_fusion), kind=kOutput, calls=%fused_computation.3 | convolution fusion | flops 309268480 | bytes 6394640 | tf_op jit(solution)/shard_map/bkp,bpq->bkq/dot_general | solution.py:811
  67.3 0.2 fusion.5
  67.5 1.6 pad_maximum_fusion
  69.2 0.7 convert_element_type.27.refs_0_
  69.9 0.7 convert_element_type.28.refs_1_
  70.6 74.9 %gather_second.1 = (bf16[1024,4096]{1,0:T(8,128)(2,1)}, bf16[4096,1024]{1,0:T(8,128)(2,1)}, f32[1024,1024]{1,0:T(8,128)}, bf16[1024,1024]{1,0:T(8,128)(2,1)}, bf...) custom-call(bf16[32,4096]{1,0:T(8,128)(2,1)} %convert_element_type.2, ...), custom_call_target="tpu_custom_call" | custom-call | tf_op jit(solution)/shard_map/gather_second/pallas_call | solution.py:503
  145.5 0.9 copy.66
  146.5 1.6 pad.18.clone
  148.0 51.0 %stage_two.1 = (bf16[4096,1024]{1,0:T(8,128)(2,1)}, bf16[1024,4096]{1,0:T(8,128)(2,1)}, bf16[1024,1024]{1,0:T(8,128)(2,1)}, f32[1024,1024]{1,0:T(8,128)}, bf16[1...) custom-call(bf16[1024,1024]{1,0:T(8,128)(2,1)} %get-tuple-element.48.c_in, f32[1024,1024]{1,0:T(8,128)} %get-tuple-element.49.h_mid, ...), custom_call_target="tpu_custom_call" | custom-call | tf_op jit(solution)/shard_map/stage_two/pallas_call | solution.py:762
  199.0 141.0 %mlp_sums.1 = (f32[32,4096]{1,0:T(8,128)}, f32[128,1024]{1,0:T(8,128)}, bf16[1024,3072]{1,0:T(8,128)(2,1)}, bf16[1024,1024]{1,0:T(8,128)(2,1)}, f32[24,1024]{1,0:T(8,128)}) custom-call(bf16[1024,1024]{1,0:T(8,128)(2,1)} %get-tuple-element.54.refs_0_, bf16[1024,4096]{1,0:T(8,128)(2,1)} %get-tuple-element.55.refs_1_, ...), custom_call_target="tpu_custom_call" | custom-call | tf_op jit(solution)/shard_map/mlp_sums/pallas_call | solution.py:687
  340.0 1.1 copy.58
  341.1 0.2 copy.57
  341.4 0.2 slice.105
  341.6 0.2 copy.61
  341.8 0.1 reshape.104
  341.9 0.3 copy.62
  342.2 0.2 slice.104
  342.4 0.2 copy.59
  342.5 0.1 reshape.102
  342.7 1.1 copy.60
  343.7 1.0 slice.102
  344.8 2.3 concatenate.20
  347.1 1.0 pad_bitcast_fusion.refs_6_
  348.1 96.6 %rest_sums.1 = (f32[32,3072]{1,0:T(8,128)}, f32[32,1024]{1,0:T(8,128)}, f32[32,1024]{1,0:T(8,128)}) custom-call(bf16[1024,1024]{1,0:T(8,128)(2,1)} %get-tuple-element.53.refs_0_, bf16[1024,3072]{1,0:T(8,128)(2,1)} %get-tuple-element.61.refs_1_, bf16[1024,1024]{1,0:T(8,128)(2,1)} %get-tuple-element.62.refs_2_, ...), custom_call_target="tpu_custom_call" | custom-call | tf_op jit(solution)/shard_map/rest_sums/pallas_call | solution.py:733
  444.7 2.1 reshape.106
  446.8 1.5 slice.106
  448.3 1.4 slice.108
  449.7 0.8 slice.114
  450.6 0.6 reshape.107
  451.2 0.8 slice.118
  452.0 0.6 reshape.108
  452.6 2.0 slice_reduce_fusion
  454.6 1.6 slice.101
  456.3 2.1 copy.65
  458.4 0.7 copy.78
  459.0 0.8 copy.79
  459.8 0.8 copy.80
  (40 shorter events, 1.1 us)
Async XLA Ops:
  0.7 5.6 %copy-start.5 = (f32[32,1024]{1,0:T(8,128)S(1)}, f32[32,1024]{1,0:T(8,128)}, u32[]{:S(2)}) copy-start(f32[32,1024]{1,0:T(8,128)} %param.33) | copy-start | bytes 393220
  57.5 4.3 copy-start.8
  67.5 1.7 copy-start.1
  67.5 2.4 copy-start.2
  70.6 74.9 %copy-start = (bf16[16,50,1024]{2,0,1:T(8,128)(2,1)S(1)}, bf16[16,50,1024]{2,0,1:T(8,128)(2,1)}, u32[]{:S(2)}) copy-start(bf16[16,50,1024]{2,0,1:T(8,128)(2,1)} %param.41) | copy-start | bytes 4915204
  199.0 142.1 %copy-start.7 = (f32[24,1024]{1,0:T(8,128)S(1)}, f32[24,1024]{1,0:T(8,128)}, u32[]{:S(2)}) copy-start(f32[24,1024]{1,0:T(8,128)} %get-tuple-element.64) | copy-start | bytes 294916
  456.3 2.1 copy-start.6
  456.3 2.7 copy-start.4
  456.3 3.5 copy-start.3
